TPU v7x, 256 devices: a whole 4x4x8 slice. The times are simulated.
256 devices in a mesh: src: 8 (over x, y_hi), rcv: 32 (over y_lo, z, core).
Axes of the slice: x: 4, y: 4 (y_hi: 2, y_lo: 2; y = y_hi * 2 + y_lo), z: 8, core: 2. Of those that a mesh axis runs over, the one named last changes fastest.
Arguments:
- wavefield: float32 [2, 16, 2048, 2048], P(None, None, 'rcv', 'src')
- surface_band: float32 [2, 2048, 1024], P(None, 'rcv'), may hold values from -0.75 to 0.75
- band_shift: int32 [32], P('rcv'), may hold values from -16 to 16
- trace_mask: int32 [2048], P('rcv'), may hold values 0 or 1
- shot_taper: float32 [5], replicated, may hold values from 0.2 to 1
Outputs:
- multiples: float32 [2, 16, 2048, 2048], P(None, None, 'rcv', 'src')
- primaries: float32 [2, 16, 2048, 2048], P(None, None, 'rcv', 'src')
All inputs are finite; a program needn't handle non-finite values. No bound on the sum of `trace_mask` on one device may be relied on, other than what follows from the above.
Results may differ from a plain program's by a relative error of at most 0.0003.
Values sent between devices are 32-bit elements; how exact they have to be, the bound alone decides.
No kernel may reach another device: no remote copies, remote signals or barrier semaphores. Data moves between devices by JAX's collectives and lax.ppermute only.
A program may use at most 64 MiB of HBM per device.

v0:
```python
import functools

import jax
import jax.numpy as jnp
from jax import lax
from jax.sharding import Mesh
from jax.sharding import PartitionSpec as P

APER = 64
SHIFT = 16
BLOCK = 64
SHALF = 2
RCV = ("rcv_0", "rcv_1", "rcv_2")
SRC = ("src_0", "src_1")
SRC_RCV = ("src_0", "src_1", "rcv_0", "rcv_1", "rcv_2")


def extended(cells, sides, width):
    for axis, dim in sides:
        count = lax.axis_size(axis)
        ends = count - 1
        head = lax.slice_in_dim(cells, 0, width, axis=dim)
        tail = lax.slice_in_dim(cells, cells.shape[dim] - width, cells.shape[dim], axis=dim)
        cells = jnp.concatenate(
            [
                lax.ppermute(tail, axis, [(i, (i + 1) % count) for i in range(ends)]),
                cells,
                lax.ppermute(head, axis, [((i + 1) % count, i) for i in range(ends)]),
            ],
            axis=dim,
        )
    return cells


def by_axis(array, axes):
    return functools.reduce(lax.psum, axes, array)


def band_matrix(band_piece):
    columns = band_piece.shape[3]
    taps = band_piece.shape[2]
    rows_index = jnp.arange(columns + taps - 1, dtype=jnp.int32)
    cols_index = jnp.arange(columns, dtype=jnp.int32)
    tap_index = jnp.arange(taps, dtype=jnp.int32)
    onehot = (
        tap_index[:, None, None] == rows_index[None, :, None] - cols_index[None, None, :]
    ).astype(jnp.float32)
    return jnp.einsum("xftc,tjc->xfjc", band_piece, onehot, precision=lax.Precision.HIGHEST)


def complex_product(window, band):
    real_part = jnp.einsum(
        "fjc,fjs->fcs", band[0], window[0], precision=lax.Precision.HIGHEST
    ) - jnp.einsum("fjc,fjs->fcs", band[1], window[1], precision=lax.Precision.HIGHEST)
    imag_part = jnp.einsum(
        "fjc,fjs->fcs", band[1], window[0], precision=lax.Precision.HIGHEST
    ) + jnp.einsum("fjc,fjs->fcs", band[0], window[1], precision=lax.Precision.HIGHEST)
    return jnp.stack([real_part, imag_part])


def receiver_products(padded, band_local, band_shift, halo_width):
    start = halo_width - APER // 2 + band_shift[0]
    window = lax.dynamic_slice_in_dim(padded, start, BLOCK + APER - 1, 2)
    outputs = complex_product(window, band_matrix(band_local))
    return outputs


def taper_rows(padded, shot_taper, shots):
    result = shot_taper[0] * padded[:, :, :, 0:shots]
    for offset_row in range(1, 2 * SHALF + 1):
        result = result + shot_taper[offset_row] * padded[:, :, :, offset_row : offset_row + shots]
    return result


def per_device(wavefield, surface_band, band_shift, trace_mask, shot_taper):
    shots = wavefield.shape[3]
    slices = wavefield.shape[1]
    receivers = wavefield.shape[2]
    band_local = jnp.transpose(surface_band.reshape(2, receivers, slices, APER), (0, 2, 3, 1))
    masked = wavefield * trace_mask.astype(jnp.float32)[None, None, :, None]
    halo_width = APER // 2 + SHIFT
    padded = extended(masked, ((RCV, 2),), halo_width)
    predicted = receiver_products(padded, band_local, band_shift, halo_width)
    shot_padded = extended(predicted, ((SRC, 3),), SHALF)
    multiples = taper_rows(shot_padded, shot_taper, shots)
    data_energy = jnp.sum(wavefield * wavefield, axis=(0, 2, 3))
    pred_energy = jnp.sum(multiples * multiples, axis=(0, 2, 3))
    data_energy, pred_energy = (by_axis(data_energy, SRC_RCV), by_axis(pred_energy, SRC_RCV))
    gain = jnp.sqrt((data_energy + 1e-06) / (pred_energy + 1e-06))
    primaries = wavefield - gain[None, :, None, None] * multiples
    return (multiples, primaries)


def solution(mesh):
    split = Mesh(mesh.devices.reshape(4, 2, 2, 8, 2), ("src_0", "src_1", "rcv_0", "rcv_1", "rcv_2"))
    return jax.shard_map(
        per_device,
        mesh=split,
        in_specs=(P(None, None, RCV, SRC), P(None, RCV, None), P(RCV), P(RCV), P()),
        out_specs=(P(None, None, RCV, SRC), P(None, None, RCV, SRC)),
        check_vma=False,
    )
```

profile of v0, /device:TPU:1, one launch (start us, length us, event | category | flops | bytes accessed | tf_op | source)
XLA Modules:
  0.0 115.3 jit_solution(8125680364762427383)
XLA Ops:
  0.6 0.7 convert_element_type.4
  1.3 2.0 %multiply_reduce_fusion.1 = (f32[16]{0:T(128)S(1)}, f32[2,16,64,256]{3,2,1,0:T(8,128)S(1)}) fusion(f32[2,16,64,256]{3,2,1,0:T(8,128)} %param.5, f32[64]{0:T(128)S(1)} %convert_element_type.4), kind=kLoop, calls=%fused_computation.25 | loop fusion | flops 1572848 | bytes 4194624 | tf_op jit(solution)/shard_map/reduce_sum | solution.py:86
  3.3 2.1 %fusion.32 = (f32[2,16,48,256]{3,2,1,0:T(8,128)}, f32[2,16,48,256]{3,2,1,0:T(8,128)}) fusion(f32[2,16,64,256]{3,2,1,0:T(8,128)S(1)} %get-tuple-element.15), kind=kLoop, calls=%fused_computation.53 | loop fusion | bytes 6291456 | tf_op jit(solution)/shard_map/slice | solution.py:22
  5.3 5.1 %collective-permute-start.1 = (f32[2,16,48,256]{3,2,1,0:T(8,128)}, f32[2,16,48,256]{3,2,1,0:T(8,128)}, u32[]{:S(2)}, u32[]{:S(2)}) collective-permute-start(f32[2,16,48,256]{3,2,1,0:T(8,128)} %get-tuple-element.20), channel_id=1, source_target_pairs={{1,0},{2,1},{3,2},{4,3},{5,4},{6,5},{7,6},{8,7},{9,8},{10,9},{11,1... | collective-permute-start | bytes 4718600 | tf_op jit(solution)/shard_map/ppermute | solution.py:28
  10.4 1.9 %collective-permute-start = (f32[2,16,48,256]{3,2,1,0:T(8,128)}, f32[2,16,48,256]{3,2,1,0:T(8,128)}, u32[]{:S(2)}, u32[]{:S(2)}) collective-permute-start(f32[2,16,48,256]{3,2,1,0:T(8,128)} %get-tuple-element.21), channel_id=1, source_target_pairs={{0,1},{1,2},{2,3},{3,4},{4,5},{5,6},{6,7},{7,8},{8,9},{9,10},{10,1... | collective-permute-start | bytes 4718600 | tf_op jit(solution)/shard_map/ppermute | solution.py:26
  13.0 1.3 %reshape.28 = f32[2,64,16,64]{3,2,1,0:T(8,128)S(1)} reshape(f32[2,64,1024]{2,1,0:T(8,128)} %param.6) | data formatting | bytes 1048576 | tf_op jit(solution)/shard_map/reshape | solution.py:79
  14.4 1.2 %fusion.14 = f32[2,16,127,64]{2,1,0,3:T(8,128)S(1)} fusion(f32[2,64,16,64]{3,2,1,0:T(8,128)S(1)} %reshape.28, s32[127,64]{0,1:T(8,128)S(1)} %iota_subtract_fusion), kind=kOutput, calls=%fused_computation.33 | convolution fusion | flops 200273920 | bytes 1597184 | tf_op jit(solution)/shard_map/xftc,tjc->xfjc/dot_general | solution.py:48
  15.6 0.1 slice_bitcast_fusion.15
  15.7 13.0 %collective-permute-done.1 = f32[2,16,48,256]{3,2,1,0:T(8,128)} collective-permute-done((f32[2,16,48,256]{3,2,1,0:T(8,128)}, f32[2,16,48,256]{3,2,1,0:T(8,128)}, u32[]{:S(2)}, u32[]{:S(2)}) %collective-permute-start.1) | collective-permute-done | bytes 1572896 | tf_op jit(solution)/shard_map/ppermute | solution.py:28
  28.7 1.4 %collective-permute-done = f32[2,16,48,256]{3,2,1,0:T(8,128)} collective-permute-done((f32[2,16,48,256]{3,2,1,0:T(8,128)}, f32[2,16,48,256]{3,2,1,0:T(8,128)}, u32[]{:S(2)}, u32[]{:S(2)}) %collective-permute-start) | collective-permute-done | bytes 1572896 | tf_op jit(solution)/shard_map/ppermute | solution.py:26
  30.0 2.9 %fusion.1 = f32[2,16,127,256]{3,2,1,0:T(8,128)S(1)} fusion(s32[]{:T(128)S(6)} %select_n.3, f32[2,16,48,256]{3,2,1,0:T(8,128)} %collective-permute-done, f32[2,16,64,256]{3,2,1,0:T(8,128)S(1)} %get-tuple-element.15, f32[2,16,48,256]{3,2,1,0:T(8,128)} %collective-permute-done.1), kind=kLoop, calls=%fused_computation.4 | loop fusion | flops 2080768 | bytes 9404420 | tf_op jit(solution)/shard_map/concatenate | solution.py:24
  32.9 1.4 %fusion.12 = f32[16,64,256]{2,1,0:T(8,128)S(1)} fusion(f32[2,16,127,256]{3,2,1,0:T(8,128)S(1)} %fusion.1, f32[16,127,64]{1,0,2:T(8,128)S(1)} %get-tuple-element.22), kind=kOutput, calls=%fused_computation.31 | convolution fusion | flops 399507456 | bytes 3670016 | tf_op jit(solution)/shard_map/fjc,fjs->fcs/dot_general | solution.py:57
  34.3 1.4 %fusion.13 = f32[16,64,256]{2,1,0:T(8,128)S(1)} fusion(f32[2,16,127,256]{3,2,1,0:T(8,128)S(1)} %fusion.1, f32[16,127,64]{1,0,2:T(8,128)S(1)} %get-tuple-element.23), kind=kOutput, calls=%fused_computation.32 | convolution fusion | flops 399507456 | bytes 3670016 | tf_op jit(solution)/shard_map/fjc,fjs->fcs/dot_general | solution.py:54
  35.7 1.4 %fusion.20 = f32[1,16,64,256]{3,2,1,0:T(8,128)S(1)} fusion(f32[16,64,256]{2,1,0:T(8,128)S(1)} %fusion.12, f32[2,16,127,256]{3,2,1,0:T(8,128)S(1)} %fusion.1, f32[16,127,64]{1,0,2:T(8,128)S(1)} %get-tuple-element.23), kind=kOutput, calls=%fused_computation.37 | convolution fusion | flops 399769600 | bytes 4718592 | tf_op jit(solution)/shard_map/fjc,fjs->fcs/dot_general | solution.py:55
  37.1 1.4 %fusion.18 = f32[1,16,64,256]{3,2,1,0:T(8,128)S(1)} fusion(f32[16,64,256]{2,1,0:T(8,128)S(1)} %fusion.13, f32[2,16,127,256]{3,2,1,0:T(8,128)S(1)} %fusion.1, f32[16,127,64]{1,0,2:T(8,128)S(1)} %get-tuple-element.22), kind=kOutput, calls=%fused_computation.35 | convolution fusion | flops 399769600 | bytes 4718592 | tf_op jit(solution)/shard_map/fjc,fjs->fcs/dot_general | solution.py:52
  38.6 1.4 %fusion.21 = (f32[2,16,64,2]{3,2,1,0:T(8,128)}, f32[2,16,64,2]{3,2,1,0:T(8,128)S(1)}) fusion(f32[1,16,64,256]{3,2,1,0:T(8,128)S(1)} %fusion.18, f32[1,16,64,256]{3,2,1,0:T(8,128)S(1)} %fusion.20), kind=kLoop, calls=%fused_computation.38 | loop fusion | flops 8192 | bytes 2129920 | tf_op jit(solution)/shard_map/stack | solution.py:58
  39.9 0.0 copy-start
  39.9 1.6 %copy.17 = f32[2,16,64,2]{2,1,3,0:T(8,128)S(1)} copy(f32[2,16,64,2]{3,2,1,0:T(8,128)} %get-tuple-element.18) | data formatting | bytes 32768 | tf_op jit(solution)/shard_map/slice | solution.py:23
  41.5 0.4 copy.19
  41.9 1.3 %collective-permute-start.3 = (f32[2,16,64,2]{2,1,3,0:T(8,128)S(1)}, f32[2,16,64,2]{2,1,3,0:T(8,128)S(1)}, u32[]{:S(2)}, u32[]{:S(2)}) collective-permute-start(f32[2,16,64,2]{2,1,3,0:T(8,128)S(1)} %copy.19), channel_id=1, source_target_pairs={{32,0},{64,32},{96,64},{128,96},{160,128},{192,160},{224,192},{33,... | collective-permute-start | bytes 49160 | tf_op jit(solution)/shard_map/ppermute | solution.py:28
  43.2 5.7 %collective-permute-start.2 = (f32[2,16,64,2]{2,1,3,0:T(8,128)S(1)}, f32[2,16,64,2]{2,1,3,0:T(8,128)S(1)}, u32[]{:S(2)}, u32[]{:S(2)}) collective-permute-start(f32[2,16,64,2]{2,1,3,0:T(8,128)S(1)} %copy.17), channel_id=1, source_target_pairs={{0,32},{32,64},{64,96},{96,128},{128,160},{160,192},{192,224},{1,3... | collective-permute-start | bytes 49160 | tf_op jit(solution)/shard_map/ppermute | solution.py:26
  48.9 0.0 copy-done
  48.9 0.7 fusion.33
  49.6 0.2 collective-permute-done.2
  49.7 0.4 copy.18
  50.1 0.0 collective-permute-done.3
  50.1 1.4 %copy.20 = f32[2,16,64,2]{3,2,1,0:T(8,128)} copy(f32[2,16,64,2]{2,1,3,0:T(8,128)S(1)} %collective-permute-done.3) | data formatting | bytes 32768 | tf_op jit(solution)/shard_map/ppermute | solution.py:28
  51.5 2.3 %maximum_maximum_fusion = (f32[2,16,64,258]{3,2,1,0:T(8,128)S(1)}, f32[2,16,64,258]{3,2,1,0:T(8,128)S(1)}) fusion(f32[1,16,64,256]{3,2,1,0:T(8,128)S(1)} %fusion.20, f32[1,16,64,256]{3,2,1,0:T(8,128)S(1)} %fusion.18, f32[2,16,64,2]{3,2,1,0:T(8,128)S(1)} %copy.18, f32[2,16,64,2]{3,2,1,0:T(8,128)} %copy.20), kind=kLoop, calls=%fused_computation.5 | loop fusion | flops 2113536 | bytes 6356992 | tf_op jit(solution)/shard_map/concatenate | solution.py:24
  53.8 6.2 %multiply_reduce_fusion = (f32[16]{0:T(128)S(1)}, f32[2,16,64,256]{3,2,1,0:T(8,128)}) fusion(f32[2,16,64,258]{3,2,1,0:T(8,128)S(1)} %get-tuple-element.17, f32[]{:T(128)} %bitcast.16, f32[]{:T(128)} %bitcast.15, f32[1,16,64,256]{3,2,1,0:T(8,128)S(1)} %fusion.20, f32[1,16,64,256]{3,2,1,0:T(8,128)S(1)} %fusion.18, f32[]{:T(128)} %bitcast.14, ...), kind=kLoop, calls=%fused_computation.24 | loop fusion | flops 6291440 | bytes 12582996 | tf_op jit(solution)/shard_map/reduce_sum | solution.py:87
  60.1 12.6 %all-reduce.1 = (f32[16]{0:T(128)S(1)}, f32[16]{0:T(128)S(1)}) all-reduce(f32[16]{0:T(128)S(1)} %get-tuple-element.12, f32[16]{0:T(128)S(1)} %get-tuple-element.14), channel_id=1, replica_groups=mesh['src_0'=4,'src_1'=2,'rcv_0'=2,'rcv_1'=8,'rcv_2'=2] {'src_0'}, use_global_device_ids=true, to_apply=%region_7.0 | all-reduce | flops 32 | bytes 256 | tf_op jit(solution)/shard_map/psum | solution.py:36
  72.7 5.3 %all-reduce.4 = (f32[16]{0:T(128)S(1)}, f32[16]{0:T(128)S(1)}) all-reduce(f32[16]{0:T(128)S(1)} %get-tuple-element.4, f32[16]{0:T(128)S(1)} %get-tuple-element.5), channel_id=1, replica_groups=mesh['src_0'=4,'src_1'=2,'rcv_0'=2,'rcv_1'=8,'rcv_2'=2] {'src_1'}, use_global_device_ids=true, to_apply=%region_8.0 | all-reduce | flops 32 | bytes 256 | tf_op jit(solution)/shard_map/psum | solution.py:36
  78.0 3.8 %all-reduce.3 = (f32[16]{0:T(128)S(1)}, f32[16]{0:T(128)S(1)}) all-reduce(f32[16]{0:T(128)S(1)} %get-tuple-element.10, f32[16]{0:T(128)S(1)} %get-tuple-element.11), channel_id=1, replica_groups=mesh['src_0'=4,'src_1'=2,'rcv_0'=2,'rcv_1'=8,'rcv_2'=2] {'rcv_0'}, use_global_device_ids=true, to_apply=%region_9.0 | all-reduce | flops 32 | bytes 256 | tf_op jit(solution)/shard_map/psum | solution.py:36
  81.7 18.1 %all-reduce = (f32[16]{0:T(128)S(1)}, f32[16]{0:T(128)S(1)}) all-reduce(f32[16]{0:T(128)S(1)} %get-tuple-element.8, f32[16]{0:T(128)S(1)} %get-tuple-element.9), channel_id=1, replica_groups=mesh['src_0'=4,'src_1'=2,'rcv_0'=2,'rcv_1'=8,'rcv_2'=2] {'rcv_1'}, use_global_device_ids=true, to_apply=%region_10.0 | all-reduce | flops 32 | bytes 256 | tf_op jit(solution)/shard_map/psum | solution.py:36
  99.9 11.4 %all-reduce.2 = (f32[16]{0:T(128)S(1)}, f32[16]{0:T(128)S(1)}) all-reduce(f32[16]{0:T(128)S(1)} %get-tuple-element.2, f32[16]{0:T(128)S(1)} %get-tuple-element.3), channel_id=1, replica_groups=mesh['src_0'=4,'src_1'=2,'rcv_0'=2,'rcv_1'=8,'rcv_2'=2] {'rcv_2'}, use_global_device_ids=true, to_apply=%region_11.0 | all-reduce | flops 32 | bytes 256 | tf_op jit(solution)/shard_map/psum | solution.py:36
  111.2 4.1 %multiply_subtract_fusion = f32[2,16,64,256]{3,2,1,0:T(8,128)} fusion(f32[2,16,64,256]{3,2,1,0:T(8,128)} %param.5, f32[2,16,64,256]{3,2,1,0:T(8,128)} %get-tuple-element.13, f32[16]{0:T(128)S(1)} %fusion.30), kind=kLoop, calls=%fused_computation.23 | loop fusion | flops 1048576 | bytes 6291520 | tf_op jit(solution)/shard_map/sub | solution.py:90
  (2 shorter events, 0.0 us)
Async XLA Ops:
  5.3 23.3 %collective-permute-start.1 = (f32[2,16,48,256]{3,2,1,0:T(8,128)}, f32[2,16,48,256]{3,2,1,0:T(8,128)}, u32[]{:S(2)}, u32[]{:S(2)}) collective-permute-start(f32[2,16,48,256]{3,2,1,0:T(8,128)} %get-tuple-element.20), channel_id=1, source_target_pairs={{1,0},{2,1},{3,2},{4,3},{5,4},{6,5},{7,6},{8,7},{9,8},{10,9},{11,1... | collective-permute-start | bytes 4718600 | tf_op jit(solution)/shard_map/ppermute | solution.py:28
  10.4 19.6 %collective-permute-start = (f32[2,16,48,256]{3,2,1,0:T(8,128)}, f32[2,16,48,256]{3,2,1,0:T(8,128)}, u32[]{:S(2)}, u32[]{:S(2)}) collective-permute-start(f32[2,16,48,256]{3,2,1,0:T(8,128)} %get-tuple-element.21), channel_id=1, source_target_pairs={{0,1},{1,2},{2,3},{3,4},{4,5},{5,6},{6,7},{7,8},{8,9},{9,10},{10,1... | collective-permute-start | bytes 4718600 | tf_op jit(solution)/shard_map/ppermute | solution.py:26
  39.9 9.0 %copy-start = (f32[5]{0:T(128)S(1)}, f32[5]{0:T(128)}, u32[]{:S(2)}) copy-start(f32[5]{0:T(128)} %param.9) | copy-start | bytes 64
  41.9 8.2 %collective-permute-start.3 = (f32[2,16,64,2]{2,1,3,0:T(8,128)S(1)}, f32[2,16,64,2]{2,1,3,0:T(8,128)S(1)}, u32[]{:S(2)}, u32[]{:S(2)}) collective-permute-start(f32[2,16,64,2]{2,1,3,0:T(8,128)S(1)} %copy.19), channel_id=1, source_target_pairs={{32,0},{64,32},{96,64},{128,96},{160,128},{192,160},{224,192},{33,... | collective-permute-start | bytes 49160 | tf_op jit(solution)/shard_map/ppermute | solution.py:28
  43.2 6.5 %collective-permute-start.2 = (f32[2,16,64,2]{2,1,3,0:T(8,128)S(1)}, f32[2,16,64,2]{2,1,3,0:T(8,128)S(1)}, u32[]{:S(2)}, u32[]{:S(2)}) collective-permute-start(f32[2,16,64,2]{2,1,3,0:T(8,128)S(1)} %copy.17), channel_id=1, source_target_pairs={{0,32},{32,64},{64,96},{96,128},{128,160},{160,192},{192,224},{1,3... | collective-permute-start | bytes 49160 | tf_op jit(solution)/shard_map/ppermute | solution.py:26
where the time goes:
time: 116 us; the launch traced here: 115 us
  blocking collectives  51.1 us (44%)
  other arithmetic  19.6 us (17%)
  waiting for transfers between devices  14.5 us (12%)
  starting transfers between devices  14 us (12%)
  local copies, waits for them, and re-layouts  7.87 us (7%)
  matrix products  6.8 us (6%)
  between operations  1.43 us (1%)
    psum x5, blocking collectives, by_axis(): return functools.reduce(lax.psum, axes, array)  51.1 us
    ppermute x2, waiting for transfers between devices, extended(): lax.ppermute(head, axis, [((i + 1) % count, i) for i in range(ends)])  13 us
    ppermute x2, starting transfers between devices, extended(): lax.ppermute(tail, axis, [(i, (i + 1) % count) for i in range(ends)])  7.59 us
    ppermute x2, starting transfers between devices, extended(): lax.ppermute(head, axis, [((i + 1) % count, i) for i in range(ends)])  6.4 us
    reduce_sum x1, other arithmetic, per_device(): pred_energy = jnp.sum(multiples * multiples, axis=(0, 2, 3))  6.24 us
    concatenate x2, other arithmetic, extended(): jnp.concatenate([lax.ppermute(tail, axis, [(i, (i + 1) % count) for i in...  5.24 us
    sub x1, other arithmetic, per_device(): primaries = wavefield - gain[None, :, None, None] * multiples  4.1 us
    slice x2, local copies, waits for them, and re-layouts, extended(): head = lax.slice_in_dim(cells, 0, width, axis=dim)  2.45 us
  transfers between devices with their start and end apart: 4, of which 3 were waited for; matrix products, arithmetic and copies ran while one was open for 3% of the time, Pallas kernels for 0%

commit v1 on v0

--- a/solution.py
+++ b/solution.py
@@ -1,5 +1,3 @@
-import functools
-
 import jax
 import jax.numpy as jnp
 from jax import lax
@@ -32,8 +30,10 @@
     return cells
 
 
-def by_axis(array, axes):
-    return functools.reduce(lax.psum, axes, array)
+def summed_everywhere(rows, axes):
+    count = lax.axis_size(axes)
+    spread = jnp.broadcast_to(rows[None], (count,) + rows.shape)
+    return jnp.sum(lax.all_to_all(spread, axes, 0, 0, tiled=True), axis=0)
 
 
 def band_matrix(band_piece):
@@ -85,7 +85,10 @@
     multiples = taper_rows(shot_padded, shot_taper, shots)
     data_energy = jnp.sum(wavefield * wavefield, axis=(0, 2, 3))
     pred_energy = jnp.sum(multiples * multiples, axis=(0, 2, 3))
-    data_energy, pred_energy = (by_axis(data_energy, SRC_RCV), by_axis(pred_energy, SRC_RCV))
+    partial = jnp.concatenate([data_energy, pred_energy])[None]
+    partial = jnp.pad(partial, ((0, 0), (0, 128 - partial.shape[1])))
+    total = summed_everywhere(partial, SRC_RCV)[0]
+    data_energy, pred_energy = (total[:slices], total[slices : 2 * slices])
     gain = jnp.sqrt((data_energy + 1e-06) / (pred_energy + 1e-06))
     primaries = wavefield - gain[None, :, None, None] * multiples
     return (multiples, primaries)

time: 116 us -> 96.8 us (0.83)
  blocking collectives: 51.1 us -> 32 us
    psum x5 -> x0, blocking collectives: 51.1 us -> none  [by_axis(): return functools.reduce(lax.psum, axes, array)]
    all_to_all x0 -> x1, blocking collectives: none -> 32 us  [summed_everywhere(): return jnp.sum(lax.all_to_all(spread, axes, 0, 0, tiled=True), axis=0)]
  transfers between devices with their start and end apart: 4 -> 4, of which waited for: 3 -> 3; matrix products, arithmetic and copies ran while one was open for 3% -> 4% of each run, Pallas kernels for 0% -> 0%
where the time goes in v1:
time: 96.8 us; the launch traced here: 96.4 us
  blocking collectives  32 us (33%)
  other arithmetic  19.7 us (20%)
  waiting for transfers between devices  14.5 us (15%)
  starting transfers between devices  14 us (14%)
  local copies, waits for them, and re-layouts  7.96 us (8%)
  matrix products  6.8 us (7%)
  between operations  1.43 us (1%)
    all_to_all x1, blocking collectives, summed_everywhere(): return jnp.sum(lax.all_to_all(spread, axes, 0, 0, tiled=True), axis=0)  32 us
    ppermute x2, waiting for transfers between devices, extended(): lax.ppermute(head, axis, [((i + 1) % count, i) for i in range(ends)])  13 us
    ppermute x2, starting transfers between devices, extended(): lax.ppermute(tail, axis, [(i, (i + 1) % count) for i in range(ends)])  7.59 us
    ppermute x2, starting transfers between devices, extended(): lax.ppermute(head, axis, [((i + 1) % count, i) for i in range(ends)])  6.4 us
    reduce_sum x1, other arithmetic, per_device(): pred_energy = jnp.sum(multiples * multiples, axis=(0, 2, 3))  6.15 us
    concatenate x2, other arithmetic, extended(): jnp.concatenate([lax.ppermute(tail, axis, [(i, (i + 1) % count) for i in...  5.24 us
    sub x1, other arithmetic, per_device(): primaries = wavefield - gain[None, :, None, None] * multiples  4.1 us
    slice x2, local copies, waits for them, and re-layouts, extended(): head = lax.slice_in_dim(cells, 0, width, axis=dim)  2.45 us
  transfers between devices with their start and end apart: 4, of which 3 were waited for; matrix products, arithmetic and copies ran while one was open for 4% of the time, Pallas kernels for 0%

profile of v1, /device:TPU:1, one launch (start us, length us, event | category | flops | bytes accessed | tf_op | source)
XLA Modules:
  0.0 96.4 jit_solution(3561635171127343966)
XLA Ops:
  0.6 0.7 convert_element_type.6
  1.3 2.0 %multiply_reduce_fusion.1 = (f32[16]{0:T(128)S(1)}, f32[2,16,64,256]{3,2,1,0:T(8,128)S(1)}) fusion(f32[2,16,64,256]{3,2,1,0:T(8,128)} %param.5, f32[64]{0:T(128)S(1)} %convert_element_type.6), kind=kLoop, calls=%fused_computation.25 | loop fusion | flops 1572848 | bytes 4194624 | tf_op jit(solution)/shard_map/reduce_sum | solution.py:86
  3.3 2.1 %fusion.31 = (f32[2,16,48,256]{3,2,1,0:T(8,128)}, f32[2,16,48,256]{3,2,1,0:T(8,128)}) fusion(f32[2,16,64,256]{3,2,1,0:T(8,128)S(1)} %get-tuple-element.5), kind=kLoop, calls=%fused_computation.55 | loop fusion | bytes 6291456 | tf_op jit(solution)/shard_map/slice | solution.py:20
  5.3 5.1 %collective-permute-start.1 = (f32[2,16,48,256]{3,2,1,0:T(8,128)}, f32[2,16,48,256]{3,2,1,0:T(8,128)}, u32[]{:S(2)}, u32[]{:S(2)}) collective-permute-start(f32[2,16,48,256]{3,2,1,0:T(8,128)} %get-tuple-element.10), channel_id=1, source_target_pairs={{1,0},{2,1},{3,2},{4,3},{5,4},{6,5},{7,6},{8,7},{9,8},{10,9},{11,1... | collective-permute-start | bytes 4718600 | tf_op jit(solution)/shard_map/ppermute | solution.py:26
  10.4 1.9 %collective-permute-start = (f32[2,16,48,256]{3,2,1,0:T(8,128)}, f32[2,16,48,256]{3,2,1,0:T(8,128)}, u32[]{:S(2)}, u32[]{:S(2)}) collective-permute-start(f32[2,16,48,256]{3,2,1,0:T(8,128)} %get-tuple-element.11), channel_id=1, source_target_pairs={{0,1},{1,2},{2,3},{3,4},{4,5},{5,6},{6,7},{7,8},{8,9},{9,10},{10,1... | collective-permute-start | bytes 4718600 | tf_op jit(solution)/shard_map/ppermute | solution.py:24
  13.0 1.3 %reshape.51 = f32[2,64,16,64]{3,2,1,0:T(8,128)S(1)} reshape(f32[2,64,1024]{2,1,0:T(8,128)} %param.6) | data formatting | bytes 1048576 | tf_op jit(solution)/shard_map/reshape | solution.py:79
  14.4 1.2 %fusion.14 = f32[2,16,127,64]{2,1,0,3:T(8,128)S(1)} fusion(f32[2,64,16,64]{3,2,1,0:T(8,128)S(1)} %reshape.51, s32[127,64]{0,1:T(8,128)S(1)} %iota_subtract_fusion), kind=kOutput, calls=%fused_computation.33 | convolution fusion | flops 200273920 | bytes 1597184 | tf_op jit(solution)/shard_map/xftc,tjc->xfjc/dot_general | solution.py:48
  15.6 0.1 slice_bitcast_fusion.15
  15.7 13.0 %collective-permute-done.1 = f32[2,16,48,256]{3,2,1,0:T(8,128)} collective-permute-done((f32[2,16,48,256]{3,2,1,0:T(8,128)}, f32[2,16,48,256]{3,2,1,0:T(8,128)}, u32[]{:S(2)}, u32[]{:S(2)}) %collective-permute-start.1) | collective-permute-done | bytes 1572896 | tf_op jit(solution)/shard_map/ppermute | solution.py:26
  28.7 1.4 %collective-permute-done = f32[2,16,48,256]{3,2,1,0:T(8,128)} collective-permute-done((f32[2,16,48,256]{3,2,1,0:T(8,128)}, f32[2,16,48,256]{3,2,1,0:T(8,128)}, u32[]{:S(2)}, u32[]{:S(2)}) %collective-permute-start) | collective-permute-done | bytes 1572896 | tf_op jit(solution)/shard_map/ppermute | solution.py:24
  30.0 2.9 %fusion.1 = f32[2,16,127,256]{3,2,1,0:T(8,128)S(1)} fusion(s32[]{:T(128)S(6)} %select_n.3, f32[2,16,48,256]{3,2,1,0:T(8,128)} %collective-permute-done, f32[2,16,64,256]{3,2,1,0:T(8,128)S(1)} %get-tuple-element.5, f32[2,16,48,256]{3,2,1,0:T(8,128)} %collective-permute-done.1), kind=kLoop, calls=%fused_computation.4 | loop fusion | flops 2080768 | bytes 9404420 | tf_op jit(solution)/shard_map/concatenate | solution.py:22
  32.9 1.4 %fusion.12 = f32[16,64,256]{2,1,0:T(8,128)S(1)} fusion(f32[2,16,127,256]{3,2,1,0:T(8,128)S(1)} %fusion.1, f32[16,127,64]{1,0,2:T(8,128)S(1)} %get-tuple-element.12), kind=kOutput, calls=%fused_computation.31 | convolution fusion | flops 399507456 | bytes 3670016 | tf_op jit(solution)/shard_map/fjc,fjs->fcs/dot_general | solution.py:57
  34.3 1.4 %fusion.13 = f32[16,64,256]{2,1,0:T(8,128)S(1)} fusion(f32[2,16,127,256]{3,2,1,0:T(8,128)S(1)} %fusion.1, f32[16,127,64]{1,0,2:T(8,128)S(1)} %get-tuple-element.13), kind=kOutput, calls=%fused_computation.32 | convolution fusion | flops 399507456 | bytes 3670016 | tf_op jit(solution)/shard_map/fjc,fjs->fcs/dot_general | solution.py:54
  35.7 1.4 %fusion.20 = f32[1,16,64,256]{3,2,1,0:T(8,128)S(1)} fusion(f32[16,64,256]{2,1,0:T(8,128)S(1)} %fusion.12, f32[2,16,127,256]{3,2,1,0:T(8,128)S(1)} %fusion.1, f32[16,127,64]{1,0,2:T(8,128)S(1)} %get-tuple-element.13), kind=kOutput, calls=%fused_computation.37 | convolution fusion | flops 399769600 | bytes 4718592 | tf_op jit(solution)/shard_map/fjc,fjs->fcs/dot_general | solution.py:55
  37.1 1.4 %fusion.18 = f32[1,16,64,256]{3,2,1,0:T(8,128)S(1)} fusion(f32[16,64,256]{2,1,0:T(8,128)S(1)} %fusion.13, f32[2,16,127,256]{3,2,1,0:T(8,128)S(1)} %fusion.1, f32[16,127,64]{1,0,2:T(8,128)S(1)} %get-tuple-element.12), kind=kOutput, calls=%fused_computation.35 | convolution fusion | flops 399769600 | bytes 4718592 | tf_op jit(solution)/shard_map/fjc,fjs->fcs/dot_general | solution.py:52
  38.6 1.4 %fusion.21 = (f32[2,16,64,2]{3,2,1,0:T(8,128)}, f32[2,16,64,2]{3,2,1,0:T(8,128)S(1)}) fusion(f32[1,16,64,256]{3,2,1,0:T(8,128)S(1)} %fusion.18, f32[1,16,64,256]{3,2,1,0:T(8,128)S(1)} %fusion.20), kind=kLoop, calls=%fused_computation.38 | loop fusion | flops 8192 | bytes 2129920 | tf_op jit(solution)/shard_map/stack | solution.py:58
  39.9 0.0 copy-start
  39.9 1.6 %copy.35 = f32[2,16,64,2]{2,1,3,0:T(8,128)S(1)} copy(f32[2,16,64,2]{3,2,1,0:T(8,128)} %get-tuple-element.8) | data formatting | bytes 32768 | tf_op jit(solution)/shard_map/slice | solution.py:21
  41.5 0.4 copy.37
  41.9 1.3 %collective-permute-start.3 = (f32[2,16,64,2]{2,1,3,0:T(8,128)S(1)}, f32[2,16,64,2]{2,1,3,0:T(8,128)S(1)}, u32[]{:S(2)}, u32[]{:S(2)}) collective-permute-start(f32[2,16,64,2]{2,1,3,0:T(8,128)S(1)} %copy.37), channel_id=1, source_target_pairs={{32,0},{64,32},{96,64},{128,96},{160,128},{192,160},{224,192},{33,... | collective-permute-start | bytes 49160 | tf_op jit(solution)/shard_map/ppermute | solution.py:26
  43.2 5.7 %collective-permute-start.2 = (f32[2,16,64,2]{2,1,3,0:T(8,128)S(1)}, f32[2,16,64,2]{2,1,3,0:T(8,128)S(1)}, u32[]{:S(2)}, u32[]{:S(2)}) collective-permute-start(f32[2,16,64,2]{2,1,3,0:T(8,128)S(1)} %copy.35), channel_id=1, source_target_pairs={{0,32},{32,64},{64,96},{96,128},{128,160},{160,192},{192,224},{1,3... | collective-permute-start | bytes 49160 | tf_op jit(solution)/shard_map/ppermute | solution.py:24
  48.9 0.0 copy-done
  48.9 0.7 fusion.32
  49.6 0.1 collective-permute-done.2
  49.7 0.4 copy.36
  50.1 0.0 collective-permute-done.3
  50.1 1.4 %copy.38 = f32[2,16,64,2]{3,2,1,0:T(8,128)} copy(f32[2,16,64,2]{2,1,3,0:T(8,128)S(1)} %collective-permute-done.3) | data formatting | bytes 32768 | tf_op jit(solution)/shard_map/ppermute | solution.py:26
  51.5 2.3 %maximum_maximum_fusion = (f32[2,16,64,258]{3,2,1,0:T(8,128)S(1)}, f32[2,16,64,258]{3,2,1,0:T(8,128)S(1)}) fusion(f32[1,16,64,256]{3,2,1,0:T(8,128)S(1)} %fusion.20, f32[1,16,64,256]{3,2,1,0:T(8,128)S(1)} %fusion.18, f32[2,16,64,2]{3,2,1,0:T(8,128)S(1)} %copy.36, f32[2,16,64,2]{3,2,1,0:T(8,128)} %copy.38), kind=kLoop, calls=%fused_computation.5 | loop fusion | flops 2113536 | bytes 6356992 | tf_op jit(solution)/shard_map/concatenate | solution.py:22
  53.8 6.1 %multiply_reduce_fusion = (f32[16]{0:T(128)S(1)}, f32[2,16,64,256]{3,2,1,0:T(8,128)}) fusion(f32[2,16,64,258]{3,2,1,0:T(8,128)S(1)} %get-tuple-element.7, f32[]{:T(128)} %bitcast.16, f32[]{:T(128)} %bitcast.15, f32[1,16,64,256]{3,2,1,0:T(8,128)S(1)} %fusion.20, f32[1,16,64,256]{3,2,1,0:T(8,128)S(1)} %fusion.18, f32[]{:T(128)} %bitcast.14, ...), kind=kLoop, calls=%fused_computation.24 | loop fusion | flops 6291440 | bytes 12582996 | tf_op jit(solution)/shard_map/reduce_sum | solution.py:87
  60.0 0.1 maximum_bitcast_fusion
  60.1 0.1 broadcast_in_dim.8
  60.2 32.0 %all_to_all.5 = f32[256,1,128]{2,1,0:T(1,128)S(1)} all-to-all(f32[256,1,128]{2,1,0:T(1,128)S(1)} %broadcast_in_dim.8), channel_id=1, replica_groups=mesh['src_0'=4,'src_1'=2,'rcv_0'=2,'rcv_1'=8,'rcv_2'=2] {'src_0','src_1'..., dimensions={0} | all-to-all | bytes 262144 | tf_op jit(solution)/shard_map/all_to_all | solution.py:36
  92.2 0.1 sqrt_bitcast_fusion
  92.3 4.1 %multiply_subtract_fusion = f32[2,16,64,256]{3,2,1,0:T(8,128)} fusion(f32[2,16,64,256]{3,2,1,0:T(8,128)} %param.5, f32[2,16,64,256]{3,2,1,0:T(8,128)} %get-tuple-element.3, f32[16]{0:T(128)S(1)} %sqrt_bitcast_fusion), kind=kLoop, calls=%fused_computation.23 | loop fusion | flops 1048576 | bytes 6291520 | tf_op jit(solution)/shard_map/sub | solution.py:93
  (3 shorter events, 0.1 us)
Async XLA Ops:
  5.3 23.3 %collective-permute-start.1 = (f32[2,16,48,256]{3,2,1,0:T(8,128)}, f32[2,16,48,256]{3,2,1,0:T(8,128)}, u32[]{:S(2)}, u32[]{:S(2)}) collective-permute-start(f32[2,16,48,256]{3,2,1,0:T(8,128)} %get-tuple-element.10), channel_id=1, source_target_pairs={{1,0},{2,1},{3,2},{4,3},{5,4},{6,5},{7,6},{8,7},{9,8},{10,9},{11,1... | collective-permute-start | bytes 4718600 | tf_op jit(solution)/shard_map/ppermute | solution.py:26
  10.4 19.6 %collective-permute-start = (f32[2,16,48,256]{3,2,1,0:T(8,128)}, f32[2,16,48,256]{3,2,1,0:T(8,128)}, u32[]{:S(2)}, u32[]{:S(2)}) collective-permute-start(f32[2,16,48,256]{3,2,1,0:T(8,128)} %get-tuple-element.11), channel_id=1, source_target_pairs={{0,1},{1,2},{2,3},{3,4},{4,5},{5,6},{6,7},{7,8},{8,9},{9,10},{10,1... | collective-permute-start | bytes 4718600 | tf_op jit(solution)/shard_map/ppermute | solution.py:24
  39.9 9.0 %copy-start = (f32[5]{0:T(128)S(1)}, f32[5]{0:T(128)}, u32[]{:S(2)}) copy-start(f32[5]{0:T(128)} %param.9) | copy-start | bytes 64
  41.9 8.2 %collective-permute-start.3 = (f32[2,16,64,2]{2,1,3,0:T(8,128)S(1)}, f32[2,16,64,2]{2,1,3,0:T(8,128)S(1)}, u32[]{:S(2)}, u32[]{:S(2)}) collective-permute-start(f32[2,16,64,2]{2,1,3,0:T(8,128)S(1)} %copy.37), channel_id=1, source_target_pairs={{32,0},{64,32},{96,64},{128,96},{160,128},{192,160},{224,192},{33,... | collective-permute-start | bytes 49160 | tf_op jit(solution)/shard_map/ppermute | solution.py:26
  43.2 6.5 %collective-permute-start.2 = (f32[2,16,64,2]{2,1,3,0:T(8,128)S(1)}, f32[2,16,64,2]{2,1,3,0:T(8,128)S(1)}, u32[]{:S(2)}, u32[]{:S(2)}) collective-permute-start(f32[2,16,64,2]{2,1,3,0:T(8,128)S(1)} %copy.35), channel_id=1, source_target_pairs={{0,32},{32,64},{64,96},{96,128},{128,160},{160,192},{192,224},{1,3... | collective-permute-start | bytes 49160 | tf_op jit(solution)/shard_map/ppermute | solution.py:24

commit v2 on v0

v2 whole, which is shorter than its diff:
```python
import functools

import jax
import jax.numpy as jnp
from jax import lax
from jax.experimental import pallas as pl
from jax.experimental.pallas import tpu as pltpu
from jax.sharding import Mesh
from jax.sharding import PartitionSpec as P

APER = 64
SHIFT = 16
BLOCK = 64
SHALF = 2
HALO = APER // 2 + SHIFT
LANES = 128
RCV = ("rcv_0", "rcv_1", "rcv_2")
SRC = ("src_0", "src_1")
SRC_RCV = ("src_0", "src_1", "rcv_0", "rcv_1", "rcv_2")
F32 = jnp.float32
BF16 = jnp.bfloat16


def iota(shape, dim):
    return lax.broadcasted_iota(jnp.int32, shape, dim)


def split(x):
    high = x.astype(BF16)
    return high, (x - high.astype(F32)).astype(BF16)


def product(a, b, transposed=False):
    dims = (((1,), (1 if transposed else 0,)), ((), ()))
    dot = functools.partial(lax.dot_general, dimension_numbers=dims, preferred_element_type=F32)
    return dot(a[0], b[0]) + (dot(a[0], b[1]) + dot(a[1], b[0]))


def mask_column(mask_ref):
    row = jnp.broadcast_to(mask_ref[...].astype(F32), (BLOCK, BLOCK))
    diagonal = iota((BLOCK, BLOCK), 0) == iota((BLOCK, BLOCK), 1)
    return jnp.sum(jnp.where(diagonal, row, 0.0), axis=1, keepdims=True)


def prepare_kernel(wave_ref, mask_ref, left_ref, right_ref, first_ref, last_ref):
    mask = mask_column(mask_ref)
    shots = wave_ref.shape[3]
    picked = iota((8, shots), 0)
    picked = jnp.where(picked < SHALF, picked, picked + (shots - 8))
    select = (iota((8, shots), 1) == picked).astype(F32)
    for f in range(wave_ref.shape[1]):
        parts = []
        for x in range(2):
            masked = wave_ref[x, f] * mask
            left_ref[x, f] = masked[:HALO]
            right_ref[x, f] = masked[BLOCK - HALO :]
            parts.append(masked)
        ends = lax.dot_general(
            select,
            jnp.concatenate(parts, axis=0),
            (((1,), (1,)), ((), ())),
            precision=lax.Precision.HIGHEST,
            preferred_element_type=F32,
        )
        first_ref[:, f * LANES : (f + 1) * LANES] = ends[:SHALF]
        last_ref[:, f * LANES : (f + 1) * LANES] = ends[8 - SHALF :]


def own_kernel(shift_ref, wave_ref, mask_ref, band_ref, oh_ref, ol_ref, hh_ref, hl_ref, pred_ref, energy_ref):
    shift = shift_ref[0]
    mask = mask_column(mask_ref)
    low_half = iota((BLOCK, LANES), 1) < APER
    from_left = iota((2 * BLOCK, LANES), 0) % BLOCK + shift < APER // 2
    for f in range(wave_ref.shape[1]):
        at = (f // 2) * LANES
        near, far = (96, 32) if f % 2 == 0 else (32, 96)
        rolled = []
        for x in range(2):
            taps = jnp.where(low_half == (f % 2 == 0), band_ref[x, :, at : at + LANES], 0.0)
            skewed = pltpu.roll(taps, 0, 1, stride=1, stride_axis=0)
            for base in (near, far):
                rolled.append(pltpu.roll(skewed, shift + base, 1))
        real, real_far, imag, imag_far = rolled
        own = jnp.concatenate(
            [jnp.where(low_half, real, -imag_far), jnp.where(low_half, imag, real_far)], axis=0
        )
        halo = jnp.concatenate(
            [jnp.where(low_half, real_far, -imag), jnp.where(low_half, imag_far, real)], axis=0
        )
        halo = jnp.concatenate(
            [jnp.where(from_left, halo, 0.0), jnp.where(from_left, 0.0, halo)], axis=1
        )
        own = split(own)
        oh_ref[f], ol_ref[f] = own
        hh_ref[f], hl_ref[f] = split(halo)
        waves = [wave_ref[x, f] for x in range(2)]
        squares = jnp.sum(waves[0] * waves[0] + waves[1] * waves[1], axis=0, keepdims=True)
        energy_ref[f : f + 1, :] = squares[:, :LANES] + squares[:, LANES:]
        masked = jnp.concatenate([w * mask for w in waves], axis=0)
        pred_ref[f] = product(own, split(masked))


def finish_kernel(
    taper_ref, pred_ref, oh_ref, ol_ref, hh_ref, hl_ref, left_ref, right_ref, after_ref, before_ref, lends_ref,
    rends_ref, mult_ref, energy_ref, ends_ref,
):
    gap = jnp.zeros((BLOCK - HALO, pred_ref.shape[2]), F32)
    lane = iota((2 * BLOCK, LANES), 1)
    weights = [taper_ref[u] for u in range(2 * SHALF + 1)]
    row = iota((8, 3 * LANES), 0)
    ends_ref[...] = jnp.zeros_like(ends_ref)
    middle = jnp.zeros((LANES - 16, 3 * LANES), F32)
    for f in range(pred_ref.shape[0]):
        at = slice(f * LANES, (f + 1) * LANES)
        window = jnp.concatenate(
            [gap, left_ref[0, f], gap, left_ref[1, f], right_ref[0, f], gap, right_ref[1, f], gap], axis=0
        )
        halo = (hh_ref[f], hl_ref[f])
        pred = pred_ref[f] + product(halo, split(window))
        for part, (first, last) in enumerate(
            [
                (after_ref[:, at], before_ref[:, at]),
                (lends_ref[:SHALF, at], lends_ref[SHALF:, at]),
                (rends_ref[:SHALF, at], rends_ref[SHALF:, at]),
            ]
        ):
            ends_ref[f, :SHALF, part * LANES : (part + 1) * LANES] = first
            ends_ref[f, 8 - SHALF :, part * LANES : (part + 1) * LANES] = last
        ends = ends_ref[f]
        ends = jnp.concatenate(
            [jnp.where(row < SHALF, ends, 0.0), middle, jnp.where(row >= 8 - SHALF, ends, 0.0)], axis=0
        )
        band = tuple(
            jnp.concatenate([own_ref[f], halo_ref[f]], axis=1)
            for own_ref, halo_ref in ((oh_ref, hh_ref), (ol_ref, hl_ref))
        )
        edge = product(band, split(ends), transposed=True)
        head, tail = pred[:, :LANES], pred[:, LANES:]
        shots = pred.shape[1]
        total = weights[SHALF] * pred
        for u in range(1, SHALF + 1):
            earlier = jnp.concatenate([head, jnp.where(lane >= LANES - u, edge, tail)], axis=1)
            later = jnp.concatenate([jnp.where(lane < u, edge, head), tail], axis=1)
            total = total + weights[SHALF - u] * pltpu.roll(earlier, u, 1)
            total = total + weights[SHALF + u] * pltpu.roll(later, shots - u, 1)
        mult_ref[0, f] = total[:BLOCK]
        mult_ref[1, f] = total[BLOCK:]
        squares = jnp.sum(total * total, axis=0, keepdims=True)
        energy_ref[f : f + 1, :] = squares[:, :LANES] + squares[:, LANES:]


def subtract_kernel(total_ref, wave_ref, mult_ref, out_ref):
    slices = wave_ref.shape[1]
    sums = jnp.sum(total_ref[...], axis=0, keepdims=True)
    lane = iota((1, LANES), 1)
    first = pl.program_id(0) * slices
    count = pl.num_programs(0) * slices
    for f in range(slices):
        data = jnp.sum(jnp.where(lane == first + f, sums, 0.0), axis=1, keepdims=True)
        pred = jnp.sum(jnp.where(lane == first + f + count, sums, 0.0), axis=1, keepdims=True)
        gain = jnp.sqrt((data + 1e-06) / (pred + 1e-06))
        for x in range(2):
            out_ref[x, f] = wave_ref[x, f] - gain * mult_ref[x, f]


def cells(slices, rows, shots):
    return pl.BlockSpec((2, slices, rows, shots), lambda i: (0, i, 0, 0))


def stacked(slices, rows, columns):
    return pl.BlockSpec((slices, rows, columns), lambda i: (i, 0, 0))


def lanes(rows, slices):
    return pl.BlockSpec((rows, slices * LANES), lambda i: (0, i))


SMEM = pl.BlockSpec(memory_space=pltpu.SMEM)


def whole(shape):
    return pl.BlockSpec(shape, lambda i: (0,) * len(shape))


def call(kernel, steps, in_specs, outs, name, flops, scratch=()):
    return pl.pallas_call(
        kernel,
        grid=(steps,),
        in_specs=in_specs,
        out_specs=[spec for spec, _, _ in outs],
        out_shape=[jax.ShapeDtypeStruct(shape, dtype) for _, shape, dtype in outs],
        scratch_shapes=list(scratch),
        name=name,
        cost_estimate=pl.CostEstimate(flops=flops, transcendentals=0, bytes_accessed=1 << 20),
        compiler_params=pltpu.CompilerParams(dimension_semantics=("arbitrary",)),
    )


def neighbours(axis):
    count = lax.axis_size(axis)
    up = [(i, i + 1) for i in range(count - 1)]
    return up, [(j, i) for i, j in up]


def per_device(wavefield, surface_band, band_shift, trace_mask, shot_taper):
    _, slices, receivers, shots = wavefield.shape
    rcv_up, rcv_down = neighbours(RCV)
    src_up, src_down = neighbours(SRC)
    mask = trace_mask.reshape(1, receivers)

    step = 4
    steps = slices // step
    to_left, to_right, first, last = call(
        prepare_kernel,
        steps,
        [cells(step, receivers, shots), whole((1, receivers))],
        [
            (cells(step, HALO, shots), (2, slices, HALO, shots), F32),
            (cells(step, HALO, shots), (2, slices, HALO, shots), F32),
            (lanes(SHALF, step), (SHALF, slices * LANES), F32),
            (lanes(SHALF, step), (SHALF, slices * LANES), F32),
        ],
        "prepare",
        1 << 20,
    )(wavefield, mask)
    from_right = lax.ppermute(to_left, RCV, rcv_down)
    from_left = lax.ppermute(to_right, RCV, rcv_up)
    after = lax.ppermute(first, SRC, src_down)
    before = lax.ppermute(last, SRC, src_up)
    ends = jnp.concatenate([after, before], axis=0)
    right_ends = lax.ppermute(ends, RCV, rcv_down)
    left_ends = lax.ppermute(ends, RCV, rcv_up)

    matrix = 2 * receivers
    own_high, own_low, halo_high, halo_low, predicted, data_energy = call(
        own_kernel,
        2,
        [
            SMEM,
            cells(8, receivers, shots),
            whole((1, receivers)),
            pl.BlockSpec((2, receivers, 8 * APER), lambda i: (0, 0, i)),
        ],
        [
            (stacked(8, matrix, LANES), (slices, matrix, LANES), BF16),
            (stacked(8, matrix, LANES), (slices, matrix, LANES), BF16),
            (stacked(8, matrix, 2 * LANES), (slices, matrix, 2 * LANES), BF16),
            (stacked(8, matrix, 2 * LANES), (slices, matrix, 2 * LANES), BF16),
            (stacked(8, matrix, shots), (slices, matrix, shots), F32),
            (pl.BlockSpec((8, LANES), lambda i: (i, 0)), (slices, LANES), F32),
        ],
        "own",
        1 << 28,
    )(band_shift, wavefield, mask, surface_band)

    multiples, pred_energy = call(
        finish_kernel,
        2,
        [
            SMEM,
            stacked(8, matrix, shots),
            stacked(8, matrix, LANES),
            stacked(8, matrix, LANES),
            stacked(8, matrix, 2 * LANES),
            stacked(8, matrix, 2 * LANES),
            cells(8, HALO, shots),
            cells(8, HALO, shots),
            lanes(SHALF, 8),
            lanes(SHALF, 8),
            lanes(2 * SHALF, 8),
            lanes(2 * SHALF, 8),
        ],
        [
            (cells(8, receivers, shots), (2, slices, receivers, shots), F32),
            (pl.BlockSpec((8, LANES), lambda i: (i, 0)), (slices, LANES), F32),
        ],
        "finish",
        1 << 28,
        [pltpu.VMEM((8, 8, 3 * LANES), F32)],
    )(
        shot_taper, predicted, own_high, own_low, halo_high, halo_low, from_left, from_right, after, before,
        left_ends, right_ends,
    )

    partial = jnp.sum(jnp.concatenate([data_energy, pred_energy], axis=0), axis=1)[None, None]
    partial = jnp.pad(partial, ((0, 0), (0, 0), (0, LANES - partial.shape[2])))
    devices = lax.axis_size(SRC_RCV)
    spread = jnp.broadcast_to(partial, (devices, 1, LANES))
    energies = lax.all_to_all(spread, SRC_RCV, 0, 0, tiled=True).reshape(devices, LANES)

    (primaries,) = call(
        subtract_kernel,
        steps,
        [whole((devices, LANES)), cells(step, receivers, shots), cells(step, receivers, shots)],
        [(cells(step, receivers, shots), (2, slices, receivers, shots), F32)],
        "subtract",
        1 << 20,
    )(energies, wavefield, multiples)
    return (multiples, primaries)


def solution(mesh):
    split_mesh = Mesh(
        mesh.devices.reshape(4, 2, 2, 8, 2), ("src_0", "src_1", "rcv_0", "rcv_1", "rcv_2")
    )
    return jax.shard_map(
        per_device,
        mesh=split_mesh,
        in_specs=(P(None, None, RCV, SRC), P(None, RCV, None), P(RCV), P(RCV), P()),
        out_specs=(P(None, None, RCV, SRC), P(None, None, RCV, SRC)),
        check_vma=False,
    )
```

time: 116 us -> 84.5 us (0.73)
  blocking collectives: 51.1 us -> 24.2 us
  Pallas kernels: 0 us -> 20.8 us
  other arithmetic: 19.6 us -> 0.82 us
  matrix products: 6.8 us -> 0 us
  local copies, waits for them, and re-layouts: 7.87 us -> 1.68 us
  starting transfers between devices: 14 us -> 19.2 us
  waiting for transfers between devices: 14.5 us -> 15.9 us
    psum x5 -> x0, blocking collectives: 51.1 us -> none  [by_axis(): return functools.reduce(lax.psum, axes, array)]
    all_to_all x0 -> x1, blocking collectives: none -> 24.2 us  [per_device(): lax.all_to_all(spread, SRC_RCV, 0, 0, tiled=True).reshape(devices, LANES)]
    pallas_call x0 -> x4, Pallas kernels: none -> 20.8 us  [the longest x1 6.66 us: per_device(): call(finish_kernel, 2, [SMEM, stacked(8, matrix, shots), stacked(8, matri...]
    reduce_sum x2 -> x1, other arithmetic: 8.22 us -> 0.81 us  [per_device(): jnp.sum(jnp.concatenate([data_energy, pred_energy], axis=0), axis=1)]
    dot_general x5 -> x0, matrix products: 6.8 us -> none  [the longest x1 1.4 us: complex_product(): jnp.einsum('fjc,fjs->fcs', band[1], window[0], precision=lax.Precision.HI...]
    concatenate x2 -> x1, other arithmetic: 5.24 us -> 0.02 us  [per_device(): ends = jnp.concatenate([after, before], axis=0)]
    ppermute x4 -> x6, starting transfers between devices: 14 us -> 19.2 us  [the longest x1 5.49 us: per_device(): before = lax.ppermute(last, SRC, src_up)]
    slice x4 -> x0, local copies, waits for them, and re-layouts: 4.7 us -> none  [the longest x2 2.45 us: extended(): head = lax.slice_in_dim(cells, 0, width, axis=dim)]
  transfers between devices with their start and end apart: 4 -> 6, of which waited for: 3 -> 1; matrix products, arithmetic and copies ran while one was open for 3% -> 0% of each run, Pallas kernels for 0% -> 5%
where the time goes in v2:
time: 84.5 us; the launch traced here: 84 us
  blocking collectives  24.2 us (29%)
  Pallas kernels  20.8 us (25%)
  starting transfers between devices  19.2 us (23%)
  waiting for transfers between devices  15.9 us (19%)
  local copies, waits for them, and re-layouts  1.68 us (2%)
  between operations  1.43 us (2%)
    all_to_all x1, blocking collectives, per_device(): lax.all_to_all(spread, SRC_RCV, 0, 0, tiled=True).reshape(devices, LANES)  24.2 us
    ppermute x1, waiting for transfers between devices, per_device(): after = lax.ppermute(first, SRC, src_down)  15.9 us
    pallas_call x1, Pallas kernels, per_device(): call(finish_kernel, 2, [SMEM, stacked(8, matrix, shots), stacked(8, matri...  6.66 us
    ppermute x1, starting transfers between devices, per_device(): before = lax.ppermute(last, SRC, src_up)  5.49 us
    pallas_call x1, Pallas kernels, per_device(): call(prepare_kernel, steps, [cells(step, receivers, shots), whole((1, rec...  5.28 us
    ppermute x1, starting transfers between devices, per_device(): from_left = lax.ppermute(to_right, RCV, rcv_up)  4.91 us
    pallas_call x1, Pallas kernels, per_device(): call(subtract_kernel, steps, [whole((devices, LANES)), cells(step, receiv...  4.45 us
    pallas_call x1, Pallas kernels, per_device(): call(own_kernel, 2, [SMEM, cells(8, receivers, shots), whole((1, receiver...  4.43 us
  transfers between devices with their start and end apart: 6, of which 1 were waited for; matrix products, arithmetic and copies ran while one was open for 0% of the time, Pallas kernels for 5%

profile of v2, /device:TPU:1, one launch (start us, length us, event | category | flops | bytes accessed | tf_op | source)
XLA Modules:
  0.0 84.0 jit_solution(11791855535155469184)
XLA Ops:
  0.6 5.3 %prepare.1 = (f32[2,16,48,256]{3,2,1,0:T(8,128)}, f32[2,16,48,256]{3,2,1,0:T(8,128)}, f32[2,2048]{1,0:T(2,128)}, f32[2,2048]{1,0:T(2,128)}) custom-call(f32[2,16,64,256]{3,2,1,0:T(8,128)} %wave_ref.5, s32[1,64]{1,0:T(1,128)} %bitcast.6), custom_call_target="tpu_custom_call" | custom-call | flops 1048576 | bytes 1048576 | tf_op jit(solution)/shard_map/prepare/pallas_call | solution.py:213
  5.9 4.9 %collective-permute-start = (f32[2,16,48,256]{3,2,1,0:T(8,128)}, f32[2,16,48,256]{3,2,1,0:T(8,128)S(1)}, u32[]{:S(2)}, u32[]{:S(2)}) collective-permute-start(f32[2,16,48,256]{3,2,1,0:T(8,128)} %get-tuple-element.19), channel_id=1, source_target_pairs={{0,1},{1,2},{2,3},{3,4},{4,5},{5,6},{6,7},{7,8},{8,9},{9,10},{10,1... | collective-permute-start | bytes 4718600 | tf_op jit(solution)/shard_map/ppermute | solution.py:227
  10.8 1.9 %collective-permute-start.1 = (f32[2,16,48,256]{3,2,1,0:T(8,128)}, f32[2,16,48,256]{3,2,1,0:T(8,128)S(1)}, u32[]{:S(2)}, u32[]{:S(2)}) collective-permute-start(f32[2,16,48,256]{3,2,1,0:T(8,128)} %get-tuple-element.20), channel_id=1, source_target_pairs={{1,0},{2,1},{3,2},{4,3},{5,4},{6,5},{7,6},{8,7},{9,8},{10,9},{11,1... | collective-permute-start | bytes 4718600 | tf_op jit(solution)/shard_map/ppermute | solution.py:226
  12.8 1.3 %collective-permute-start.2 = (f32[2,2048]{1,0:T(2,128)}, f32[2,2048]{1,0:T(2,128)S(1)}, u32[]{:S(2)}, u32[]{:S(2)}) collective-permute-start(f32[2,2048]{1,0:T(2,128)} %get-tuple-element.21), channel_id=1, source_target_pairs={{32,0},{64,32},{96,64},{128,96},{160,128},{192,160},{224,192},{33,... | collective-permute-start | bytes 49160 | tf_op jit(solution)/shard_map/ppermute | solution.py:228
  14.1 5.5 %collective-permute-start.3 = (f32[2,2048]{1,0:T(2,128)}, f32[2,2048]{1,0:T(2,128)S(1)}, u32[]{:S(2)}, u32[]{:S(2)}) collective-permute-start(f32[2,2048]{1,0:T(2,128)} %get-tuple-element.22), channel_id=1, source_target_pairs={{0,32},{32,64},{64,96},{96,128},{128,160},{160,192},{192,224},{1,3... | collective-permute-start | bytes 49160 | tf_op jit(solution)/shard_map/ppermute | solution.py:229
  19.6 15.9 %collective-permute-done.2.after_ref = f32[2,2048]{1,0:T(2,128)S(1)} collective-permute-done((f32[2,2048]{1,0:T(2,128)}, f32[2,2048]{1,0:T(2,128)S(1)}, u32[]{:S(2)}, u32[]{:S(2)}) %collective-permute-start.2) | collective-permute-done | bytes 16416 | tf_op jit(solution)/shard_map/ppermute | solution.py:228
  35.4 0.0 copy-start.2
  35.4 0.0 collective-permute-done.3.before_ref
  35.4 0.0 copy-start.3
  35.5 2.3 %collective-permute-start.5 = (f32[4,2048]{1,0:T(4,128)S(1)}, f32[4,2048]{1,0:T(4,128)S(1)}, u32[]{:S(2)}, u32[]{:S(2)}) collective-permute-start(f32[4,2048]{1,0:T(4,128)S(1)} %pad_maximum_fusion), channel_id=1, source_target_pairs={{1,0},{2,1},{3,2},{4,3},{5,4},{6,5},{7,6},{8,7},{9,8},{10,9},{11,1... | collective-permute-start | bytes 98312 | tf_op jit(solution)/shard_map/ppermute | solution.py:231
  37.8 3.3 %collective-permute-start.4 = (f32[4,2048]{1,0:T(4,128)S(1)}, f32[4,2048]{1,0:T(4,128)S(1)}, u32[]{:S(2)}, u32[]{:S(2)}) collective-permute-start(f32[4,2048]{1,0:T(4,128)S(1)} %pad_maximum_fusion), channel_id=1, source_target_pairs={{0,1},{1,2},{2,3},{3,4},{4,5},{5,6},{6,7},{7,8},{8,9},{9,10},{10,1... | collective-permute-start | bytes 98312 | tf_op jit(solution)/shard_map/ppermute | solution.py:232
  41.7 4.4 %own.1 = (bf16[16,128,128]{2,1,0:T(8,128)(2,1)}, bf16[16,128,128]{2,1,0:T(8,128)(2,1)}, bf16[16,128,256]{2,1,0:T(8,128)(2,1)}, bf16[16,128,256]{2,1,0:T(8,128)(2...) custom-call(s32[1]{0:T(128)S(6)} %copy.7.shift_ref, f32[2,16,64,256]{3,2,1,0:T(8,128)} %wave_ref.5, s32[1,64]{1,0:T(1,128)} %bitcast.7, ...), custom_call_target="tpu_custom_call" | custom-call | flops 268435456 | bytes 1048576 | tf_op jit(solution)/shard_map/own/pallas_call | solution.py:235
  46.1 0.0 collective-permute-done.5.rends_ref
  46.1 0.0 copy-start.4
  46.1 0.0 collective-permute-done.4.lends_ref
  46.1 0.0 copy-start.5
  46.2 0.0 collective-permute-done.left_ref
  46.2 0.0 copy-start
  46.2 0.0 collective-permute-done.1.right_ref
  46.2 0.0 copy-start.1
  46.2 0.0 copy-done.2
  46.2 0.0 copy-done.3
  46.2 0.5 copy-done.4
  46.7 0.0 copy-done.5
  46.7 0.6 copy-done
  47.3 0.5 copy-done.1
  47.8 0.0 copy-start.6
  47.8 6.7 %finish.1 = (f32[2,16,64,256]{3,2,1,0:T(8,128)}, f32[16,128]{1,0:T(8,128)}) custom-call(f32[5]{0:T(128)} %taper_ref.1, f32[16,128,256]{2,1,0:T(8,128)} %get-tuple-element.14.pred_ref, bf16[16,128,128]{2,1,0:T(8,128)(2,1)} %get-tuple-element.15.oh_ref, bf16[16,128,128]{2,1,0:T(8,128)(2,1)} %get-tuple-element.16.ol_ref, ...), custom_call_target="tpu_custom_call" | custom-call | flops 268435456 | bytes 1048576 | tf_op jit(solution)/shard_map/finish/pallas_call | solution.py:256
  54.5 0.0 copy-done.6
  54.5 0.8 maximum_reduce_fusion
  55.3 0.1 broadcast_in_dim.12
  55.4 24.2 %all_to_all.5 = f32[256,1,128]{2,1,0:T(1,128)} all-to-all(f32[256,1,128]{2,1,0:T(1,128)S(1)} %broadcast_in_dim.12), channel_id=1, replica_groups=mesh['src_0'=4,'src_1'=2,'rcv_0'=2,'rcv_1'=8,'rcv_2'=2] {'src_0','src_1'..., dimensions={0} | all-to-all | bytes 262144 | tf_op jit(solution)/shard_map/all_to_all | solution.py:289
  79.6 4.4 %subtract.1 = f32[2,16,64,256]{3,2,1,0:T(8,128)} custom-call(f32[256,128]{1,0:T(8,128)} %bitcast.5, f32[2,16,64,256]{3,2,1,0:T(8,128)} %wave_ref.5, f32[2,16,64,256]{3,2,1,0:T(8,128)} %get-tuple-element.12.mult_ref), custom_call_target="tpu_custom_call" | custom-call | flops 1048576 | bytes 1048576 | tf_op jit(solution)/shard_map/subtract/pallas_call | solution.py:291
  (2 shorter events, 0.0 us)
Async XLA Ops:
  5.9 40.3 %collective-permute-start = (f32[2,16,48,256]{3,2,1,0:T(8,128)}, f32[2,16,48,256]{3,2,1,0:T(8,128)S(1)}, u32[]{:S(2)}, u32[]{:S(2)}) collective-permute-start(f32[2,16,48,256]{3,2,1,0:T(8,128)} %get-tuple-element.19), channel_id=1, source_target_pairs={{0,1},{1,2},{2,3},{3,4},{4,5},{5,6},{6,7},{7,8},{8,9},{9,10},{10,1... | collective-permute-start | bytes 4718600 | tf_op jit(solution)/shard_map/ppermute | solution.py:227
  10.8 35.4 %collective-permute-start.1 = (f32[2,16,48,256]{3,2,1,0:T(8,128)}, f32[2,16,48,256]{3,2,1,0:T(8,128)S(1)}, u32[]{:S(2)}, u32[]{:S(2)}) collective-permute-start(f32[2,16,48,256]{3,2,1,0:T(8,128)} %get-tuple-element.20), channel_id=1, source_target_pairs={{1,0},{2,1},{3,2},{4,3},{5,4},{6,5},{7,6},{8,7},{9,8},{10,9},{11,1... | collective-permute-start | bytes 4718600 | tf_op jit(solution)/shard_map/ppermute | solution.py:226
  12.8 22.7 %collective-permute-start.2 = (f32[2,2048]{1,0:T(2,128)}, f32[2,2048]{1,0:T(2,128)S(1)}, u32[]{:S(2)}, u32[]{:S(2)}) collective-permute-start(f32[2,2048]{1,0:T(2,128)} %get-tuple-element.21), channel_id=1, source_target_pairs={{32,0},{64,32},{96,64},{128,96},{160,128},{192,160},{224,192},{33,... | collective-permute-start | bytes 49160 | tf_op jit(solution)/shard_map/ppermute | solution.py:228
  14.1 21.4 %collective-permute-start.3 = (f32[2,2048]{1,0:T(2,128)}, f32[2,2048]{1,0:T(2,128)S(1)}, u32[]{:S(2)}, u32[]{:S(2)}) collective-permute-start(f32[2,2048]{1,0:T(2,128)} %get-tuple-element.22), channel_id=1, source_target_pairs={{0,32},{32,64},{64,96},{96,128},{128,160},{160,192},{192,224},{1,3... | collective-permute-start | bytes 49160 | tf_op jit(solution)/shard_map/ppermute | solution.py:229
  35.4 10.8 %copy-start.2 = (f32[2,2048]{1,0:T(2,128)}, f32[2,2048]{1,0:T(2,128)S(1)}, u32[]{:S(2)}) copy-start(f32[2,2048]{1,0:T(2,128)S(1)} %collective-permute-done.2.after_ref) | copy-start | bytes 49156
  35.4 10.8 %copy-start.3 = (f32[2,2048]{1,0:T(2,128)}, f32[2,2048]{1,0:T(2,128)S(1)}, u32[]{:S(2)}) copy-start(f32[2,2048]{1,0:T(2,128)S(1)} %collective-permute-done.3.before_ref) | copy-start | bytes 49156
  35.5 10.7 %collective-permute-start.5 = (f32[4,2048]{1,0:T(4,128)S(1)}, f32[4,2048]{1,0:T(4,128)S(1)}, u32[]{:S(2)}, u32[]{:S(2)}) collective-permute-start(f32[4,2048]{1,0:T(4,128)S(1)} %pad_maximum_fusion), channel_id=1, source_target_pairs={{1,0},{2,1},{3,2},{4,3},{5,4},{6,5},{7,6},{8,7},{9,8},{10,9},{11,1... | collective-permute-start | bytes 98312 | tf_op jit(solution)/shard_map/ppermute | solution.py:231
  37.8 8.4 %collective-permute-start.4 = (f32[4,2048]{1,0:T(4,128)S(1)}, f32[4,2048]{1,0:T(4,128)S(1)}, u32[]{:S(2)}, u32[]{:S(2)}) collective-permute-start(f32[4,2048]{1,0:T(4,128)S(1)} %pad_maximum_fusion), channel_id=1, source_target_pairs={{0,1},{1,2},{2,3},{3,4},{4,5},{5,6},{6,7},{7,8},{8,9},{9,10},{10,1... | collective-permute-start | bytes 98312 | tf_op jit(solution)/shard_map/ppermute | solution.py:232
  46.1 0.6 copy-start.4
  46.1 0.6 copy-start.5
  46.2 1.2 %copy-start = (f32[2,16,48,256]{3,2,1,0:T(8,128)}, f32[2,16,48,256]{3,2,1,0:T(8,128)S(1)}, u32[]{:S(2)}) copy-start(f32[2,16,48,256]{3,2,1,0:T(8,128)S(1)} %collective-permute-done.left_ref) | copy-start | bytes 4718596
  46.2 1.6 %copy-start.1 = (f32[2,16,48,256]{3,2,1,0:T(8,128)}, f32[2,16,48,256]{3,2,1,0:T(8,128)S(1)}, u32[]{:S(2)}) copy-start(f32[2,16,48,256]{3,2,1,0:T(8,128)S(1)} %collective-permute-done.1.right_ref) | copy-start | bytes 4718596
  47.8 6.7 %copy-start.6 = (f32[16,128]{1,0:T(8,128)S(1)}, f32[16,128]{1,0:T(8,128)}, u32[]{:S(2)}) copy-start(f32[16,128]{1,0:T(8,128)} %get-tuple-element.24) | copy-start | bytes 24580

commit v3 on v0

v3 whole, which is shorter than its diff:
```python
import functools

import jax
import jax.numpy as jnp
from jax import lax
from jax.experimental import pallas as pl
from jax.experimental.pallas import tpu as pltpu
from jax.sharding import Mesh
from jax.sharding import PartitionSpec as P

APER = 64
SHIFT = 16
BLOCK = 64
SHALF = 2
HALO = APER // 2 + SHIFT
SPARE = BLOCK - HALO
LANES = 128
RCV = ("rcv_0", "rcv_1", "rcv_2")
SRC = ("src_0", "src_1")
SRC_RCV = ("src_0", "src_1", "rcv_0", "rcv_1", "rcv_2")
F32 = jnp.float32
BF16 = jnp.bfloat16
FIRST = 11
KEPT = 8


def iota(shape, dim):
    return lax.broadcasted_iota(jnp.int32, shape, dim)


def split(x):
    high = x.astype(BF16)
    return high, (x - high.astype(F32)).astype(BF16)


def product(a, b):
    dot = functools.partial(jnp.dot, preferred_element_type=F32)
    return dot(a[0], b[0]) + (dot(a[0], b[1]) + dot(a[1], b[0]))


def mask_column(mask_ref):
    row = jnp.broadcast_to(mask_ref[...].astype(F32), (BLOCK, BLOCK))
    diagonal = iota((BLOCK, BLOCK), 0) == iota((BLOCK, BLOCK), 1)
    return jnp.sum(jnp.where(diagonal, row, 0.0), axis=1, keepdims=True)


def is_odd():
    return lax.axis_index("rcv_2") == 1


def at_end(column, tail):
    return jnp.where(tail, column[SPARE:], column[:HALO])


def head_kernel(wave_ref, mask_ref, out_ref, held_ref, sems):
    tail = is_odd()
    start = pl.multiple_of(jnp.where(tail, SPARE, 0), 8)
    slices = wave_ref.shape[1]
    copies = []
    for i, (low, high) in enumerate([(0, FIRST), (FIRST, slices)]):
        part = pl.ds(low, high - low)
        copies.append(pltpu.make_async_copy(wave_ref.at[:, part], held_ref.at[:, part], sems.at[i]))
        copies[-1].start()
    mask = at_end(mask_column(mask_ref), tail)
    copies[0].wait()
    for x in range(2):
        for f in range(FIRST):
            out_ref[x, f] = held_ref[x, f, pl.ds(start, HALO)] * mask
    copies[1].wait()


def rest_kernel(wave_ref, mask_ref, link_ref, chip_ref, ends_ref):
    odd = is_odd()
    mask = mask_column(mask_ref)
    lane = iota((BLOCK, LANES), 1)
    slices = wave_ref.shape[1]
    ends = jnp.zeros((BLOCK, LANES), F32)
    for f in range(slices):
        for x in range(2):
            masked = wave_ref[x, f] * mask
            place = 4 * (x * slices + f)
            row = (2 * f + x) * HALO
            chip_ref[row : row + HALO] = at_end(masked, jnp.logical_not(odd))
            if f >= FIRST:
                row -= 2 * FIRST * HALO
                link_ref[row : row + HALO] = at_end(masked, odd)
            last = pltpu.roll(masked[:, -LANES:], (place + SHALF) % LANES, 1)
            first = pltpu.roll(masked[:, :LANES], place + SHALF, 1)
            ends = jnp.where(lane // 2 == place // 2, last, ends)
            ends = jnp.where(lane // 2 == place // 2 + 1, first, ends)
    ends_ref[...] = ends


def merged_ends(before_ref, after_ref):
    return jnp.where(iota((BLOCK, LANES), 1) % 4 < SHALF, before_ref[...], after_ref[...])


def pack_kernel(before_ref, after_ref, _link_in, _chip_in, link_ref, chip_ref):
    odd = is_odd()
    ends = merged_ends(before_ref, after_ref)
    for ref, tail in ((link_ref, odd), (chip_ref, jnp.logical_not(odd))):
        rows = at_end(ends, tail)
        ref[ref.shape[0] - HALO // 2 :] = jnp.concatenate([rows[: HALO // 2], rows[HALO // 2 :]], axis=1)


def band_kernel(shift_ref, wave_ref, band_ref, high_ref, low_ref, energy_ref):
    shift = shift_ref[0]
    odd = is_odd()
    low_half = iota((BLOCK, LANES), 1) < APER
    left = iota((2 * BLOCK, LANES), 0) % BLOCK + shift < APER // 2
    on_chip = left == odd
    for f in range(wave_ref.shape[1]):
        at = (f // 2) * LANES
        near, far = (96, 32) if f % 2 == 0 else (32, 96)
        rolled = []
        for x in range(2):
            taps = jnp.where(low_half == (f % 2 == 0), band_ref[x, :, at : at + LANES], 0.0)
            skewed = pltpu.roll(taps, 0, 1, stride=1, stride_axis=0)
            for base in (near, far):
                rolled.append(pltpu.roll(skewed, shift + base, 1))
        real, real_far, imag, imag_far = rolled
        own = jnp.concatenate(
            [jnp.where(low_half, real, -imag_far), jnp.where(low_half, imag, real_far)], axis=0
        )
        halo = jnp.concatenate(
            [jnp.where(low_half, real_far, -imag), jnp.where(low_half, imag_far, real)], axis=0
        )
        halo = jnp.where(left, pltpu.roll(halo, LANES - SPARE, 1), halo)
        parts = [own, jnp.where(on_chip, halo, 0.0), jnp.where(on_chip, 0.0, halo)]
        for part, value in enumerate(parts):
            high, low = split(value)
            high_ref[f, :, part * LANES : (part + 1) * LANES] = high
            low_ref[f, :, part * LANES : (part + 1) * LANES] = low
        squares = wave_ref[0, f] * wave_ref[0, f] + wave_ref[1, f] * wave_ref[1, f]
        squares = jnp.sum(squares, axis=0, keepdims=True)
        energy_ref[f : f + 1, :] = squares[:, :LANES] + squares[:, LANES:]


def finish_kernel(
    taper_ref, wave_ref, mask_ref, high_ref, low_ref, head_ref, link_ref, chip_ref, before_ref, after_ref, data_ref,
    mult_ref, spread_ref, kept_ref,
):
    slices = wave_ref.shape[1]
    shots = wave_ref.shape[3]
    mask = mask_column(mask_ref)
    lane = iota((2 * BLOCK, LANES), 1)
    weights = [taper_ref[u] for u in range(2 * SHALF + 1)]
    gap = jnp.zeros((SPARE, shots + LANES), F32)

    def unpacked(ref):
        rows = ref[ref.shape[0] - HALO // 2 :]
        return jnp.concatenate([rows[:, :LANES], rows[:, LANES:]], axis=0)

    ends = merged_ends(before_ref, after_ref)
    link_ends = unpacked(link_ref)
    chip_ends = unpacked(chip_ref)
    row = iota((1, LANES), 1)
    energies = jnp.zeros((1, LANES), F32)
    for f in range(slices):
        pieces = []
        for source in range(3):
            for x in range(2):
                place = LANES - (4 * (x * slices + f) + SHALF)
                at = (2 * f + x) * HALO
                if source == 0:
                    pieces.append(jnp.concatenate([wave_ref[x, f] * mask, pltpu.roll(ends, place, 1)], axis=1))
                    continue
                if source == 1:
                    main, edge = chip_ref[at : at + HALO], chip_ends
                elif f < FIRST:
                    main, edge = head_ref[x, f], link_ends
                else:
                    at -= 2 * FIRST * HALO
                    main, edge = link_ref[at : at + HALO], link_ends
                pieces.append(jnp.concatenate([main, pltpu.roll(edge, place, 1)], axis=1))
                pieces.append(gap)
        whole = product((high_ref[f], low_ref[f]), split(jnp.concatenate(pieces, axis=0)))
        pred, edge = whole[:, :shots], whole[:, shots:]
        head, tail = pred[:, :LANES], pred[:, LANES:]
        total = weights[SHALF] * pred
        for u in range(1, SHALF + 1):
            earlier = jnp.concatenate([head, jnp.where(lane >= LANES - u, edge, tail)], axis=1)
            later = jnp.concatenate([jnp.where(lane < u, edge, head), tail], axis=1)
            total = total + weights[SHALF - u] * pltpu.roll(earlier, u, 1)
            total = total + weights[SHALF + u] * pltpu.roll(later, shots - u, 1)
        mult_ref[0, f] = total[:BLOCK]
        mult_ref[1, f] = total[BLOCK:]
        squares = jnp.sum(total * total, axis=0, keepdims=True)
        pred_energy = jnp.sum(squares[:, :LANES] + squares[:, LANES:], axis=1, keepdims=True)
        data_energy = jnp.sum(data_ref[f : f + 1, :], axis=1, keepdims=True)
        energies = jnp.where(row == f, data_energy, energies)
        energies = jnp.where(row == slices + f, pred_energy, energies)
    spread_ref[...] = jnp.broadcast_to(energies, spread_ref.shape)
    kept_ref[...] = wave_ref[:, :KEPT]


def subtract_kernel(total_ref, kept_ref, wave_ref, mult_ref, out_ref, held_ref, in_sems, out_sems):
    slices = wave_ref.shape[1]
    reads = {}
    for f in range(KEPT, slices):
        reads[f] = pltpu.make_async_copy(wave_ref.at[:, f], held_ref.at[:, f], in_sems.at[f])
        reads[f].start()
    sums = jnp.sum(total_ref[...], axis=0, keepdims=True)
    row = iota((1, LANES), 1)
    writes = []
    for f in range(slices):
        data = jnp.sum(jnp.where(row == f, sums, 0.0), axis=1, keepdims=True)
        pred = jnp.sum(jnp.where(row == slices + f, sums, 0.0), axis=1, keepdims=True)
        gain = jnp.sqrt((data + 1e-06) / (pred + 1e-06))
        if f in reads:
            reads[f].wait()
        source_ref = held_ref if f in reads else kept_ref
        for x in range(2):
            held_ref[x, f] = source_ref[x, f] - gain * mult_ref[x, f]
        writes.append(pltpu.make_async_copy(held_ref.at[:, f], out_ref.at[:, f], out_sems.at[f]))
        writes[-1].start()
    for copy in writes:
        copy.wait()


VMEM = pl.BlockSpec(memory_space=pltpu.VMEM)
SMEM = pl.BlockSpec(memory_space=pltpu.SMEM)
HBM = pl.BlockSpec(memory_space=pltpu.HBM)
ANY = pl.BlockSpec(memory_space=pl.ANY)


def on_chip(*arrays):
    return [pltpu.with_memory_space_constraint(a, pltpu.VMEM) for a in arrays]


def call(kernel, in_specs, out_shapes, flops, out_specs=None, scratch=(), aliases=None):
    return pl.pallas_call(
        kernel,
        in_specs=in_specs,
        out_specs=out_specs or [VMEM] * len(out_shapes),
        out_shape=out_shapes,
        scratch_shapes=list(scratch),
        input_output_aliases=aliases or {},
        cost_estimate=pl.CostEstimate(flops=flops, transcendentals=0, bytes_accessed=1 << 20),
        compiler_params=pltpu.CompilerParams(vmem_limit_bytes=24 << 20),
    )


def neighbours(axis):
    count = lax.axis_size(axis)
    up = [(i, i + 1) for i in range(count - 1)]
    return up, [(j, i) for i, j in up]


def swaps(axis, first):
    count = lax.axis_size(axis)
    pairs = [(i, i + 1) for i in range(first, count - 1, 2)]
    return pairs + [(j, i) for i, j in pairs]


def per_device(wavefield, surface_band, band_shift, trace_mask, shot_taper):
    _, slices, receivers, shots = wavefield.shape
    src_up, src_down = neighbours(SRC)
    mask = trace_mask.reshape(1, receivers)
    devices = lax.axis_size(SRC_RCV)
    in_hbm = pltpu.with_memory_space_constraint(wavefield, pltpu.HBM)

    head, wave = call(
        head_kernel,
        [HBM, VMEM],
        [
            pltpu.VMEM((2, FIRST, HALO, shots), F32),
            pltpu.VMEM((2, slices, receivers, shots), F32),
        ],
        1 << 20,
        scratch=[pltpu.SemaphoreType.DMA((2,))],
    )(in_hbm, mask)
    head = lax.ppermute(head, RCV, swaps(RCV, 1))

    wave, band = on_chip(wave, surface_band)
    link, chip, ends = call(
        rest_kernel,
        [VMEM, VMEM],
        [
            pltpu.VMEM((2 * (slices - FIRST) * HALO + HALO // 2, shots), F32),
            pltpu.VMEM((2 * slices * HALO + HALO // 2, shots), F32),
            pltpu.VMEM((BLOCK, LANES), F32),
        ],
        1 << 20,
    )(wave, mask)
    after = lax.ppermute(ends, SRC, src_down)
    before = lax.ppermute(ends, SRC, src_up)

    rows = 2 * receivers
    high, low, data_energy = call(
        band_kernel,
        [SMEM, VMEM, VMEM],
        [
            pltpu.VMEM((slices, rows, 3 * LANES), BF16),
            pltpu.VMEM((slices, rows, 3 * LANES), BF16),
            pltpu.VMEM((slices, LANES), F32),
        ],
        1 << 28,
    )(band_shift, wave, band)

    before, after, link, chip = on_chip(before, after, link, chip)
    link, chip = call(
        pack_kernel,
        [VMEM, VMEM, ANY, ANY],
        [pltpu.VMEM(link.shape, F32), pltpu.VMEM(chip.shape, F32)],
        1 << 16,
        aliases={2: 0, 3: 1},
    )(before, after, link, chip)
    link = lax.ppermute(link, RCV, swaps(RCV, 1))
    chip = lax.ppermute(chip, RCV, swaps(RCV, 0))

    multiples, spread, kept = call(
        finish_kernel,
        [SMEM] + [VMEM] * 10,
        [
            pltpu.VMEM((2, slices, receivers, shots), F32),
            pltpu.VMEM((devices, LANES), F32),
            pltpu.VMEM((2, KEPT, receivers, shots), F32),
        ],
        1 << 28,
    )(shot_taper, wave, mask, *on_chip(high, low, head, link, chip), before, after, *on_chip(data_energy))

    energies = lax.all_to_all(spread[:, None], SRC_RCV, 0, 0, tiled=True).reshape(devices, LANES)

    (primaries,) = call(
        subtract_kernel,
        [VMEM, VMEM, HBM, VMEM],
        [jax.ShapeDtypeStruct((2, slices, receivers, shots), F32)],
        1 << 20,
        out_specs=[HBM],
        scratch=[pltpu.VMEM((2, slices, receivers, shots), F32)] + [pltpu.SemaphoreType.DMA((slices,))] * 2,
    )(*on_chip(energies, kept), in_hbm, *on_chip(multiples))
    return (multiples, primaries)


def solution(mesh):
    split_mesh = Mesh(
        mesh.devices.reshape(4, 2, 2, 8, 2), ("src_0", "src_1", "rcv_0", "rcv_1", "rcv_2")
    )
    return jax.shard_map(
        per_device,
        mesh=split_mesh,
        in_specs=(P(None, None, RCV, SRC), P(None, RCV, None), P(RCV), P(RCV), P()),
        out_specs=(P(None, None, RCV, SRC), P(None, None, RCV, SRC)),
        check_vma=False,
    )
```

time: 116 us -> 75.6 us (0.65)
  blocking collectives: 51.1 us -> 0 us
  other arithmetic: 19.6 us -> 0 us
  starting transfers between devices: 14 us -> 32.4 us
  Pallas kernels: 0 us -> 14.9 us
  waiting for transfers between devices: 14.5 us -> 24.7 us
  matrix products: 6.8 us -> 0 us
  local copies, waits for them, and re-layouts: 7.87 us -> 1.98 us
    psum x5 -> x0, blocking collectives: 51.1 us -> none  [by_axis(): return functools.reduce(lax.psum, axes, array)]
    all_to_all x0 -> x1, starting transfers between devices: none -> 15.5 us  [per_device(): lax.all_to_all(spread[:, None], SRC_RCV, 0, 0, tiled=True)]
    pallas_call x0 -> x6, Pallas kernels: none -> 14.9 us  [the longest x1 6.12 us: per_device(): call(finish_kernel, [SMEM] + [VMEM] * 10, [pltpu.VMEM((2, slices, receive...]
    all_to_all x0 -> x1, waiting for transfers between devices: none -> 11.5 us  [per_device(): lax.all_to_all(spread[:, None], SRC_RCV, 0, 0, tiled=True)]
    reduce_sum x2 -> x0, other arithmetic: 8.22 us -> none  [the longest x1 6.24 us: per_device(): pred_energy = jnp.sum(multiples * multiples, axis=(0, 2, 3))]
    dot_general x5 -> x0, matrix products: 6.8 us -> none  [the longest x1 1.4 us: complex_product(): jnp.einsum('fjc,fjs->fcs', band[1], window[0], precision=lax.Precision.HI...]
    concatenate x2 -> x0, other arithmetic: 5.24 us -> none  [extended(): jnp.concatenate([lax.ppermute(tail, axis, [(i, (i + 1) % count) for i in...]
    slice x4 -> x0, local copies, waits for them, and re-layouts: 4.7 us -> none  [the longest x2 2.45 us: extended(): head = lax.slice_in_dim(cells, 0, width, axis=dim)]
  transfers between devices with their start and end apart: 4 -> 6, of which waited for: 3 -> 3; matrix products, arithmetic and copies ran while one was open for 3% -> 2% of each run, Pallas kernels for 0% -> 5%
where the time goes in v3:
time: 75.6 us; the launch traced here: 75.3 us
  starting transfers between devices  32.4 us (43%)
  waiting for transfers between devices  24.7 us (33%)
  Pallas kernels  14.9 us (20%)
  local copies, waits for them, and re-layouts  1.98 us (3%)
  between operations  1.38 us (2%)
    all_to_all x1, starting transfers between devices, per_device(): lax.all_to_all(spread[:, None], SRC_RCV, 0, 0, tiled=True)  15.5 us
    ppermute x1, waiting for transfers between devices, per_device(): link = lax.ppermute(link, RCV, swaps(RCV, 1))  12.1 us
    all_to_all x1, waiting for transfers between devices, per_device(): lax.all_to_all(spread[:, None], SRC_RCV, 0, 0, tiled=True)  11.5 us
    ppermute x1, starting transfers between devices, per_device(): before = lax.ppermute(ends, SRC, src_up)  6.27 us
    pallas_call x1, Pallas kernels, per_device(): call(finish_kernel, [SMEM] + [VMEM] * 10, [pltpu.VMEM((2, slices, receive...  6.12 us
    ppermute x1, starting transfers between devices, per_device(): chip = lax.ppermute(chip, RCV, swaps(RCV, 0))  3.65 us
    pallas_call x1, Pallas kernels, per_device(): call(band_kernel, [SMEM, VMEM, VMEM], [pltpu.VMEM((slices, rows, 3 * LANE...  3.65 us
    ppermute x1, starting transfers between devices, per_device(): link = lax.ppermute(link, RCV, swaps(RCV, 1))  3.64 us
  transfers between devices with their start and end apart: 6, of which 3 were waited for; matrix products, arithmetic and copies ran while one was open for 2% of the time, Pallas kernels for 5%

profile of v3, /device:TPU:1, one launch (start us, length us, event | category | flops | bytes accessed | tf_op | source)
XLA Modules:
  0.0 75.3 jit_solution(3722948026489957171)
XLA Ops:
  0.6 0.0 copy-start.1
  0.6 0.6 copy-done.1
  1.3 1.5 %shard_map.68 = (f32[2,11,48,256]{3,2,1,0:T(8,128)S(1)}, f32[2,16,64,256]{3,2,1,0:T(8,128)S(1)}) custom-call(f32[2,16,64,256]{3,2,1,0:T(8,128)} %wave_ref.3, s32[1,64]{1,0:T(1,128)S(1)} %bitcast.6), custom_call_target="tpu_custom_call" | custom-call | flops 1048576 | bytes 1048576 | tf_op jit(solution)/shard_map/pallas_call | solution.py:263
  2.8 0.8 %shard_map.70 = (f32[504,256]{1,0:T(8,128)S(1)}, f32[1560,256]{1,0:T(8,128)S(1)}, f32[64,128]{1,0:T(8,128)S(1)}) custom-call(f32[2,16,64,256]{3,2,1,0:T(8,128)S(1)} %get-tuple-element.15.wave_ref, s32[1,64]{1,0:T(1,128)S(1)} %bitcast.7), custom_call_target="tpu_custom_call" | custom-call | flops 1048576 | bytes 1048576 | tf_op jit(solution)/shard_map/pallas_call | solution.py:276
  3.6 0.0 copy-start
  3.7 1.4 %collective-permute-start.2 = (f32[64,128]{1,0:T(8,128)S(1)}, f32[64,128]{1,0:T(8,128)S(1)}, u32[]{:S(2)}, u32[]{:S(2)}) collective-permute-start(f32[64,128]{1,0:T(8,128)S(1)} %get-tuple-element.19), channel_id=1, source_target_pairs={{32,0},{64,32},{96,64},{128,96},{160,128},{192,160},{224,192},{33,... | collective-permute-start | bytes 98312 | tf_op jit(solution)/shard_map/ppermute | solution.py:286
  5.1 6.3 %collective-permute-start.1 = (f32[64,128]{1,0:T(8,128)S(1)}, f32[64,128]{1,0:T(8,128)S(1)}, u32[]{:S(2)}, u32[]{:S(2)}) collective-permute-start(f32[64,128]{1,0:T(8,128)S(1)} %get-tuple-element.19), channel_id=1, source_target_pairs={{0,32},{32,64},{64,96},{96,128},{128,160},{160,192},{192,224},{1,3... | collective-permute-start | bytes 98312 | tf_op jit(solution)/shard_map/ppermute | solution.py:287
  11.4 0.0 collective-permute-done.2.after_ref
  11.4 1.0 %collective-permute-done.1.before_ref = f32[64,128]{1,0:T(8,128)S(1)} collective-permute-done((f32[64,128]{1,0:T(8,128)S(1)}, f32[64,128]{1,0:T(8,128)S(1)}, u32[]{:S(2)}, u32[]{:S(2)}) %collective-permute-start.1) | collective-permute-done | bytes 32800 | tf_op jit(solution)/shard_map/ppermute | solution.py:287
  12.4 0.0 copy-start.2
  12.4 3.6 %collective-permute-start.4 = (f32[1560,256]{1,0:T(8,128)S(1)}, f32[1560,256]{1,0:T(8,128)S(1)}, u32[]{:S(2)}, u32[]{:S(2)}) collective-permute-start(f32[1560,256]{1,0:T(8,128)S(1)} %get-tuple-element.23), channel_id=1, source_target_pairs={{0,1},{2,3},{4,5},{6,7},{8,9},{10,11},{12,13},{14,15},{16,17},{18,... | collective-permute-start | bytes 4792328 | tf_op jit(solution)/shard_map/ppermute | solution.py:310
  16.0 1.9 %collective-permute-start = (f32[2,11,48,256]{3,2,1,0:T(8,128)S(1)}, f32[2,11,48,256]{3,2,1,0:T(8,128)S(1)}, u32[]{:S(2)}, u32[]{:S(2)}) collective-permute-start(f32[2,11,48,256]{3,2,1,0:T(8,128)S(1)} %get-tuple-element.18), channel_id=1, source_target_pairs={{1,2},{3,4},{5,6},{7,8},{9,10},{11,12},{13,14},{15,16},{17,18},{19... | collective-permute-start | bytes 3244040 | tf_op jit(solution)/shard_map/ppermute | solution.py:273
  18.0 3.6 %collective-permute-start.3 = (f32[504,256]{1,0:T(8,128)S(1)}, f32[504,256]{1,0:T(8,128)S(1)}, u32[]{:S(2)}, u32[]{:S(2)}) collective-permute-start(f32[504,256]{1,0:T(8,128)S(1)} %get-tuple-element.22), channel_id=1, source_target_pairs={{1,2},{3,4},{5,6},{7,8},{9,10},{11,12},{13,14},{15,16},{17,18},{19... | collective-permute-start | bytes 1548296 | tf_op jit(solution)/shard_map/ppermute | solution.py:309
  22.3 0.0 copy-done
  22.3 3.6 %shard_map.69 = (bf16[16,128,384]{2,1,0:T(8,128)(2,1)S(1)}, bf16[16,128,384]{2,1,0:T(8,128)(2,1)S(1)}, f32[16,128]{1,0:T(8,128)S(1)}) custom-call(s32[1]{0:T(128)S(6)} %copy.13.shift_ref, f32[2,16,64,256]{3,2,1,0:T(8,128)S(1)} %get-tuple-element.15.wave_ref, f32[2,64,1024]{2,1,0:T(8,128)S(1)} %copy-done), custom_call_target="tpu_custom_call" | custom-call | flops 268435456 | bytes 1048576 | tf_op jit(solution)/shard_map/pallas_call | solution.py:290
  25.9 12.1 %collective-permute-done.3.link_ref = f32[504,256]{1,0:T(8,128)S(1)} collective-permute-done((f32[504,256]{1,0:T(8,128)S(1)}, f32[504,256]{1,0:T(8,128)S(1)}, u32[]{:S(2)}, u32[]{:S(2)}) %collective-permute-start.3) | collective-permute-done | bytes 516128 | tf_op jit(solution)/shard_map/ppermute | solution.py:309
  38.0 0.0 collective-permute-done.head_ref
  38.0 0.0 collective-permute-done.4.chip_ref
  38.0 0.0 copy-done.2
  38.0 6.1 %shard_map.72 = (f32[2,16,64,256]{3,2,1,0:T(8,128)S(1)}, f32[256,128]{1,0:T(8,128)}, f32[2,8,64,256]{3,2,1,0:T(8,128)S(1)}) custom-call(f32[5]{0:T(128)S(1)} %copy-done.2, f32[2,16,64,256]{3,2,1,0:T(8,128)S(1)} %get-tuple-element.15.wave_ref, s32[1,64]{1,0:T(1,128)S(1)} %bitcast.8, bf16[16,128,384]{2,1,0:T(8,128)(2,1)S(1)} %get-tuple-element.16.high_ref, ...), custom_call_target="tpu_custom_call" | custom-call | flops 268435456 | bytes 1048576 | tf_op jit(solution)/shard_map/pallas_call | solution.py:312
  44.2 15.5 %all-to-all-start = ((f32[256,1,128]{2,1,0:T(1,128)}), f32[256,1,128]{2,1,0:T(1,128)S(1)}, u32[]{:S(2)}, u32[]{:S(2)}) async-start(f32[256,1,128]{2,1,0:T(1,128)} %bitcast.2), calls=%async_computation | async-start | bytes 262144 | tf_op jit(solution)/shard_map/all_to_all | solution.py:323
  59.7 1.3 %copy.12 = f32[2,16,64,256]{3,2,1,0:T(8,128)} copy(f32[2,16,64,256]{3,2,1,0:T(8,128)S(1)} %get-tuple-element.28.mult_ref) | data formatting | bytes 4194304
  61.0 11.5 %all-to-all-done = f32[256,1,128]{2,1,0:T(1,128)S(1)} async-done(((f32[256,1,128]{2,1,0:T(1,128)}), f32[256,1,128]{2,1,0:T(1,128)S(1)}, u32[]{:S(2)}, u32[]{:S(2)}) %all-to-all-start) | async-done | bytes 131104 | tf_op jit(solution)/shard_map/all_to_all | solution.py:323
  72.6 2.7 %shard_map.73 = f32[2,16,64,256]{3,2,1,0:T(8,128)} custom-call(f32[256,128]{1,0:T(8,128)S(1)} %bitcast.5, f32[2,8,64,256]{3,2,1,0:T(8,128)S(1)} %get-tuple-element.27.kept_ref, f32[2,16,64,256]{3,2,1,0:T(8,128)} %wave_ref.3, f32[2,16,64,256]{3,2,1,0:T(8,128)S(1)} %get-tuple-element.28.mult_ref), custom_call_target="tpu_custom_call" | custom-call | flops 1048576 | bytes 1048576 | tf_op jit(solution)/shard_map/pallas_call | solution.py:325
  (1 shorter events, 0.0 us)
Async XLA Ops:
  0.6 0.7 copy-start.1
  3.6 18.6 %copy-start = (f32[2,64,1024]{2,1,0:T(8,128)S(1)}, f32[2,64,1024]{2,1,0:T(8,128)}, u32[]{:S(2)}) copy-start(f32[2,64,1024]{2,1,0:T(8,128)} %band_ref.1) | copy-start | bytes 1572868
  3.7 7.7 %collective-permute-start.2 = (f32[64,128]{1,0:T(8,128)S(1)}, f32[64,128]{1,0:T(8,128)S(1)}, u32[]{:S(2)}, u32[]{:S(2)}) collective-permute-start(f32[64,128]{1,0:T(8,128)S(1)} %get-tuple-element.19), channel_id=1, source_target_pairs={{32,0},{64,32},{96,64},{128,96},{160,128},{192,160},{224,192},{33,... | collective-permute-start | bytes 98312 | tf_op jit(solution)/shard_map/ppermute | solution.py:286
  5.1 7.3 %collective-permute-start.1 = (f32[64,128]{1,0:T(8,128)S(1)}, f32[64,128]{1,0:T(8,128)S(1)}, u32[]{:S(2)}, u32[]{:S(2)}) collective-permute-start(f32[64,128]{1,0:T(8,128)S(1)} %get-tuple-element.19), channel_id=1, source_target_pairs={{0,32},{32,64},{64,96},{96,128},{128,160},{160,192},{192,224},{1,3... | collective-permute-start | bytes 98312 | tf_op jit(solution)/shard_map/ppermute | solution.py:287
  12.4 25.7 %copy-start.2 = (f32[5]{0:T(128)S(1)}, f32[5]{0:T(128)}, u32[]{:S(2)}) copy-start(f32[5]{0:T(128)} %taper_ref.1) | copy-start | bytes 64
  12.4 25.6 %collective-permute-start.4 = (f32[1560,256]{1,0:T(8,128)S(1)}, f32[1560,256]{1,0:T(8,128)S(1)}, u32[]{:S(2)}, u32[]{:S(2)}) collective-permute-start(f32[1560,256]{1,0:T(8,128)S(1)} %get-tuple-element.23), channel_id=1, source_target_pairs={{0,1},{2,3},{4,5},{6,7},{8,9},{10,11},{12,13},{14,15},{16,17},{18,... | collective-permute-start | bytes 4792328 | tf_op jit(solution)/shard_map/ppermute | solution.py:310
  16.0 22.0 %collective-permute-start = (f32[2,11,48,256]{3,2,1,0:T(8,128)S(1)}, f32[2,11,48,256]{3,2,1,0:T(8,128)S(1)}, u32[]{:S(2)}, u32[]{:S(2)}) collective-permute-start(f32[2,11,48,256]{3,2,1,0:T(8,128)S(1)} %get-tuple-element.18), channel_id=1, source_target_pairs={{1,2},{3,4},{5,6},{7,8},{9,10},{11,12},{13,14},{15,16},{17,18},{19... | collective-permute-start | bytes 3244040 | tf_op jit(solution)/shard_map/ppermute | solution.py:273
  18.0 20.1 %collective-permute-start.3 = (f32[504,256]{1,0:T(8,128)S(1)}, f32[504,256]{1,0:T(8,128)S(1)}, u32[]{:S(2)}, u32[]{:S(2)}) collective-permute-start(f32[504,256]{1,0:T(8,128)S(1)} %get-tuple-element.22), channel_id=1, source_target_pairs={{1,2},{3,4},{5,6},{7,8},{9,10},{11,12},{13,14},{15,16},{17,18},{19... | collective-permute-start | bytes 1548296 | tf_op jit(solution)/shard_map/ppermute | solution.py:309
  44.2 28.4 %all-to-all-start = ((f32[256,1,128]{2,1,0:T(1,128)}), f32[256,1,128]{2,1,0:T(1,128)S(1)}, u32[]{:S(2)}, u32[]{:S(2)}) async-start(f32[256,1,128]{2,1,0:T(1,128)} %bitcast.2), calls=%async_computation | async-start | bytes 262144 | tf_op jit(solution)/shard_map/all_to_all | solution.py:323

commit v4 on v3

--- a/solution.py
+++ b/solution.py
@@ -20,7 +20,7 @@
 SRC_RCV = ("src_0", "src_1", "rcv_0", "rcv_1", "rcv_2")
 F32 = jnp.float32
 BF16 = jnp.bfloat16
-FIRST = 11
+FIRST = 14
 KEPT = 8
 
 
@@ -52,21 +52,23 @@
     return jnp.where(tail, column[SPARE:], column[:HALO])
 
 
-def head_kernel(wave_ref, mask_ref, out_ref, held_ref, sems):
+def head_kernel(wave_ref, mask_ref, out_ref, held_ref, live_ref, sems):
     tail = is_odd()
     start = pl.multiple_of(jnp.where(tail, SPARE, 0), 8)
     slices = wave_ref.shape[1]
-    copies = []
+    copies = [pltpu.make_async_copy(mask_ref, live_ref, sems.at[2])]
     for i, (low, high) in enumerate([(0, FIRST), (FIRST, slices)]):
         part = pl.ds(low, high - low)
         copies.append(pltpu.make_async_copy(wave_ref.at[:, part], held_ref.at[:, part], sems.at[i]))
-        copies[-1].start()
-    mask = at_end(mask_column(mask_ref), tail)
+    for copy in copies:
+        copy.start()
     copies[0].wait()
+    mask = at_end(mask_column(live_ref), tail)
+    copies[1].wait()
     for x in range(2):
         for f in range(FIRST):
             out_ref[x, f] = held_ref[x, f, pl.ds(start, HALO)] * mask
-    copies[1].wait()
+    copies[2].wait()
 
 
 def rest_kernel(wave_ref, mask_ref, link_ref, chip_ref, ends_ref):
@@ -103,79 +105,98 @@
         ref[ref.shape[0] - HALO // 2 :] = jnp.concatenate([rows[: HALO // 2], rows[HALO // 2 :]], axis=1)
 
 
-def band_kernel(shift_ref, wave_ref, band_ref, high_ref, low_ref, energy_ref):
-    shift = shift_ref[0]
-    odd = is_odd()
+def band_kernel(wave_ref, band_ref, high_ref, low_ref, energy_ref):
     low_half = iota((BLOCK, LANES), 1) < APER
-    left = iota((2 * BLOCK, LANES), 0) % BLOCK + shift < APER // 2
-    on_chip = left == odd
     for f in range(wave_ref.shape[1]):
         at = (f // 2) * LANES
-        near, far = (96, 32) if f % 2 == 0 else (32, 96)
-        rolled = []
+        skewed = []
         for x in range(2):
             taps = jnp.where(low_half == (f % 2 == 0), band_ref[x, :, at : at + LANES], 0.0)
-            skewed = pltpu.roll(taps, 0, 1, stride=1, stride_axis=0)
-            for base in (near, far):
-                rolled.append(pltpu.roll(skewed, shift + base, 1))
-        real, real_far, imag, imag_far = rolled
-        own = jnp.concatenate(
-            [jnp.where(low_half, real, -imag_far), jnp.where(low_half, imag, real_far)], axis=0
-        )
-        halo = jnp.concatenate(
-            [jnp.where(low_half, real_far, -imag), jnp.where(low_half, imag_far, real)], axis=0
-        )
-        halo = jnp.where(left, pltpu.roll(halo, LANES - SPARE, 1), halo)
-        parts = [own, jnp.where(on_chip, halo, 0.0), jnp.where(on_chip, 0.0, halo)]
-        for part, value in enumerate(parts):
-            high, low = split(value)
-            high_ref[f, :, part * LANES : (part + 1) * LANES] = high
-            low_ref[f, :, part * LANES : (part + 1) * LANES] = low
+            skewed.append(pltpu.roll(taps, APER * (f % 2), 1, stride=1, stride_axis=0))
+        real, imag = skewed
+        for row, parts in enumerate([(real, -imag), (imag, real)]):
+            for column, part in enumerate(parts):
+                place = (f, slice(row * BLOCK, (row + 1) * BLOCK), slice(column * LANES, (column + 1) * LANES))
+                high_ref[place], low_ref[place] = split(part)
         squares = wave_ref[0, f] * wave_ref[0, f] + wave_ref[1, f] * wave_ref[1, f]
         squares = jnp.sum(squares, axis=0, keepdims=True)
         energy_ref[f : f + 1, :] = squares[:, :LANES] + squares[:, LANES:]
 
 
+def framed(frame_ref, own, chip, link, start):
+    odd = is_odd()
+    left, right = 0, HALO + BLOCK
+    frame_ref[HALO : HALO + BLOCK] = own
+    frame_ref[pl.ds(pl.multiple_of(jnp.where(odd, left, right), 8), HALO)] = chip
+    frame_ref[pl.ds(pl.multiple_of(jnp.where(odd, right, left), 8), HALO)] = link
+    return frame_ref[pl.ds(start, LANES)]
+
+
+def window(frames_ref, wave_ref, mask, chip_ref, link, f, start):
+    rows = []
+    for x in range(2):
+        own = wave_ref[x, f] * mask
+        at = (2 * f + x) * HALO
+        chip = chip_ref[at : at + HALO]
+        other = link(x)
+        columns = []
+        for tile in range(own.shape[1] // LANES):
+            part = slice(tile * LANES, (tile + 1) * LANES)
+            columns.append(framed(frames_ref.at[x, tile], own[:, part], chip[:, part], other[:, part], start))
+        rows.append(jnp.concatenate(columns, axis=1))
+    return jnp.concatenate(rows, axis=0)
+
+
+def gather_kernel(shift_ref, wave_ref, mask_ref, high_ref, low_ref, head_ref, chip_ref, pred_ref, frames_ref):
+    start = SPARE + shift_ref[0]
+    mask = mask_column(mask_ref)
+    for f in range(FIRST):
+        data = window(frames_ref.at[f], wave_ref, mask, chip_ref, lambda x, f=f: head_ref[x, f], f, start)
+        pred_ref[f] = product((high_ref[f], low_ref[f]), split(data))
+
+
 def finish_kernel(
-    taper_ref, wave_ref, mask_ref, high_ref, low_ref, head_ref, link_ref, chip_ref, before_ref, after_ref, data_ref,
-    mult_ref, spread_ref, kept_ref,
+    shift_ref, taper_ref, wave_ref, mask_ref, high_ref, low_ref, pred_ref, link_ref, chip_ref, before_ref, after_ref,
+    data_ref, mult_ref, spread_ref, kept_ref, frames_ref, edges_ref,
 ):
+    start = SPARE + shift_ref[0]
     slices = wave_ref.shape[1]
     shots = wave_ref.shape[3]
     mask = mask_column(mask_ref)
     lane = iota((2 * BLOCK, LANES), 1)
     weights = [taper_ref[u] for u in range(2 * SHALF + 1)]
-    gap = jnp.zeros((SPARE, shots + LANES), F32)
 
     def unpacked(ref):
         rows = ref[ref.shape[0] - HALO // 2 :]
         return jnp.concatenate([rows[:, :LANES], rows[:, LANES:]], axis=0)
 
-    ends = merged_ends(before_ref, after_ref)
-    link_ends = unpacked(link_ref)
-    chip_ends = unpacked(chip_ref)
+    ends = framed(
+        frames_ref.at[slices - FIRST, 0, 0], merged_ends(before_ref, after_ref), unpacked(chip_ref), unpacked(link_ref),
+        start,
+    )
+    ends = split(ends)
+    rows = 2 * BLOCK * slices
+    for x in range(2):
+        part = slice(x * LANES, (x + 1) * LANES)
+        matrices = tuple(ref[:, :, part].reshape(rows, LANES) for ref in (high_ref, low_ref))
+        edges_ref[x] = product(matrices, ends).reshape(slices, 2 * BLOCK, LANES)
+
+    def linked(x, f):
+        at = (2 * (f - FIRST) + x) * HALO
+        return link_ref[at : at + HALO]
+
     row = iota((1, LANES), 1)
     energies = jnp.zeros((1, LANES), F32)
     for f in range(slices):
-        pieces = []
-        for source in range(3):
-            for x in range(2):
-                place = LANES - (4 * (x * slices + f) + SHALF)
-                at = (2 * f + x) * HALO
-                if source == 0:
-                    pieces.append(jnp.concatenate([wave_ref[x, f] * mask, pltpu.roll(ends, place, 1)], axis=1))
-                    continue
-                if source == 1:
-                    main, edge = chip_ref[at : at + HALO], chip_ends
-                elif f < FIRST:
-                    main, edge = head_ref[x, f], link_ends
-                else:
-                    at -= 2 * FIRST * HALO
-                    main, edge = link_ref[at : at + HALO], link_ends
-                pieces.append(jnp.concatenate([main, pltpu.roll(edge, place, 1)], axis=1))
-                pieces.append(gap)
-        whole = product((high_ref[f], low_ref[f]), split(jnp.concatenate(pieces, axis=0)))
-        pred, edge = whole[:, :shots], whole[:, shots:]
+        if f < FIRST:
+            pred = pred_ref[f]
+        else:
+            frames = frames_ref.at[f - FIRST]
+            data = window(frames, wave_ref, mask, chip_ref, lambda x, f=f: linked(x, f), f, start)
+            pred = product((high_ref[f], low_ref[f]), split(data))
+        edge = sum(
+            pltpu.roll(edges_ref[x, f], LANES - (4 * (x * slices + f) + SHALF), 1) for x in range(2)
+        )
         head, tail = pred[:, :LANES], pred[:, LANES:]
         total = weights[SHALF] * pred
         for u in range(1, SHALF + 1):
@@ -262,14 +283,14 @@
 
     head, wave = call(
         head_kernel,
-        [HBM, VMEM],
+        [HBM, HBM],
         [
             pltpu.VMEM((2, FIRST, HALO, shots), F32),
             pltpu.VMEM((2, slices, receivers, shots), F32),
         ],
         1 << 20,
-        scratch=[pltpu.SemaphoreType.DMA((2,))],
-    )(in_hbm, mask)
+        scratch=[pltpu.VMEM((1, receivers), jnp.int32), pltpu.SemaphoreType.DMA((3,))],
+    )(in_hbm, pltpu.with_memory_space_constraint(mask, pltpu.HBM))
     head = lax.ppermute(head, RCV, swaps(RCV, 1))
 
     wave, band = on_chip(wave, surface_band)
@@ -285,18 +306,6 @@
     )(wave, mask)
     after = lax.ppermute(ends, SRC, src_down)
     before = lax.ppermute(ends, SRC, src_up)
-
-    rows = 2 * receivers
-    high, low, data_energy = call(
-        band_kernel,
-        [SMEM, VMEM, VMEM],
-        [
-            pltpu.VMEM((slices, rows, 3 * LANES), BF16),
-            pltpu.VMEM((slices, rows, 3 * LANES), BF16),
-            pltpu.VMEM((slices, LANES), F32),
-        ],
-        1 << 28,
-    )(band_shift, wave, band)
 
     before, after, link, chip = on_chip(before, after, link, chip)
     link, chip = call(
@@ -309,16 +318,43 @@
     link = lax.ppermute(link, RCV, swaps(RCV, 1))
     chip = lax.ppermute(chip, RCV, swaps(RCV, 0))
 
+    rows = 2 * receivers
+    high, low, data_energy = call(
+        band_kernel,
+        [VMEM, VMEM],
+        [
+            pltpu.VMEM((slices, rows, 2 * LANES), BF16),
+            pltpu.VMEM((slices, rows, 2 * LANES), BF16),
+            pltpu.VMEM((slices, LANES), F32),
+        ],
+        1 << 28,
+    )(wave, band)
+    high, low, head, chip = on_chip(high, low, head, chip)
+    frame = (2, shots // LANES, 2 * HALO + BLOCK, LANES)
+    (predicted,) = call(
+        gather_kernel,
+        [SMEM] + [VMEM] * 6,
+        [pltpu.VMEM((FIRST, rows, shots), F32)],
+        1 << 28,
+        scratch=[pltpu.VMEM((FIRST,) + frame, F32)],
+    )(band_shift, wave, mask, high, low, head, chip)
     multiples, spread, kept = call(
         finish_kernel,
-        [SMEM] + [VMEM] * 10,
+        [SMEM, SMEM] + [VMEM] * 10,
         [
             pltpu.VMEM((2, slices, receivers, shots), F32),
             pltpu.VMEM((devices, LANES), F32),
             pltpu.VMEM((2, KEPT, receivers, shots), F32),
         ],
         1 << 28,
-    )(shot_taper, wave, mask, *on_chip(high, low, head, link, chip), before, after, *on_chip(data_energy))
+        scratch=[
+            pltpu.VMEM((slices - FIRST + 1,) + frame, F32),
+            pltpu.VMEM((2, slices, rows, LANES), F32),
+        ],
+    )(
+        band_shift, shot_taper, wave, mask, high, low, *on_chip(predicted, link), chip, before, after,
+        *on_chip(data_energy),
+    )
 
     energies = lax.all_to_all(spread[:, None], SRC_RCV, 0, 0, tiled=True).reshape(devices, LANES)
 

time: 75.6 us -> 74.9 us (level)
  Pallas kernels: 14.9 us -> 13.5 us
  waiting for transfers between devices: 24.7 us -> 26 us
    ppermute x1, waiting for transfers between devices: 0.01 us -> 12.9 us  [per_device(): head = lax.ppermute(head, RCV, swaps(RCV, 1))]
    ppermute x1, waiting for transfers between devices: 12.1 us -> 0.65 us  [per_device(): link = lax.ppermute(link, RCV, swaps(RCV, 1))]
    pallas_call x3 -> x4, Pallas kernels: 11.3 us -> 9.98 us  [the longest x1 6.1 us: per_device(): call(finish_kernel, [SMEM, SMEM] + [VMEM] * 10, [pltpu.VMEM((2, slices, r...]
  transfers between devices with their start and end apart: 6 -> 6, of which waited for: 3 -> 4; matrix products, arithmetic and copies ran while one was open for 2% -> 2% of each run, Pallas kernels for 5% -> 3%
where the time goes in v4:
time: 74.9 us; the launch traced here: 74.6 us
  starting transfers between devices  32.3 us (43%)
  waiting for transfers between devices  26 us (35%)
  Pallas kernels  13.5 us (18%)
  between operations  1.38 us (2%)
  local copies, waits for them, and re-layouts  1.34 us (2%)
    all_to_all x1, starting transfers between devices, per_device(): lax.all_to_all(spread[:, None], SRC_RCV, 0, 0, tiled=True)  15.6 us
    ppermute x1, waiting for transfers between devices, per_device(): head = lax.ppermute(head, RCV, swaps(RCV, 1))  12.9 us
    all_to_all x1, waiting for transfers between devices, per_device(): lax.all_to_all(spread[:, None], SRC_RCV, 0, 0, tiled=True)  11.5 us
    ppermute x1, starting transfers between devices, per_device(): before = lax.ppermute(ends, SRC, src_up)  6.27 us
    pallas_call x1, Pallas kernels, per_device(): call(finish_kernel, [SMEM, SMEM] + [VMEM] * 10, [pltpu.VMEM((2, slices, r...  6.1 us
    ppermute x1, starting transfers between devices, per_device(): chip = lax.ppermute(chip, RCV, swaps(RCV, 0))  3.65 us
    ppermute x1, starting transfers between devices, per_device(): link = lax.ppermute(link, RCV, swaps(RCV, 1))  3.64 us
    pallas_call x1, Pallas kernels, per_device(): call(subtract_kernel, [VMEM, VMEM, HBM, VMEM], [jax.ShapeDtypeStruct((2,...  2.73 us
  transfers between devices with their start and end apart: 6, of which 4 were waited for; matrix products, arithmetic and copies ran while one was open for 2% of the time, Pallas kernels for 3%

profile of v4, /device:TPU:1, one launch (start us, length us, event | category | flops | bytes accessed | tf_op | source)
XLA Modules:
  0.0 74.6 jit_solution(8843449762486118600)
XLA Ops:
  0.6 0.0 copy-start.1
  0.6 1.6 %shard_map.68 = (f32[2,14,48,256]{3,2,1,0:T(8,128)S(1)}, f32[2,16,64,256]{3,2,1,0:T(8,128)S(1)}) custom-call(f32[2,16,64,256]{3,2,1,0:T(8,128)} %wave_ref.3, s32[1,64]{1,0:T(1,128)} %bitcast.6), custom_call_target="tpu_custom_call" | custom-call | flops 1048576 | bytes 1048576 | tf_op jit(solution)/shard_map/pallas_call | solution.py:284
  2.3 0.0 copy-done.1
  2.3 0.0 copy-start
  2.3 0.8 %shard_map.70 = (f32[216,256]{1,0:T(8,128)S(1)}, f32[1560,256]{1,0:T(8,128)S(1)}, f32[64,128]{1,0:T(8,128)S(1)}) custom-call(f32[2,16,64,256]{3,2,1,0:T(8,128)S(1)} %get-tuple-element.15.wave_ref, s32[1,64]{1,0:T(1,128)S(1)} %bitcast.7), custom_call_target="tpu_custom_call" | custom-call | flops 1048576 | bytes 1048576 | tf_op jit(solution)/shard_map/pallas_call | solution.py:297
  3.1 1.3 %collective-permute-start.2 = (f32[64,128]{1,0:T(8,128)S(1)}, f32[64,128]{1,0:T(8,128)S(1)}, u32[]{:S(2)}, u32[]{:S(2)}) collective-permute-start(f32[64,128]{1,0:T(8,128)S(1)} %get-tuple-element.19), channel_id=1, source_target_pairs={{32,0},{64,32},{96,64},{128,96},{160,128},{192,160},{224,192},{33,... | collective-permute-start | bytes 98312 | tf_op jit(solution)/shard_map/ppermute | solution.py:307
  4.4 6.3 %collective-permute-start.1 = (f32[64,128]{1,0:T(8,128)S(1)}, f32[64,128]{1,0:T(8,128)S(1)}, u32[]{:S(2)}, u32[]{:S(2)}) collective-permute-start(f32[64,128]{1,0:T(8,128)S(1)} %get-tuple-element.19), channel_id=1, source_target_pairs={{0,32},{32,64},{64,96},{96,128},{128,160},{160,192},{192,224},{1,3... | collective-permute-start | bytes 98312 | tf_op jit(solution)/shard_map/ppermute | solution.py:308
  10.7 0.0 collective-permute-done.2.after_ref
  10.7 1.0 %collective-permute-done.1.before_ref = f32[64,128]{1,0:T(8,128)S(1)} collective-permute-done((f32[64,128]{1,0:T(8,128)S(1)}, f32[64,128]{1,0:T(8,128)S(1)}, u32[]{:S(2)}, u32[]{:S(2)}) %collective-permute-start.1) | collective-permute-done | bytes 32800 | tf_op jit(solution)/shard_map/ppermute | solution.py:308
  11.7 3.6 %collective-permute-start.3 = (f32[1560,256]{1,0:T(8,128)S(1)}, f32[1560,256]{1,0:T(8,128)S(1)}, u32[]{:S(2)}, u32[]{:S(2)}) collective-permute-start(f32[1560,256]{1,0:T(8,128)S(1)} %get-tuple-element.22), channel_id=1, source_target_pairs={{0,1},{2,3},{4,5},{6,7},{8,9},{10,11},{12,13},{14,15},{16,17},{18,... | collective-permute-start | bytes 4792328 | tf_op jit(solution)/shard_map/ppermute | solution.py:319
  15.4 1.9 %collective-permute-start = (f32[2,14,48,256]{3,2,1,0:T(8,128)S(1)}, f32[2,14,48,256]{3,2,1,0:T(8,128)S(1)}, u32[]{:S(2)}, u32[]{:S(2)}) collective-permute-start(f32[2,14,48,256]{3,2,1,0:T(8,128)S(1)} %get-tuple-element.18), channel_id=1, source_target_pairs={{1,2},{3,4},{5,6},{7,8},{9,10},{11,12},{13,14},{15,16},{17,18},{19... | collective-permute-start | bytes 4128776 | tf_op jit(solution)/shard_map/ppermute | solution.py:294
  17.3 3.6 %collective-permute-start.4 = (f32[216,256]{1,0:T(8,128)S(1)}, f32[216,256]{1,0:T(8,128)S(1)}, u32[]{:S(2)}, u32[]{:S(2)}) collective-permute-start(f32[216,256]{1,0:T(8,128)S(1)} %get-tuple-element.23), channel_id=1, source_target_pairs={{1,2},{3,4},{5,6},{7,8},{9,10},{11,12},{13,14},{15,16},{17,18},{19... | collective-permute-start | bytes 663560 | tf_op jit(solution)/shard_map/ppermute | solution.py:318
  21.6 0.0 copy-done
  21.6 0.5 shard_map.69
  22.1 12.9 %collective-permute-done.head_ref = f32[2,14,48,256]{3,2,1,0:T(8,128)S(1)} collective-permute-done((f32[2,14,48,256]{3,2,1,0:T(8,128)S(1)}, f32[2,14,48,256]{3,2,1,0:T(8,128)S(1)}, u32[]{:S(2)}, u32[]{:S(2)}) %collective-permute-start) | collective-permute-done | bytes 1376288 | tf_op jit(solution)/shard_map/ppermute | solution.py:294
  35.0 0.0 collective-permute-done.3.chip_ref
  35.0 0.0 copy-start.2
  35.0 1.7 %shard_map.72.pred_ref = f32[14,128,256]{2,1,0:T(8,128)S(1)} custom-call(s32[1]{0:T(128)S(6)} %copy.13.shift_ref, f32[2,16,64,256]{3,2,1,0:T(8,128)S(1)} %get-tuple-element.15.wave_ref, s32[1,64]{1,0:T(1,128)S(1)} %bitcast.8, bf16[16,128,256]{2,1,0:T(8,128)(2,1)S(1)} %get-tuple-element.16.high_ref, bf16[16,128,256]{2,1,0:T(8,128)(2,1)S(1)} %get-tuple-element.17.low_ref, ...), custom_call_target="tpu_custom_call" | custom-call | flops 268435456 | bytes 1048576 | tf_op jit(solution)/shard_map/pallas_call | solution.py:334
  36.7 0.6 collective-permute-done.4.link_ref
  37.3 0.0 copy-done.2
  37.3 6.1 %shard_map.73 = (f32[2,16,64,256]{3,2,1,0:T(8,128)S(1)}, f32[256,128]{1,0:T(8,128)}, f32[2,8,64,256]{3,2,1,0:T(8,128)S(1)}) custom-call(s32[1]{0:T(128)S(6)} %copy.13.shift_ref, f32[5]{0:T(128)S(1)} %copy-done.2, f32[2,16,64,256]{3,2,1,0:T(8,128)S(1)} %get-tuple-element.15.wave_ref, s32[1,64]{1,0:T(1,128)S(1)} %bitcast.9, ...), custom_call_target="tpu_custom_call" | custom-call | flops 268435456 | bytes 1048576 | tf_op jit(solution)/shard_map/pallas_call | solution.py:341
  43.4 15.6 %all-to-all-start = ((f32[256,1,128]{2,1,0:T(1,128)}), f32[256,1,128]{2,1,0:T(1,128)S(1)}, u32[]{:S(2)}, u32[]{:S(2)}) async-start(f32[256,1,128]{2,1,0:T(1,128)} %bitcast.2), calls=%async_computation | async-start | bytes 262144 | tf_op jit(solution)/shard_map/all_to_all | solution.py:359
  59.0 1.3 %copy.12 = f32[2,16,64,256]{3,2,1,0:T(8,128)} copy(f32[2,16,64,256]{3,2,1,0:T(8,128)S(1)} %get-tuple-element.28.mult_ref) | data formatting | bytes 4194304
  60.3 11.5 %all-to-all-done = f32[256,1,128]{2,1,0:T(1,128)S(1)} async-done(((f32[256,1,128]{2,1,0:T(1,128)}), f32[256,1,128]{2,1,0:T(1,128)S(1)}, u32[]{:S(2)}, u32[]{:S(2)}) %all-to-all-start) | async-done | bytes 131104 | tf_op jit(solution)/shard_map/all_to_all | solution.py:359
  71.9 2.7 %shard_map.74 = f32[2,16,64,256]{3,2,1,0:T(8,128)} custom-call(f32[256,128]{1,0:T(8,128)S(1)} %bitcast.5, f32[2,8,64,256]{3,2,1,0:T(8,128)S(1)} %get-tuple-element.27.kept_ref, f32[2,16,64,256]{3,2,1,0:T(8,128)} %wave_ref.3, f32[2,16,64,256]{3,2,1,0:T(8,128)S(1)} %get-tuple-element.28.mult_ref), custom_call_target="tpu_custom_call" | custom-call | flops 1048576 | bytes 1048576 | tf_op jit(solution)/shard_map/pallas_call | solution.py:361
  (1 shorter events, 0.0 us)
Async XLA Ops:
  0.6 1.7 %copy-start.1 = (s32[64]{0:T(128)S(1)}, s32[64]{0:T(128)}, u32[]{:S(2)}) copy-start(s32[64]{0:T(128)} %param.8) | copy-start | bytes 772
  2.3 19.3 %copy-start = (f32[2,64,1024]{2,1,0:T(8,128)S(1)}, f32[2,64,1024]{2,1,0:T(8,128)}, u32[]{:S(2)}) copy-start(f32[2,64,1024]{2,1,0:T(8,128)} %band_ref.1) | copy-start | bytes 1572868
  3.1 7.6 %collective-permute-start.2 = (f32[64,128]{1,0:T(8,128)S(1)}, f32[64,128]{1,0:T(8,128)S(1)}, u32[]{:S(2)}, u32[]{:S(2)}) collective-permute-start(f32[64,128]{1,0:T(8,128)S(1)} %get-tuple-element.19), channel_id=1, source_target_pairs={{32,0},{64,32},{96,64},{128,96},{160,128},{192,160},{224,192},{33,... | collective-permute-start | bytes 98312 | tf_op jit(solution)/shard_map/ppermute | solution.py:307
  4.4 7.3 %collective-permute-start.1 = (f32[64,128]{1,0:T(8,128)S(1)}, f32[64,128]{1,0:T(8,128)S(1)}, u32[]{:S(2)}, u32[]{:S(2)}) collective-permute-start(f32[64,128]{1,0:T(8,128)S(1)} %get-tuple-element.19), channel_id=1, source_target_pairs={{0,32},{32,64},{64,96},{96,128},{128,160},{160,192},{192,224},{1,3... | collective-permute-start | bytes 98312 | tf_op jit(solution)/shard_map/ppermute | solution.py:308
  11.7 23.3 %collective-permute-start.3 = (f32[1560,256]{1,0:T(8,128)S(1)}, f32[1560,256]{1,0:T(8,128)S(1)}, u32[]{:S(2)}, u32[]{:S(2)}) collective-permute-start(f32[1560,256]{1,0:T(8,128)S(1)} %get-tuple-element.22), channel_id=1, source_target_pairs={{0,1},{2,3},{4,5},{6,7},{8,9},{10,11},{12,13},{14,15},{16,17},{18,... | collective-permute-start | bytes 4792328 | tf_op jit(solution)/shard_map/ppermute | solution.py:319
  15.4 19.6 %collective-permute-start = (f32[2,14,48,256]{3,2,1,0:T(8,128)S(1)}, f32[2,14,48,256]{3,2,1,0:T(8,128)S(1)}, u32[]{:S(2)}, u32[]{:S(2)}) collective-permute-start(f32[2,14,48,256]{3,2,1,0:T(8,128)S(1)} %get-tuple-element.18), channel_id=1, source_target_pairs={{1,2},{3,4},{5,6},{7,8},{9,10},{11,12},{13,14},{15,16},{17,18},{19... | collective-permute-start | bytes 4128776 | tf_op jit(solution)/shard_map/ppermute | solution.py:294
  17.3 20.1 %collective-permute-start.4 = (f32[216,256]{1,0:T(8,128)S(1)}, f32[216,256]{1,0:T(8,128)S(1)}, u32[]{:S(2)}, u32[]{:S(2)}) collective-permute-start(f32[216,256]{1,0:T(8,128)S(1)} %get-tuple-element.23), channel_id=1, source_target_pairs={{1,2},{3,4},{5,6},{7,8},{9,10},{11,12},{13,14},{15,16},{17,18},{19... | collective-permute-start | bytes 663560 | tf_op jit(solution)/shard_map/ppermute | solution.py:318
  35.0 2.4 %copy-start.2 = (f32[5]{0:T(128)S(1)}, f32[5]{0:T(128)}, u32[]{:S(2)}) copy-start(f32[5]{0:T(128)} %taper_ref.1) | copy-start | bytes 64
  43.4 28.4 %all-to-all-start = ((f32[256,1,128]{2,1,0:T(1,128)}), f32[256,1,128]{2,1,0:T(1,128)S(1)}, u32[]{:S(2)}, u32[]{:S(2)}) async-start(f32[256,1,128]{2,1,0:T(1,128)} %bitcast.2), calls=%async_computation | async-start | bytes 262144 | tf_op jit(solution)/shard_map/all_to_all | solution.py:359

commit v5 on v4

--- a/solution.py
+++ b/solution.py
@@ -52,45 +52,45 @@
     return jnp.where(tail, column[SPARE:], column[:HALO])
 
 
-def head_kernel(wave_ref, mask_ref, out_ref, held_ref, live_ref, sems):
-    tail = is_odd()
-    start = pl.multiple_of(jnp.where(tail, SPARE, 0), 8)
+def head_kernel(wave_ref, mask_ref, held_ref, ends_ref, live_ref, sems):
     slices = wave_ref.shape[1]
+    group = slices // 2
     copies = [pltpu.make_async_copy(mask_ref, live_ref, sems.at[2])]
-    for i, (low, high) in enumerate([(0, FIRST), (FIRST, slices)]):
-        part = pl.ds(low, high - low)
+    for i in range(2):
+        part = pl.ds(i * group, group)
         copies.append(pltpu.make_async_copy(wave_ref.at[:, part], held_ref.at[:, part], sems.at[i]))
     for copy in copies:
         copy.start()
     copies[0].wait()
-    mask = at_end(mask_column(live_ref), tail)
-    copies[1].wait()
-    for x in range(2):
-        for f in range(FIRST):
-            out_ref[x, f] = held_ref[x, f, pl.ds(start, HALO)] * mask
-    copies[2].wait()
-
-
-def rest_kernel(wave_ref, mask_ref, link_ref, chip_ref, ends_ref):
+    mask = mask_column(live_ref)
+    lane = iota((BLOCK, LANES), 1)
+    ends = jnp.zeros((BLOCK, LANES), F32)
+    for f in range(slices):
+        if f % group == 0:
+            copies[1 + f // group].wait()
+        for x in range(2):
+            place = 4 * (x * slices + f)
+            last = pltpu.roll(held_ref[x, f, :, -LANES:], (place + SHALF) % LANES, 1)
+            first = pltpu.roll(held_ref[x, f, :, :LANES], place + SHALF, 1)
+            ends = jnp.where(lane // 2 == place // 2, last, ends)
+            ends = jnp.where(lane // 2 == place // 2 + 1, first, ends)
+    ends_ref[...] = ends * mask
+
+
+def rest_kernel(wave_ref, mask_ref, head_ref, link_ref, chip_ref):
     odd = is_odd()
     mask = mask_column(mask_ref)
-    lane = iota((BLOCK, LANES), 1)
     slices = wave_ref.shape[1]
-    ends = jnp.zeros((BLOCK, LANES), F32)
     for f in range(slices):
         for x in range(2):
             masked = wave_ref[x, f] * mask
-            place = 4 * (x * slices + f)
             row = (2 * f + x) * HALO
             chip_ref[row : row + HALO] = at_end(masked, jnp.logical_not(odd))
-            if f >= FIRST:
+            if f < FIRST:
+                head_ref[row : row + HALO] = at_end(masked, odd)
+            else:
                 row -= 2 * FIRST * HALO
                 link_ref[row : row + HALO] = at_end(masked, odd)
-            last = pltpu.roll(masked[:, -LANES:], (place + SHALF) % LANES, 1)
-            first = pltpu.roll(masked[:, :LANES], place + SHALF, 1)
-            ends = jnp.where(lane // 2 == place // 2, last, ends)
-            ends = jnp.where(lane // 2 == place // 2 + 1, first, ends)
-    ends_ref[...] = ends
 
 
 def merged_ends(before_ref, after_ref):
@@ -147,72 +147,107 @@
     return jnp.concatenate(rows, axis=0)
 
 
-def gather_kernel(shift_ref, wave_ref, mask_ref, high_ref, low_ref, head_ref, chip_ref, pred_ref, frames_ref):
+def gather_kernel(
+    shift_ref, taper_ref, wave_ref, mask_ref, high_ref, low_ref, head_ref, chip_ref, mult_ref, th_ref, tl_ref, frames_ref,
+    ph_ref, pl_ref,
+):
     start = SPARE + shift_ref[0]
     mask = mask_column(mask_ref)
+    shots = wave_ref.shape[3]
+    taper = split(weights_at(taper_ref, iota((shots, shots), 0) - iota((shots, shots), 1)))
+    th_ref[...], tl_ref[...] = taper
+    rows = 2 * BLOCK
     for f in range(FIRST):
-        data = window(frames_ref.at[f], wave_ref, mask, chip_ref, lambda x, f=f: head_ref[x, f], f, start)
-        pred_ref[f] = product((high_ref[f], low_ref[f]), split(data))
+        at = 2 * f * HALO
+        data = window(
+            frames_ref.at[f], wave_ref, mask, chip_ref, lambda x, at=at: head_ref[at + x * HALO : at + (x + 1) * HALO], f, start
+        )
+        part = slice(f * rows, (f + 1) * rows)
+        ph_ref[part], pl_ref[part] = split(product((high_ref[f], low_ref[f]), split(data)))
+    group = FIRST // 2
+    for i in range(2):
+        part = slice(i * group * rows, (i + 1) * group * rows)
+        whole = product((ph_ref[part], pl_ref[part]), taper)
+        mult_ref[i * group : (i + 1) * group] = whole.reshape(group, rows, shots)
+
+
+def weights_at(taper_ref, ahead):
+    weights = jnp.zeros(ahead.shape, F32)
+    for u in range(2 * SHALF + 1):
+        weights = jnp.where(ahead == u - SHALF, taper_ref[u], weights)
+    return weights
 
 
 def finish_kernel(
-    shift_ref, taper_ref, wave_ref, mask_ref, high_ref, low_ref, pred_ref, link_ref, chip_ref, before_ref, after_ref,
-    data_ref, mult_ref, spread_ref, kept_ref, frames_ref, edges_ref,
+    shift_ref, taper_ref, wave_ref, mask_ref, high_ref, low_ref, part_ref, th_ref, tl_ref, link_ref, chip_ref, before_ref,
+    after_ref, data_ref, out_ref, mult_ref, spread_ref, kept_ref, frames_ref, pred_ref, sems,
 ):
     start = SPARE + shift_ref[0]
     slices = wave_ref.shape[1]
     shots = wave_ref.shape[3]
+    rows = 2 * BLOCK
     mask = mask_column(mask_ref)
-    lane = iota((2 * BLOCK, LANES), 1)
-    weights = [taper_ref[u] for u in range(2 * SHALF + 1)]
+
+    def linked(x, f):
+        at = (2 * (f - FIRST) + x) * HALO
+        return link_ref[at : at + HALO]
 
     def unpacked(ref):
-        rows = ref[ref.shape[0] - HALO // 2 :]
-        return jnp.concatenate([rows[:, :LANES], rows[:, LANES:]], axis=0)
+        cells = ref[ref.shape[0] - HALO // 2 :]
+        return jnp.concatenate([cells[:, :LANES], cells[:, LANES:]], axis=0)
 
     ends = framed(
         frames_ref.at[slices - FIRST, 0, 0], merged_ends(before_ref, after_ref), unpacked(chip_ref), unpacked(link_ref),
         start,
     )
     ends = split(ends)
-    rows = 2 * BLOCK * slices
-    for x in range(2):
-        part = slice(x * LANES, (x + 1) * LANES)
-        matrices = tuple(ref[:, :, part].reshape(rows, LANES) for ref in (high_ref, low_ref))
-        edges_ref[x] = product(matrices, ends).reshape(slices, 2 * BLOCK, LANES)
-
-    def linked(x, f):
-        at = (2 * (f - FIRST) + x) * HALO
-        return link_ref[at : at + HALO]
-
-    row = iota((1, LANES), 1)
-    energies = jnp.zeros((1, LANES), F32)
+    kind = iota((LANES, LANES), 0) % 4
+    source = jnp.where(kind < SHALF, kind - SHALF, kind - SHALF + shots)
+    target = iota((LANES, LANES), 1)
+    target = jnp.where(target < LANES // 2, target, target + shots - LANES)
+    reach = split(weights_at(taper_ref, source - target))
+    for f in range(FIRST, slices):
+        data = window(frames_ref.at[f - FIRST], wave_ref, mask, chip_ref, lambda x, f=f: linked(x, f), f, start)
+        pred = split(product((high_ref[f], low_ref[f]), split(data)))
+        pred_ref[f - FIRST] = product(pred, (th_ref[...], tl_ref[...]))
+    near = iota((rows, LANES), 1) < LANES // 2
+    squares = []
+    writes = []
+    group = 4
+    for first in range(0, slices, group):
+        shape = (group, rows, LANES)
+        owner = iota(shape, 2) // 4 - iota(shape, 0) - first
+        edge = jnp.zeros(shape, F32)
+        for x in range(2):
+            part = slice(x * LANES, (x + 1) * LANES)
+            matrices = tuple(ref[first : first + group, :, part].reshape(group * rows, LANES) for ref in (high_ref, low_ref))
+            edge = jnp.where(owner == x * slices, product(matrices, ends).reshape(shape), edge)
+        edge = product(split(edge.reshape(group * rows, LANES)), reach)
+        for f in range(first, first + group):
+            own = part_ref[f] if f < FIRST else pred_ref[f - FIRST]
+            extra = edge[(f - first) * rows : (f - first + 1) * rows]
+            total = jnp.concatenate(
+                [own[:, :LANES] + jnp.where(near, extra, 0.0), own[:, LANES:] + jnp.where(near, 0.0, extra)], axis=1
+            )
+            mult_ref[0, f] = total[:BLOCK]
+            mult_ref[1, f] = total[BLOCK:]
+            total = jnp.sum(total * total, axis=0, keepdims=True)
+            squares.append(total[:, :LANES] + total[:, LANES:])
+        part = pl.ds(first, group)
+        writes.append(pltpu.make_async_copy(mult_ref.at[:, part], out_ref.at[:, part], sems.at[first // group]))
+        writes[-1].start()
+    lane = iota((slices, LANES), 1) - iota((slices, LANES), 0)
+    row = iota((slices, LANES), 0)
+    pred_rows = jnp.zeros((slices, LANES), F32)
     for f in range(slices):
-        if f < FIRST:
-            pred = pred_ref[f]
-        else:
-            frames = frames_ref.at[f - FIRST]
-            data = window(frames, wave_ref, mask, chip_ref, lambda x, f=f: linked(x, f), f, start)
-            pred = product((high_ref[f], low_ref[f]), split(data))
-        edge = sum(
-            pltpu.roll(edges_ref[x, f], LANES - (4 * (x * slices + f) + SHALF), 1) for x in range(2)
-        )
-        head, tail = pred[:, :LANES], pred[:, LANES:]
-        total = weights[SHALF] * pred
-        for u in range(1, SHALF + 1):
-            earlier = jnp.concatenate([head, jnp.where(lane >= LANES - u, edge, tail)], axis=1)
-            later = jnp.concatenate([jnp.where(lane < u, edge, head), tail], axis=1)
-            total = total + weights[SHALF - u] * pltpu.roll(earlier, u, 1)
-            total = total + weights[SHALF + u] * pltpu.roll(later, shots - u, 1)
-        mult_ref[0, f] = total[:BLOCK]
-        mult_ref[1, f] = total[BLOCK:]
-        squares = jnp.sum(total * total, axis=0, keepdims=True)
-        pred_energy = jnp.sum(squares[:, :LANES] + squares[:, LANES:], axis=1, keepdims=True)
-        data_energy = jnp.sum(data_ref[f : f + 1, :], axis=1, keepdims=True)
-        energies = jnp.where(row == f, data_energy, energies)
-        energies = jnp.where(row == slices + f, pred_energy, energies)
-    spread_ref[...] = jnp.broadcast_to(energies, spread_ref.shape)
+        pred_rows = jnp.where(row == f, squares[f], pred_rows)
+    pred_energy = jnp.sum(pred_rows, axis=1, keepdims=True)
+    data_energy = jnp.sum(data_ref[...], axis=1, keepdims=True)
+    energies = jnp.where(lane == 0, data_energy, jnp.where(lane == slices, pred_energy, 0.0))
+    spread_ref[...] = jnp.broadcast_to(jnp.sum(energies, axis=0, keepdims=True), spread_ref.shape)
     kept_ref[...] = wave_ref[:, :KEPT]
+    for copy in writes:
+        copy.wait()
 
 
 def subtract_kernel(total_ref, kept_ref, wave_ref, mult_ref, out_ref, held_ref, in_sems, out_sems):
@@ -281,31 +316,28 @@
     devices = lax.axis_size(SRC_RCV)
     in_hbm = pltpu.with_memory_space_constraint(wavefield, pltpu.HBM)
 
-    head, wave = call(
+    wave, ends = call(
         head_kernel,
         [HBM, HBM],
-        [
-            pltpu.VMEM((2, FIRST, HALO, shots), F32),
-            pltpu.VMEM((2, slices, receivers, shots), F32),
-        ],
+        [pltpu.VMEM((2, slices, receivers, shots), F32), pltpu.VMEM((BLOCK, LANES), F32)],
         1 << 20,
         scratch=[pltpu.VMEM((1, receivers), jnp.int32), pltpu.SemaphoreType.DMA((3,))],
     )(in_hbm, pltpu.with_memory_space_constraint(mask, pltpu.HBM))
-    head = lax.ppermute(head, RCV, swaps(RCV, 1))
+    after = lax.ppermute(ends, SRC, src_down)
+    before = lax.ppermute(ends, SRC, src_up)
 
     wave, band = on_chip(wave, surface_band)
-    link, chip, ends = call(
+    head, link, chip = call(
         rest_kernel,
         [VMEM, VMEM],
         [
+            pltpu.VMEM((2 * FIRST * HALO, shots), F32),
             pltpu.VMEM((2 * (slices - FIRST) * HALO + HALO // 2, shots), F32),
             pltpu.VMEM((2 * slices * HALO + HALO // 2, shots), F32),
-            pltpu.VMEM((BLOCK, LANES), F32),
         ],
         1 << 20,
     )(wave, mask)
-    after = lax.ppermute(ends, SRC, src_down)
-    before = lax.ppermute(ends, SRC, src_up)
+    head = lax.ppermute(head, RCV, swaps(RCV, 1))
 
     before, after, link, chip = on_chip(before, after, link, chip)
     link, chip = call(
@@ -331,29 +363,36 @@
     )(wave, band)
     high, low, head, chip = on_chip(high, low, head, chip)
     frame = (2, shots // LANES, 2 * HALO + BLOCK, LANES)
-    (predicted,) = call(
+    partial, taper_high, taper_low = call(
         gather_kernel,
-        [SMEM] + [VMEM] * 6,
-        [pltpu.VMEM((FIRST, rows, shots), F32)],
+        [SMEM, SMEM] + [VMEM] * 6,
+        [
+            pltpu.VMEM((FIRST, rows, shots), F32),
+            pltpu.VMEM((shots, shots), BF16),
+            pltpu.VMEM((shots, shots), BF16),
+        ],
         1 << 28,
-        scratch=[pltpu.VMEM((FIRST,) + frame, F32)],
-    )(band_shift, wave, mask, high, low, head, chip)
-    multiples, spread, kept = call(
+        scratch=[pltpu.VMEM((FIRST,) + frame, F32)] + [pltpu.VMEM((FIRST * rows, shots), BF16)] * 2,
+    )(band_shift, shot_taper, wave, mask, high, low, head, chip)
+    multiples, scaled, spread, kept = call(
         finish_kernel,
-        [SMEM, SMEM] + [VMEM] * 10,
+        [SMEM, SMEM] + [VMEM] * 12,
         [
+            jax.ShapeDtypeStruct((2, slices, receivers, shots), F32),
             pltpu.VMEM((2, slices, receivers, shots), F32),
             pltpu.VMEM((devices, LANES), F32),
             pltpu.VMEM((2, KEPT, receivers, shots), F32),
         ],
         1 << 28,
+        out_specs=[HBM, VMEM, VMEM, VMEM],
         scratch=[
             pltpu.VMEM((slices - FIRST + 1,) + frame, F32),
-            pltpu.VMEM((2, slices, rows, LANES), F32),
+            pltpu.VMEM((slices - FIRST, rows, shots), F32),
+            pltpu.SemaphoreType.DMA((slices // 4,)),
         ],
     )(
-        band_shift, shot_taper, wave, mask, high, low, *on_chip(predicted, link), chip, before, after,
-        *on_chip(data_energy),
+        band_shift, shot_taper, wave, mask, high, low, *on_chip(partial, taper_high, taper_low, link), chip, before,
+        after, *on_chip(data_energy),
     )
 
     energies = lax.all_to_all(spread[:, None], SRC_RCV, 0, 0, tiled=True).reshape(devices, LANES)
@@ -365,7 +404,7 @@
         1 << 20,
         out_specs=[HBM],
         scratch=[pltpu.VMEM((2, slices, receivers, shots), F32)] + [pltpu.SemaphoreType.DMA((slices,))] * 2,
-    )(*on_chip(energies, kept), in_hbm, *on_chip(multiples))
+    )(*on_chip(energies, kept), in_hbm, *on_chip(scaled))
     return (multiples, primaries)
 
 

time: 74.9 us -> 72.9 us (0.973)
  blocking collectives: 0 us -> 28.4 us
  starting transfers between devices: 32.3 us -> 16.8 us
  waiting for transfers between devices: 26 us -> 13.5 us
  local copies, waits for them, and re-layouts: 1.34 us -> 0.01 us
  Pallas kernels: 13.5 us -> 12.6 us
    all_to_all x0 -> x1, blocking collectives: none -> 28.4 us  [per_device(): lax.all_to_all(spread[:, None], SRC_RCV, 0, 0, tiled=True)]
    all_to_all x1 -> x0, starting transfers between devices: 15.6 us -> none  [per_device(): lax.all_to_all(spread[:, None], SRC_RCV, 0, 0, tiled=True)]
    all_to_all x1 -> x0, waiting for transfers between devices: 11.5 us -> none  [per_device(): lax.all_to_all(spread[:, None], SRC_RCV, 0, 0, tiled=True)]
    unnamed x7 -> x6, local copies, waits for them, and re-layouts: 1.34 us -> 0.01 us
    pallas_call x4, Pallas kernels: 10.3 us -> 9.29 us  [the longest x1 4.04 us: per_device(): call(finish_kernel, [SMEM, SMEM] + [VMEM] * 12, [jax.ShapeDtypeStruct((2,...]
  transfers between devices with their start and end apart: 6 -> 5, of which waited for: 4 -> 2; matrix products, arithmetic and copies ran while one was open for 2% -> 0% of each run, Pallas kernels for 3% -> 5%
where the time goes in v5:
time: 72.9 us; the launch traced here: 72.6 us
  blocking collectives  28.4 us (39%)
  starting transfers between devices  16.8 us (23%)
  waiting for transfers between devices  13.5 us (19%)
  Pallas kernels  12.6 us (17%)
  between operations  1.39 us (2%)
    all_to_all x1, blocking collectives, per_device(): lax.all_to_all(spread[:, None], SRC_RCV, 0, 0, tiled=True)  28.4 us
    ppermute x1, waiting for transfers between devices, per_device(): head = lax.ppermute(head, RCV, swaps(RCV, 1))  12.9 us
    ppermute x1, starting transfers between devices, per_device(): before = lax.ppermute(ends, SRC, src_up)  6.27 us
    pallas_call x1, Pallas kernels, per_device(): call(finish_kernel, [SMEM, SMEM] + [VMEM] * 12, [jax.ShapeDtypeStruct((2,...  4.04 us
    ppermute x1, starting transfers between devices, per_device(): chip = lax.ppermute(chip, RCV, swaps(RCV, 0))  3.65 us
    ppermute x1, starting transfers between devices, per_device(): link = lax.ppermute(link, RCV, swaps(RCV, 1))  3.64 us
    pallas_call x1, Pallas kernels, per_device(): call(gather_kernel, [SMEM, SMEM] + [VMEM] * 6, [pltpu.VMEM((FIRST, rows,...  3 us
    pallas_call x1, Pallas kernels, per_device(): call(subtract_kernel, [VMEM, VMEM, HBM, VMEM], [jax.ShapeDtypeStruct((2,...  2.73 us
  transfers between devices with their start and end apart: 5, of which 2 were waited for; matrix products, arithmetic and copies ran while one was open for 0% of the time, Pallas kernels for 5%

profile of v5, /device:TPU:1, one launch (start us, length us, event | category | flops | bytes accessed | tf_op | source)
XLA Modules:
  0.0 72.6 jit_solution(12445230168117075090)
XLA Ops:
  0.6 0.0 copy-start.1
  0.6 1.9 %shard_map.68 = (f32[2,16,64,256]{3,2,1,0:T(8,128)S(1)}, f32[64,128]{1,0:T(8,128)S(1)}) custom-call(f32[2,16,64,256]{3,2,1,0:T(8,128)} %wave_ref.3, s32[1,64]{1,0:T(1,128)} %bitcast.7), custom_call_target="tpu_custom_call" | custom-call | flops 1048576 | bytes 1048576 | tf_op jit(solution)/shard_map/pallas_call | solution.py:319
  2.6 1.3 %collective-permute-start.2 = (f32[64,128]{1,0:T(8,128)S(1)}, f32[64,128]{1,0:T(8,128)S(1)}, u32[]{:S(2)}, u32[]{:S(2)}) collective-permute-start(f32[64,128]{1,0:T(8,128)S(1)} %get-tuple-element.23), channel_id=1, source_target_pairs={{32,0},{64,32},{96,64},{128,96},{160,128},{192,160},{224,192},{33,... | collective-permute-start | bytes 98312 | tf_op jit(solution)/shard_map/ppermute | solution.py:326
  3.9 6.3 %collective-permute-start.1 = (f32[64,128]{1,0:T(8,128)S(1)}, f32[64,128]{1,0:T(8,128)S(1)}, u32[]{:S(2)}, u32[]{:S(2)}) collective-permute-start(f32[64,128]{1,0:T(8,128)S(1)} %get-tuple-element.23), channel_id=1, source_target_pairs={{0,32},{32,64},{64,96},{96,128},{128,160},{160,192},{192,224},{1,3... | collective-permute-start | bytes 98312 | tf_op jit(solution)/shard_map/ppermute | solution.py:327
  10.2 0.0 copy-done.1
  10.2 0.0 copy-start
  10.2 0.3 shard_map.70
  10.5 0.0 collective-permute-done.2.after_ref
  10.5 0.7 collective-permute-done.1.before_ref
  11.2 0.0 copy-start.2
  11.2 3.6 %collective-permute-start.3 = (f32[1560,256]{1,0:T(8,128)S(1)}, f32[1560,256]{1,0:T(8,128)S(1)}, u32[]{:S(2)}, u32[]{:S(2)}) collective-permute-start(f32[1560,256]{1,0:T(8,128)S(1)} %get-tuple-element.26), channel_id=1, source_target_pairs={{0,1},{2,3},{4,5},{6,7},{8,9},{10,11},{12,13},{14,15},{16,17},{18,... | collective-permute-start | bytes 4792328 | tf_op jit(solution)/shard_map/ppermute | solution.py:351
  14.8 1.9 %collective-permute-start = (f32[1344,256]{1,0:T(8,128)S(1)}, f32[1344,256]{1,0:T(8,128)S(1)}, u32[]{:S(2)}, u32[]{:S(2)}) collective-permute-start(f32[1344,256]{1,0:T(8,128)S(1)} %get-tuple-element.22), channel_id=1, source_target_pairs={{1,2},{3,4},{5,6},{7,8},{9,10},{11,12},{13,14},{15,16},{17,18},{19... | collective-permute-start | bytes 4128776 | tf_op jit(solution)/shard_map/ppermute | solution.py:340
  16.8 3.6 %collective-permute-start.4 = (f32[216,256]{1,0:T(8,128)S(1)}, f32[216,256]{1,0:T(8,128)S(1)}, u32[]{:S(2)}, u32[]{:S(2)}) collective-permute-start(f32[216,256]{1,0:T(8,128)S(1)} %get-tuple-element.30), channel_id=1, source_target_pairs={{1,2},{3,4},{5,6},{7,8},{9,10},{11,12},{13,14},{15,16},{17,18},{19... | collective-permute-start | bytes 663560 | tf_op jit(solution)/shard_map/ppermute | solution.py:350
  21.1 0.0 copy-done
  21.1 0.5 shard_map.69
  21.6 12.9 %collective-permute-done.head_ref = f32[1344,256]{1,0:T(8,128)S(1)} collective-permute-done((f32[1344,256]{1,0:T(8,128)S(1)}, f32[1344,256]{1,0:T(8,128)S(1)}, u32[]{:S(2)}, u32[]{:S(2)}) %collective-permute-start) | collective-permute-done | bytes 1376288 | tf_op jit(solution)/shard_map/ppermute | solution.py:340
  34.5 0.0 collective-permute-done.3.chip_ref
  34.5 0.0 copy-done.2
  34.5 3.0 %shard_map.72 = (f32[14,128,256]{2,1,0:T(8,128)S(1)}, bf16[256,256]{1,0:T(8,128)(2,1)S(1)}, bf16[256,256]{1,0:T(8,128)(2,1)S(1)}) custom-call(s32[1]{0:T(128)S(6)} %copy.12.shift_ref, f32[5]{0:T(128)S(1)} %copy-done.2, f32[2,16,64,256]{3,2,1,0:T(8,128)S(1)} %get-tuple-element.19.wave_ref, s32[1,64]{1,0:T(1,128)S(1)} %bitcast.9, ...), custom_call_target="tpu_custom_call" | custom-call | flops 268435456 | bytes 1048576 | tf_op jit(solution)/shard_map/pallas_call | solution.py:366
  37.5 0.0 collective-permute-done.4.link_ref
  37.5 4.0 %shard_map.73 = (f32[2,16,64,256]{3,2,1,0:T(8,128)}, f32[2,16,64,256]{3,2,1,0:T(8,128)S(1)}, f32[256,128]{1,0:T(8,128)S(1)}, f32[2,8,64,256]{3,2,1,0:T(8,128)S(1)}) custom-call(s32[1]{0:T(128)S(6)} %copy.12.shift_ref, f32[5]{0:T(128)S(1)} %copy-done.2, f32[2,16,64,256]{3,2,1,0:T(8,128)S(1)} %get-tuple-element.19.wave_ref, s32[1,64]{1,0:T(1,128)S(1)} %bitcast.10, ...), custom_call_target="tpu_custom_call" | custom-call | flops 268435456 | bytes 1048576 | tf_op jit(solution)/shard_map/pallas_call | solution.py:377
  41.5 28.4 %all_to_all.5 = f32[256,1,128]{2,1,0:T(1,128)S(1)} all-to-all(f32[256,1,128]{2,1,0:T(1,128)S(1)} %bitcast.6), channel_id=1, replica_groups=mesh['src_0'=4,'src_1'=2,'rcv_0'=2,'rcv_1'=8,'rcv_2'=2] {'src_0','src_1'..., dimensions={0} | all-to-all | bytes 262144 | tf_op jit(solution)/shard_map/all_to_all | solution.py:398
  69.9 2.7 %shard_map.74 = f32[2,16,64,256]{3,2,1,0:T(8,128)} custom-call(f32[256,128]{1,0:T(8,128)S(1)} %bitcast.5, f32[2,8,64,256]{3,2,1,0:T(8,128)S(1)} %get-tuple-element.34.kept_ref, f32[2,16,64,256]{3,2,1,0:T(8,128)} %wave_ref.3, f32[2,16,64,256]{3,2,1,0:T(8,128)S(1)} %get-tuple-element.35.mult_ref), custom_call_target="tpu_custom_call" | custom-call | flops 1048576 | bytes 1048576 | tf_op jit(solution)/shard_map/pallas_call | solution.py:400
  (1 shorter events, 0.0 us)
Async XLA Ops:
  0.6 9.5 %copy-start.1 = (s32[64]{0:T(128)S(1)}, s32[64]{0:T(128)}, u32[]{:S(2)}) copy-start(s32[64]{0:T(128)} %param.8) | copy-start | bytes 772
  2.6 7.9 %collective-permute-start.2 = (f32[64,128]{1,0:T(8,128)S(1)}, f32[64,128]{1,0:T(8,128)S(1)}, u32[]{:S(2)}, u32[]{:S(2)}) collective-permute-start(f32[64,128]{1,0:T(8,128)S(1)} %get-tuple-element.23), channel_id=1, source_target_pairs={{32,0},{64,32},{96,64},{128,96},{160,128},{192,160},{224,192},{33,... | collective-permute-start | bytes 98312 | tf_op jit(solution)/shard_map/ppermute | solution.py:326
  3.9 7.3 %collective-permute-start.1 = (f32[64,128]{1,0:T(8,128)S(1)}, f32[64,128]{1,0:T(8,128)S(1)}, u32[]{:S(2)}, u32[]{:S(2)}) collective-permute-start(f32[64,128]{1,0:T(8,128)S(1)} %get-tuple-element.23), channel_id=1, source_target_pairs={{0,32},{32,64},{64,96},{96,128},{128,160},{160,192},{192,224},{1,3... | collective-permute-start | bytes 98312 | tf_op jit(solution)/shard_map/ppermute | solution.py:327
  10.2 10.9 %copy-start = (f32[2,64,1024]{2,1,0:T(8,128)S(1)}, f32[2,64,1024]{2,1,0:T(8,128)}, u32[]{:S(2)}) copy-start(f32[2,64,1024]{2,1,0:T(8,128)} %band_ref.1) | copy-start | bytes 1572868
  11.2 23.3 %copy-start.2 = (f32[5]{0:T(128)S(1)}, f32[5]{0:T(128)}, u32[]{:S(2)}) copy-start(f32[5]{0:T(128)} %taper_ref.3) | copy-start | bytes 64
  11.2 23.3 %collective-permute-start.3 = (f32[1560,256]{1,0:T(8,128)S(1)}, f32[1560,256]{1,0:T(8,128)S(1)}, u32[]{:S(2)}, u32[]{:S(2)}) collective-permute-start(f32[1560,256]{1,0:T(8,128)S(1)} %get-tuple-element.26), channel_id=1, source_target_pairs={{0,1},{2,3},{4,5},{6,7},{8,9},{10,11},{12,13},{14,15},{16,17},{18,... | collective-permute-start | bytes 4792328 | tf_op jit(solution)/shard_map/ppermute | solution.py:351
  14.8 19.6 %collective-permute-start = (f32[1344,256]{1,0:T(8,128)S(1)}, f32[1344,256]{1,0:T(8,128)S(1)}, u32[]{:S(2)}, u32[]{:S(2)}) collective-permute-start(f32[1344,256]{1,0:T(8,128)S(1)} %get-tuple-element.22), channel_id=1, source_target_pairs={{1,2},{3,4},{5,6},{7,8},{9,10},{11,12},{13,14},{15,16},{17,18},{19... | collective-permute-start | bytes 4128776 | tf_op jit(solution)/shard_map/ppermute | solution.py:340
  16.8 20.7 %collective-permute-start.4 = (f32[216,256]{1,0:T(8,128)S(1)}, f32[216,256]{1,0:T(8,128)S(1)}, u32[]{:S(2)}, u32[]{:S(2)}) collective-permute-start(f32[216,256]{1,0:T(8,128)S(1)} %get-tuple-element.30), channel_id=1, source_target_pairs={{1,2},{3,4},{5,6},{7,8},{9,10},{11,12},{13,14},{15,16},{17,18},{19... | collective-permute-start | bytes 663560 | tf_op jit(solution)/shard_map/ppermute | solution.py:350

commit v6 on v5

--- a/solution.py
+++ b/solution.py
@@ -20,7 +20,8 @@
 SRC_RCV = ("src_0", "src_1", "rcv_0", "rcv_1", "rcv_2")
 F32 = jnp.float32
 BF16 = jnp.bfloat16
-FIRST = 14
+EARLY = 9
+FIRST = 13
 KEPT = 8
 
 
@@ -52,60 +53,66 @@
     return jnp.where(tail, column[SPARE:], column[:HALO])
 
 
-def head_kernel(wave_ref, mask_ref, held_ref, ends_ref, live_ref, sems):
+def head_kernel(wave_ref, mask_ref, held_ref, early_ref, live_ref, sems):
+    tail = is_odd()
     slices = wave_ref.shape[1]
-    group = slices // 2
     copies = [pltpu.make_async_copy(mask_ref, live_ref, sems.at[2])]
-    for i in range(2):
-        part = pl.ds(i * group, group)
+    for i, (low, high) in enumerate([(0, EARLY), (EARLY, slices)]):
+        part = pl.ds(low, high - low)
         copies.append(pltpu.make_async_copy(wave_ref.at[:, part], held_ref.at[:, part], sems.at[i]))
     for copy in copies:
         copy.start()
     copies[0].wait()
-    mask = mask_column(live_ref)
-    lane = iota((BLOCK, LANES), 1)
-    ends = jnp.zeros((BLOCK, LANES), F32)
-    for f in range(slices):
-        if f % group == 0:
-            copies[1 + f // group].wait()
-        for x in range(2):
-            place = 4 * (x * slices + f)
-            last = pltpu.roll(held_ref[x, f, :, -LANES:], (place + SHALF) % LANES, 1)
-            first = pltpu.roll(held_ref[x, f, :, :LANES], place + SHALF, 1)
-            ends = jnp.where(lane // 2 == place // 2, last, ends)
-            ends = jnp.where(lane // 2 == place // 2 + 1, first, ends)
-    ends_ref[...] = ends * mask
-
-
-def rest_kernel(wave_ref, mask_ref, head_ref, link_ref, chip_ref):
+    mask = at_end(mask_column(live_ref), tail)
+    start = pl.multiple_of(jnp.where(tail, SPARE, 0), 8)
+    copies[1].wait()
+    for x in range(2):
+        for f in range(EARLY):
+            row = (2 * f + x) * HALO
+            early_ref[row : row + HALO] = held_ref[x, f, pl.ds(start, HALO)] * mask
+    copies[2].wait()
+
+
+def rest_kernel(wave_ref, mask_ref, late_ref, link_ref, chip_ref, ends_ref):
     odd = is_odd()
     mask = mask_column(mask_ref)
     slices = wave_ref.shape[1]
+    lane = iota((BLOCK, LANES), 1)
+    ends = jnp.zeros((BLOCK, LANES), F32)
     for f in range(slices):
         for x in range(2):
             masked = wave_ref[x, f] * mask
             row = (2 * f + x) * HALO
             chip_ref[row : row + HALO] = at_end(masked, jnp.logical_not(odd))
-            if f < FIRST:
-                head_ref[row : row + HALO] = at_end(masked, odd)
-            else:
+            if f >= FIRST:
                 row -= 2 * FIRST * HALO
                 link_ref[row : row + HALO] = at_end(masked, odd)
+            elif f >= EARLY:
+                row -= 2 * EARLY * HALO
+                late_ref[row : row + HALO] = at_end(masked, odd)
+            place = 4 * (x * slices + f)
+            last = pltpu.roll(masked[:, -LANES:], (place + SHALF) % LANES, 1)
+            first = pltpu.roll(masked[:, :LANES], place + SHALF, 1)
+            ends = jnp.where(lane // 2 == place // 2, last, ends)
+            ends = jnp.where(lane // 2 == place // 2 + 1, first, ends)
+    ends_ref[...] = ends
 
 
 def merged_ends(before_ref, after_ref):
     return jnp.where(iota((BLOCK, LANES), 1) % 4 < SHALF, before_ref[...], after_ref[...])
 
 
-def pack_kernel(before_ref, after_ref, _link_in, _chip_in, link_ref, chip_ref):
+def pack_kernel(before_ref, after_ref, _link_in, link_ref, ends_ref):
     odd = is_odd()
     ends = merged_ends(before_ref, after_ref)
-    for ref, tail in ((link_ref, odd), (chip_ref, jnp.logical_not(odd))):
-        rows = at_end(ends, tail)
-        ref[ref.shape[0] - HALO // 2 :] = jnp.concatenate([rows[: HALO // 2], rows[HALO // 2 :]], axis=1)
-
-
-def band_kernel(wave_ref, band_ref, high_ref, low_ref, energy_ref):
+    rows = at_end(ends, odd)
+    link_ref[link_ref.shape[0] - HALO // 2 :] = jnp.concatenate([rows[: HALO // 2], rows[HALO // 2 :]], axis=1)
+    ends_ref[...] = at_end(ends, jnp.logical_not(odd))
+
+
+def band_kernel(taper_ref, wave_ref, band_ref, high_ref, low_ref, th_ref, tl_ref, energy_ref):
+    shots = wave_ref.shape[3]
+    th_ref[...], tl_ref[...] = split(weights_at(taper_ref, iota((shots, shots), 0) - iota((shots, shots), 1)))
     low_half = iota((BLOCK, LANES), 1) < APER
     for f in range(wave_ref.shape[1]):
         at = (f // 2) * LANES
@@ -148,27 +155,25 @@
 
 
 def gather_kernel(
-    shift_ref, taper_ref, wave_ref, mask_ref, high_ref, low_ref, head_ref, chip_ref, mult_ref, th_ref, tl_ref, frames_ref,
+    base, shift_ref, wave_ref, mask_ref, high_ref, low_ref, th_ref, tl_ref, link_ref, chip_ref, part_ref, frames_ref,
     ph_ref, pl_ref,
 ):
     start = SPARE + shift_ref[0]
     mask = mask_column(mask_ref)
-    shots = wave_ref.shape[3]
-    taper = split(weights_at(taper_ref, iota((shots, shots), 0) - iota((shots, shots), 1)))
-    th_ref[...], tl_ref[...] = taper
-    rows = 2 * BLOCK
-    for f in range(FIRST):
-        at = 2 * f * HALO
-        data = window(
-            frames_ref.at[f], wave_ref, mask, chip_ref, lambda x, at=at: head_ref[at + x * HALO : at + (x + 1) * HALO], f, start
+    count, rows, shots = part_ref.shape
+
+    def linked(x, i):
+        at = (2 * i + x) * HALO
+        return link_ref[at : at + HALO]
+
+    for i in range(count):
+        f = base + i
+        data = window(frames_ref.at[i], wave_ref, mask, chip_ref, lambda x, i=i: linked(x, i), f, start)
+        ph_ref[i * rows : (i + 1) * rows], pl_ref[i * rows : (i + 1) * rows] = split(
+            product((high_ref[f], low_ref[f]), split(data))
         )
-        part = slice(f * rows, (f + 1) * rows)
-        ph_ref[part], pl_ref[part] = split(product((high_ref[f], low_ref[f]), split(data)))
-    group = FIRST // 2
-    for i in range(2):
-        part = slice(i * group * rows, (i + 1) * group * rows)
-        whole = product((ph_ref[part], pl_ref[part]), taper)
-        mult_ref[i * group : (i + 1) * group] = whole.reshape(group, rows, shots)
+    whole = product((ph_ref[...], pl_ref[...]), (th_ref[...], tl_ref[...]))
+    part_ref[...] = whole.reshape(count, rows, shots)
 
 
 def weights_at(taper_ref, ahead):
@@ -179,8 +184,8 @@
 
 
 def finish_kernel(
-    shift_ref, taper_ref, wave_ref, mask_ref, high_ref, low_ref, part_ref, th_ref, tl_ref, link_ref, chip_ref, before_ref,
-    after_ref, data_ref, out_ref, mult_ref, spread_ref, kept_ref, frames_ref, pred_ref, sems,
+    shift_ref, taper_ref, wave_ref, mask_ref, high_ref, low_ref, th_ref, tl_ref, early_ref, late_ref, link_ref, chip_ref,
+    ends_ref, before_ref, after_ref, data_ref, mult_ref, sums_ref, kept_ref, frames_ref, pred_ref,
 ):
     start = SPARE + shift_ref[0]
     slices = wave_ref.shape[1]
@@ -192,13 +197,10 @@
         at = (2 * (f - FIRST) + x) * HALO
         return link_ref[at : at + HALO]
 
-    def unpacked(ref):
-        cells = ref[ref.shape[0] - HALO // 2 :]
-        return jnp.concatenate([cells[:, :LANES], cells[:, LANES:]], axis=0)
-
+    packed = link_ref[link_ref.shape[0] - HALO // 2 :]
+    packed = jnp.concatenate([packed[:, :LANES], packed[:, LANES:]], axis=0)
     ends = framed(
-        frames_ref.at[slices - FIRST, 0, 0], merged_ends(before_ref, after_ref), unpacked(chip_ref), unpacked(link_ref),
-        start,
+        frames_ref.at[slices - FIRST, 0, 0], merged_ends(before_ref, after_ref), ends_ref[...], packed, start
     )
     ends = split(ends)
     kind = iota((LANES, LANES), 0) % 4
@@ -212,7 +214,6 @@
         pred_ref[f - FIRST] = product(pred, (th_ref[...], tl_ref[...]))
     near = iota((rows, LANES), 1) < LANES // 2
     squares = []
-    writes = []
     group = 4
     for first in range(0, slices, group):
         shape = (group, rows, LANES)
@@ -224,7 +225,7 @@
             edge = jnp.where(owner == x * slices, product(matrices, ends).reshape(shape), edge)
         edge = product(split(edge.reshape(group * rows, LANES)), reach)
         for f in range(first, first + group):
-            own = part_ref[f] if f < FIRST else pred_ref[f - FIRST]
+            own = early_ref[f] if f < EARLY else late_ref[f - EARLY] if f < FIRST else pred_ref[f - FIRST]
             extra = edge[(f - first) * rows : (f - first + 1) * rows]
             total = jnp.concatenate(
                 [own[:, :LANES] + jnp.where(near, extra, 0.0), own[:, LANES:] + jnp.where(near, 0.0, extra)], axis=1
@@ -233,9 +234,6 @@
             mult_ref[1, f] = total[BLOCK:]
             total = jnp.sum(total * total, axis=0, keepdims=True)
             squares.append(total[:, :LANES] + total[:, LANES:])
-        part = pl.ds(first, group)
-        writes.append(pltpu.make_async_copy(mult_ref.at[:, part], out_ref.at[:, part], sems.at[first // group]))
-        writes[-1].start()
     lane = iota((slices, LANES), 1) - iota((slices, LANES), 0)
     row = iota((slices, LANES), 0)
     pred_rows = jnp.zeros((slices, LANES), F32)
@@ -244,10 +242,8 @@
     pred_energy = jnp.sum(pred_rows, axis=1, keepdims=True)
     data_energy = jnp.sum(data_ref[...], axis=1, keepdims=True)
     energies = jnp.where(lane == 0, data_energy, jnp.where(lane == slices, pred_energy, 0.0))
-    spread_ref[...] = jnp.broadcast_to(jnp.sum(energies, axis=0, keepdims=True), spread_ref.shape)
+    sums_ref[...] = jnp.sum(energies, axis=0, keepdims=True)
     kept_ref[...] = wave_ref[:, :KEPT]
-    for copy in writes:
-        copy.wait()
 
 
 def subtract_kernel(total_ref, kept_ref, wave_ref, mult_ref, out_ref, held_ref, in_sems, out_sems):
@@ -316,86 +312,87 @@
     devices = lax.axis_size(SRC_RCV)
     in_hbm = pltpu.with_memory_space_constraint(wavefield, pltpu.HBM)
 
-    wave, ends = call(
+    rows = 2 * receivers
+
+    def in_vmem(*shape, dtype=F32):
+        return pltpu.VMEM(shape, dtype)
+
+    wave, early = call(
         head_kernel,
         [HBM, HBM],
-        [pltpu.VMEM((2, slices, receivers, shots), F32), pltpu.VMEM((BLOCK, LANES), F32)],
+        [in_vmem(2, slices, receivers, shots), in_vmem(2 * EARLY * HALO, shots)],
         1 << 20,
         scratch=[pltpu.VMEM((1, receivers), jnp.int32), pltpu.SemaphoreType.DMA((3,))],
     )(in_hbm, pltpu.with_memory_space_constraint(mask, pltpu.HBM))
-    after = lax.ppermute(ends, SRC, src_down)
-    before = lax.ppermute(ends, SRC, src_up)
+    early = lax.ppermute(early, RCV, swaps(RCV, 1))
 
     wave, band = on_chip(wave, surface_band)
-    head, link, chip = call(
+    late, link, chip, ends = call(
         rest_kernel,
         [VMEM, VMEM],
         [
-            pltpu.VMEM((2 * FIRST * HALO, shots), F32),
-            pltpu.VMEM((2 * (slices - FIRST) * HALO + HALO // 2, shots), F32),
-            pltpu.VMEM((2 * slices * HALO + HALO // 2, shots), F32),
+            in_vmem(2 * (FIRST - EARLY) * HALO, shots),
+            in_vmem(2 * (slices - FIRST) * HALO + HALO // 2, shots),
+            in_vmem(2 * slices * HALO, shots),
+            in_vmem(BLOCK, LANES),
         ],
         1 << 20,
     )(wave, mask)
-    head = lax.ppermute(head, RCV, swaps(RCV, 1))
-
-    before, after, link, chip = on_chip(before, after, link, chip)
-    link, chip = call(
-        pack_kernel,
-        [VMEM, VMEM, ANY, ANY],
-        [pltpu.VMEM(link.shape, F32), pltpu.VMEM(chip.shape, F32)],
-        1 << 16,
-        aliases={2: 0, 3: 1},
-    )(before, after, link, chip)
+    after = lax.ppermute(ends, SRC, src_down)
+    before = lax.ppermute(ends, SRC, src_up)
+    late = lax.ppermute(late, RCV, swaps(RCV, 1))
+
+    chip = lax.ppermute(chip, RCV, swaps(RCV, 0))
+
+    before, after, link = on_chip(before, after, link)
+    link, ends = call(
+        pack_kernel, [VMEM, VMEM, ANY], [in_vmem(*link.shape), in_vmem(HALO, LANES)], 1 << 16, aliases={2: 0}
+    )(before, after, link)
     link = lax.ppermute(link, RCV, swaps(RCV, 1))
-    chip = lax.ppermute(chip, RCV, swaps(RCV, 0))
-
-    rows = 2 * receivers
-    high, low, data_energy = call(
+    ends = lax.ppermute(ends, RCV, swaps(RCV, 0))
+
+    high, low, taper_high, taper_low, data_energy = call(
         band_kernel,
-        [VMEM, VMEM],
+        [SMEM, VMEM, VMEM],
         [
-            pltpu.VMEM((slices, rows, 2 * LANES), BF16),
-            pltpu.VMEM((slices, rows, 2 * LANES), BF16),
-            pltpu.VMEM((slices, LANES), F32),
+            in_vmem(slices, rows, 2 * LANES, dtype=BF16),
+            in_vmem(slices, rows, 2 * LANES, dtype=BF16),
+            in_vmem(shots, shots, dtype=BF16),
+            in_vmem(shots, shots, dtype=BF16),
+            in_vmem(slices, LANES),
         ],
         1 << 28,
-    )(wave, band)
-    high, low, head, chip = on_chip(high, low, head, chip)
+    )(shot_taper, wave, band)
+    matrices = on_chip(high, low, taper_high, taper_low)
+    early, late, link, chip, ends = on_chip(early, late, link, chip, ends)
     frame = (2, shots // LANES, 2 * HALO + BLOCK, LANES)
-    partial, taper_high, taper_low = call(
-        gather_kernel,
-        [SMEM, SMEM] + [VMEM] * 6,
-        [
-            pltpu.VMEM((FIRST, rows, shots), F32),
-            pltpu.VMEM((shots, shots), BF16),
-            pltpu.VMEM((shots, shots), BF16),
-        ],
+
+    def gathered(base, count, message):
+        (part,) = call(
+            functools.partial(gather_kernel, base),
+            [SMEM] + [VMEM] * 8,
+            [in_vmem(count, rows, shots)],
+            1 << 28,
+            scratch=[pltpu.VMEM((count,) + frame, F32)] + [pltpu.VMEM((count * rows, shots), BF16)] * 2,
+        )(band_shift, wave, mask, *matrices, message, chip)
+        return part
+
+    parts = on_chip(gathered(0, EARLY, early), gathered(EARLY, FIRST - EARLY, late))
+    multiples, sums, kept = call(
+        finish_kernel,
+        [SMEM, SMEM] + [VMEM] * 14,
+        [in_vmem(2, slices, receivers, shots), in_vmem(1, LANES), in_vmem(2, KEPT, receivers, shots)],
         1 << 28,
-        scratch=[pltpu.VMEM((FIRST,) + frame, F32)] + [pltpu.VMEM((FIRST * rows, shots), BF16)] * 2,
-    )(band_shift, shot_taper, wave, mask, high, low, head, chip)
-    multiples, scaled, spread, kept = call(
-        finish_kernel,
-        [SMEM, SMEM] + [VMEM] * 12,
-        [
-            jax.ShapeDtypeStruct((2, slices, receivers, shots), F32),
-            pltpu.VMEM((2, slices, receivers, shots), F32),
-            pltpu.VMEM((devices, LANES), F32),
-            pltpu.VMEM((2, KEPT, receivers, shots), F32),
-        ],
-        1 << 28,
-        out_specs=[HBM, VMEM, VMEM, VMEM],
         scratch=[
             pltpu.VMEM((slices - FIRST + 1,) + frame, F32),
             pltpu.VMEM((slices - FIRST, rows, shots), F32),
-            pltpu.SemaphoreType.DMA((slices // 4,)),
         ],
     )(
-        band_shift, shot_taper, wave, mask, high, low, *on_chip(partial, taper_high, taper_low, link), chip, before,
-        after, *on_chip(data_energy),
+        band_shift, shot_taper, wave, mask, *matrices, *parts, link, chip, ends, before, after, *on_chip(data_energy),
     )
 
-    energies = lax.all_to_all(spread[:, None], SRC_RCV, 0, 0, tiled=True).reshape(devices, LANES)
+    spread = jnp.broadcast_to(sums[None], (devices, 1, LANES))
+    energies = lax.all_to_all(spread, SRC_RCV, 0, 0, tiled=True).reshape(devices, LANES)
 
     (primaries,) = call(
         subtract_kernel,
@@ -404,7 +401,7 @@
         1 << 20,
         out_specs=[HBM],
         scratch=[pltpu.VMEM((2, slices, receivers, shots), F32)] + [pltpu.SemaphoreType.DMA((slices,))] * 2,
-    )(*on_chip(energies, kept), in_hbm, *on_chip(scaled))
+    )(*on_chip(energies, kept), in_hbm, *on_chip(multiples))
     return (multiples, primaries)
 
 

time: 72.9 us -> 68.2 us (0.936)
  blocking collectives: 28.4 us -> 0 us
  waiting for transfers between devices: 13.5 us -> 24.4 us
  starting transfers between devices: 16.8 us -> 27.6 us
  local copies, waits for them, and re-layouts: 0.01 us -> 2.06 us
    all_to_all x1 -> x0, blocking collectives: 28.4 us -> none  [per_device(): lax.all_to_all(spread[:, None], SRC_RCV, 0, 0, tiled=True)]
    ppermute x1 -> x3, waiting for transfers between devices: 12.9 us -> 0.01 us  [the longest x1 0.01 us: per_device(): late = lax.ppermute(late, RCV, swaps(RCV, 1))]
    all_to_all x0 -> x1, waiting for transfers between devices: none -> 11.5 us  [per_device(): lax.all_to_all(spread, SRC_RCV, 0, 0, tiled=True).reshape(devices, LANES)]
    ppermute x1, waiting for transfers between devices: 0.01 us -> 11 us  [per_device(): after = lax.ppermute(ends, SRC, src_down)]
    all_to_all x0 -> x1, starting transfers between devices: none -> 9.97 us  [per_device(): lax.all_to_all(spread, SRC_RCV, 0, 0, tiled=True).reshape(devices, LANES)]
    ppermute x1 -> x3, starting transfers between devices: 1.91 us -> 5.64 us  [the longest x1 3.64 us: per_device(): late = lax.ppermute(late, RCV, swaps(RCV, 1))]
    ppermute x1, waiting for transfers between devices: 0.01 us -> 1.81 us  [per_device(): link = lax.ppermute(link, RCV, swaps(RCV, 1))]
    ppermute x1, starting transfers between devices: 3.64 us -> 1.92 us  [per_device(): link = lax.ppermute(link, RCV, swaps(RCV, 1))]
  transfers between devices with their start and end apart: 5 -> 8, of which waited for: 2 -> 3; matrix products, arithmetic and copies ran while one was open for 0% -> 2% of each run, Pallas kernels for 5% -> 6%
where the time goes in v6:
time: 68.2 us; the launch traced here: 67.9 us
  starting transfers between devices  27.6 us (40%)
  waiting for transfers between devices  24.4 us (36%)
  Pallas kernels  12.4 us (18%)
  local copies, waits for them, and re-layouts  2.06 us (3%)
  between operations  1.45 us (2%)
    all_to_all x1, waiting for transfers between devices, per_device(): lax.all_to_all(spread, SRC_RCV, 0, 0, tiled=True).reshape(devices, LANES)  11.5 us
    ppermute x1, waiting for transfers between devices, per_device(): after = lax.ppermute(ends, SRC, src_down)  11 us
    all_to_all x1, starting transfers between devices, per_device(): lax.all_to_all(spread, SRC_RCV, 0, 0, tiled=True).reshape(devices, LANES)  9.97 us
    ppermute x1, starting transfers between devices, per_device(): before = lax.ppermute(ends, SRC, src_up)  5.49 us
    ppermute x1, starting transfers between devices, per_device(): late = lax.ppermute(late, RCV, swaps(RCV, 1))  3.64 us
    pallas_call x1, Pallas kernels, per_device(): call(finish_kernel, [SMEM, SMEM] + [VMEM] * 14, [in_vmem(2, slices, recei...  3.44 us
    ppermute x1, starting transfers between devices, per_device(): chip = lax.ppermute(chip, RCV, swaps(RCV, 0))  3.29 us
    pallas_call x1, Pallas kernels, per_device(): call(subtract_kernel, [VMEM, VMEM, HBM, VMEM], [jax.ShapeDtypeStruct((2,...  2.73 us
  transfers between devices with their start and end apart: 8, of which 3 were waited for; matrix products, arithmetic and copies ran while one was open for 2% of the time, Pallas kernels for 6%

profile of v6, /device:TPU:1, one launch (start us, length us, event | category | flops | bytes accessed | tf_op | source)
XLA Modules:
  0.0 67.9 jit_solution(17459314556418445956)
XLA Ops:
  0.6 0.0 copy-start.1
  0.6 0.0 copy-start
  0.7 0.0 copy-start.2
  0.7 1.6 %shard_map.68 = (f32[2,16,64,256]{3,2,1,0:T(8,128)S(1)}, f32[864,256]{1,0:T(8,128)S(1)}) custom-call(f32[2,16,64,256]{3,2,1,0:T(8,128)} %wave_ref.3, s32[1,64]{1,0:T(1,128)} %bitcast.4), custom_call_target="tpu_custom_call" | custom-call | flops 1048576 | bytes 1048576 | tf_op jit(solution)/shard_map/pallas_call | solution.py:320
  2.3 0.0 copy-done.1
  2.3 0.8 %shard_map.70 = (f32[384,256]{1,0:T(8,128)S(1)}, f32[312,256]{1,0:T(8,128)S(1)}, f32[1536,256]{1,0:T(8,128)S(1)}, f32[64,128]{1,0:T(8,128)S(1)}) custom-call(f32[2,16,64,256]{3,2,1,0:T(8,128)S(1)} %get-tuple-element.18.wave_ref, s32[1,64]{1,0:T(1,128)S(1)} %bitcast.5), custom_call_target="tpu_custom_call" | custom-call | flops 1048576 | bytes 1048576 | tf_op jit(solution)/shard_map/pallas_call | solution.py:330
  3.1 3.3 %collective-permute-start.1 = (f32[1536,256]{1,0:T(8,128)S(1)}, f32[1536,256]{1,0:T(8,128)S(1)}, u32[]{:S(2)}, u32[]{:S(2)}) collective-permute-start(f32[1536,256]{1,0:T(8,128)S(1)} %get-tuple-element.24), channel_id=1, source_target_pairs={{0,1},{2,3},{4,5},{6,7},{8,9},{10,11},{12,13},{14,15},{16,17},{18,... | collective-permute-start | bytes 4718600 | tf_op jit(solution)/shard_map/ppermute | solution.py:345
  6.4 1.9 %collective-permute-start = (f32[864,256]{1,0:T(8,128)S(1)}, f32[864,256]{1,0:T(8,128)S(1)}, u32[]{:S(2)}, u32[]{:S(2)}) collective-permute-start(f32[864,256]{1,0:T(8,128)S(1)} %get-tuple-element.23), channel_id=1, source_target_pairs={{1,2},{3,4},{5,6},{7,8},{9,10},{11,12},{13,14},{15,16},{17,18},{19... | collective-permute-start | bytes 2654216 | tf_op jit(solution)/shard_map/ppermute | solution.py:327
  8.3 3.6 %collective-permute-start.2 = (f32[384,256]{1,0:T(8,128)S(1)}, f32[384,256]{1,0:T(8,128)S(1)}, u32[]{:S(2)}, u32[]{:S(2)}) collective-permute-start(f32[384,256]{1,0:T(8,128)S(1)} %get-tuple-element.25), channel_id=1, source_target_pairs={{1,2},{3,4},{5,6},{7,8},{9,10},{11,12},{13,14},{15,16},{17,18},{19... | collective-permute-start | bytes 1179656 | tf_op jit(solution)/shard_map/ppermute | solution.py:343
  12.0 1.3 %collective-permute-start.4 = (f32[64,128]{1,0:T(8,128)S(1)}, f32[64,128]{1,0:T(8,128)S(1)}, u32[]{:S(2)}, u32[]{:S(2)}) collective-permute-start(f32[64,128]{1,0:T(8,128)S(1)} %get-tuple-element.26), channel_id=1, source_target_pairs={{32,0},{64,32},{96,64},{128,96},{160,128},{192,160},{224,192},{33,... | collective-permute-start | bytes 98312 | tf_op jit(solution)/shard_map/ppermute | solution.py:341
  13.3 5.5 %collective-permute-start.3 = (f32[64,128]{1,0:T(8,128)S(1)}, f32[64,128]{1,0:T(8,128)S(1)}, u32[]{:S(2)}, u32[]{:S(2)}) collective-permute-start(f32[64,128]{1,0:T(8,128)S(1)} %get-tuple-element.26), channel_id=1, source_target_pairs={{0,32},{32,64},{64,96},{96,128},{128,160},{160,192},{192,224},{1,3... | collective-permute-start | bytes 98312 | tf_op jit(solution)/shard_map/ppermute | solution.py:342
  18.8 11.0 %collective-permute-done.4.after_ref = f32[64,128]{1,0:T(8,128)S(1)} collective-permute-done((f32[64,128]{1,0:T(8,128)S(1)}, f32[64,128]{1,0:T(8,128)S(1)}, u32[]{:S(2)}, u32[]{:S(2)}) %collective-permute-start.4) | collective-permute-done | bytes 32800 | tf_op jit(solution)/shard_map/ppermute | solution.py:341
  29.8 0.0 collective-permute-done.3.before_ref
  29.8 1.9 %collective-permute-start.5 = (f32[312,256]{1,0:T(8,128)S(1)}, f32[312,256]{1,0:T(8,128)S(1)}, u32[]{:S(2)}, u32[]{:S(2)}) collective-permute-start(f32[312,256]{1,0:T(8,128)S(1)} %get-tuple-element.28), channel_id=1, source_target_pairs={{1,2},{3,4},{5,6},{7,8},{9,10},{11,12},{13,14},{15,16},{17,18},{19... | collective-permute-start | bytes 958472 | tf_op jit(solution)/shard_map/ppermute | solution.py:351
  32.4 0.0 copy-done
  32.4 0.0 copy-done.2
  32.4 1.2 %shard_map.69 = (bf16[16,128,256]{2,1,0:T(8,128)(2,1)S(1)}, bf16[16,128,256]{2,1,0:T(8,128)(2,1)S(1)}, bf16[256,256]{1,0:T(8,128)(2,1)S(1)}, bf16[256,256]{1,0:T(8,128)(2,1)S(1)}, f32[16,128]{1,0:T(8,128)S(1)}) custom-call(f32[5]{0:T(128)S(1)} %copy-done.2, f32[2,16,64,256]{3,2,1,0:T(8,128)S(1)} %get-tuple-element.18.wave_ref, f32[2,64,1024]{2,1,0:T(8,128)S(1)} %copy-done), custom_call_target="tpu_custom_call" | custom-call | flops 268435456 | bytes 1048576 | tf_op jit(solution)/shard_map/pallas_call | solution.py:354
  33.6 0.1 collective-permute-start.6
  33.7 0.0 collective-permute-done.2.link_ref
  33.7 0.0 collective-permute-done.1.chip_ref
  33.7 0.9 %shard_map.72.late_ref = f32[4,128,256]{2,1,0:T(8,128)S(1)} custom-call(s32[1]{0:T(128)S(6)} %copy.10.shift_ref, f32[2,16,64,256]{3,2,1,0:T(8,128)S(1)} %get-tuple-element.18.wave_ref, s32[1,64]{1,0:T(1,128)S(1)} %bitcast.6, bf16[16,128,256]{2,1,0:T(8,128)(2,1)S(1)} %get-tuple-element.19.high_ref, bf16[16,128,256]{2,1,0:T(8,128)(2,1)S(1)} %get-tuple-element.20.low_ref, ...), custom_call_target="tpu_custom_call" | custom-call | flops 268435456 | bytes 1048576 | tf_op jit(solution)/shard_map/pallas_call | solution.py:371
  34.6 0.0 collective-permute-done.link_ref
  34.6 1.7 %shard_map.71.early_ref = f32[9,128,256]{2,1,0:T(8,128)S(1)} custom-call(s32[1]{0:T(128)S(6)} %copy.10.shift_ref, f32[2,16,64,256]{3,2,1,0:T(8,128)S(1)} %get-tuple-element.18.wave_ref, s32[1,64]{1,0:T(1,128)S(1)} %bitcast.7, bf16[16,128,256]{2,1,0:T(8,128)(2,1)S(1)} %get-tuple-element.19.high_ref, bf16[16,128,256]{2,1,0:T(8,128)(2,1)S(1)} %get-tuple-element.20.low_ref, ...), custom_call_target="tpu_custom_call" | custom-call | flops 268435456 | bytes 1048576 | tf_op jit(solution)/shard_map/pallas_call | solution.py:371
  36.3 0.0 collective-permute-done.6.ends_ref
  36.3 1.8 %collective-permute-done.5.link_ref = f32[312,256]{1,0:T(8,128)S(1)} collective-permute-done((f32[312,256]{1,0:T(8,128)S(1)}, f32[312,256]{1,0:T(8,128)S(1)}, u32[]{:S(2)}, u32[]{:S(2)}) %collective-permute-start.5) | collective-permute-done | bytes 319520 | tf_op jit(solution)/shard_map/ppermute | solution.py:351
  38.1 3.4 %shard_map.74 = (f32[2,16,64,256]{3,2,1,0:T(8,128)S(1)}, f32[1,128]{1,0:T(1,128)S(1)}, f32[2,8,64,256]{3,2,1,0:T(8,128)S(1)}) custom-call(s32[1]{0:T(128)S(6)} %copy.10.shift_ref, f32[5]{0:T(128)S(1)} %copy-done.2, f32[2,16,64,256]{3,2,1,0:T(8,128)S(1)} %get-tuple-element.18.wave_ref, s32[1,64]{1,0:T(1,128)S(1)} %bitcast.8, ...), custom_call_target="tpu_custom_call" | custom-call | flops 268435456 | bytes 1048576 | tf_op jit(solution)/shard_map/pallas_call | solution.py:381
  41.6 0.7 %broadcast_in_dim.9 = f32[256,1,128]{2,1,0:T(1,128)} broadcast(f32[128]{0:T(128)S(1)} %bitcast.9), dimensions={2} | broadcast | bytes 131584 | tf_op jit(solution)/shard_map/broadcast_in_dim | solution.py:394
  42.3 10.0 %all-to-all-start = ((f32[256,1,128]{2,1,0:T(1,128)}), f32[256,1,128]{2,1,0:T(1,128)S(1)}, u32[]{:S(2)}, u32[]{:S(2)}) async-start(f32[256,1,128]{2,1,0:T(1,128)} %broadcast_in_dim.9), calls=%async_computation | async-start | bytes 262144 | tf_op jit(solution)/shard_map/all_to_all | solution.py:395
  52.3 1.3 %copy.9 = f32[2,16,64,256]{3,2,1,0:T(8,128)} copy(f32[2,16,64,256]{3,2,1,0:T(8,128)S(1)} %get-tuple-element.34.mult_ref) | data formatting | bytes 4194304
  53.6 11.5 %all-to-all-done = f32[256,1,128]{2,1,0:T(1,128)S(1)} async-done(((f32[256,1,128]{2,1,0:T(1,128)}), f32[256,1,128]{2,1,0:T(1,128)S(1)}, u32[]{:S(2)}, u32[]{:S(2)}) %all-to-all-start) | async-done | bytes 131104 | tf_op jit(solution)/shard_map/all_to_all | solution.py:395
  65.2 2.7 %shard_map.75 = f32[2,16,64,256]{3,2,1,0:T(8,128)} custom-call(f32[256,128]{1,0:T(8,128)S(1)} %bitcast.3, f32[2,8,64,256]{3,2,1,0:T(8,128)S(1)} %get-tuple-element.33.kept_ref, f32[2,16,64,256]{3,2,1,0:T(8,128)} %wave_ref.3, f32[2,16,64,256]{3,2,1,0:T(8,128)S(1)} %get-tuple-element.34.mult_ref), custom_call_target="tpu_custom_call" | custom-call | flops 1048576 | bytes 1048576 | tf_op jit(solution)/shard_map/pallas_call | solution.py:397
  (1 shorter events, 0.0 us)
Async XLA Ops:
  0.6 1.7 %copy-start.1 = (s32[64]{0:T(128)S(1)}, s32[64]{0:T(128)}, u32[]{:S(2)}) copy-start(s32[64]{0:T(128)} %param.8) | copy-start | bytes 772
  0.6 31.8 %copy-start = (f32[2,64,1024]{2,1,0:T(8,128)S(1)}, f32[2,64,1024]{2,1,0:T(8,128)}, u32[]{:S(2)}) copy-start(f32[2,64,1024]{2,1,0:T(8,128)} %band_ref.1) | copy-start | bytes 1572868
  0.7 31.8 %copy-start.2 = (f32[5]{0:T(128)S(1)}, f32[5]{0:T(128)}, u32[]{:S(2)}) copy-start(f32[5]{0:T(128)} %taper_ref.3) | copy-start | bytes 64
  3.1 30.6 %collective-permute-start.1 = (f32[1536,256]{1,0:T(8,128)S(1)}, f32[1536,256]{1,0:T(8,128)S(1)}, u32[]{:S(2)}, u32[]{:S(2)}) collective-permute-start(f32[1536,256]{1,0:T(8,128)S(1)} %get-tuple-element.24), channel_id=1, source_target_pairs={{0,1},{2,3},{4,5},{6,7},{8,9},{10,11},{12,13},{14,15},{16,17},{18,... | collective-permute-start | bytes 4718600 | tf_op jit(solution)/shard_map/ppermute | solution.py:345
  6.4 28.2 %collective-permute-start = (f32[864,256]{1,0:T(8,128)S(1)}, f32[864,256]{1,0:T(8,128)S(1)}, u32[]{:S(2)}, u32[]{:S(2)}) collective-permute-start(f32[864,256]{1,0:T(8,128)S(1)} %get-tuple-element.23), channel_id=1, source_target_pairs={{1,2},{3,4},{5,6},{7,8},{9,10},{11,12},{13,14},{15,16},{17,18},{19... | collective-permute-start | bytes 2654216 | tf_op jit(solution)/shard_map/ppermute | solution.py:327
  8.3 25.3 %collective-permute-start.2 = (f32[384,256]{1,0:T(8,128)S(1)}, f32[384,256]{1,0:T(8,128)S(1)}, u32[]{:S(2)}, u32[]{:S(2)}) collective-permute-start(f32[384,256]{1,0:T(8,128)S(1)} %get-tuple-element.25), channel_id=1, source_target_pairs={{1,2},{3,4},{5,6},{7,8},{9,10},{11,12},{13,14},{15,16},{17,18},{19... | collective-permute-start | bytes 1179656 | tf_op jit(solution)/shard_map/ppermute | solution.py:343
  12.0 17.8 %collective-permute-start.4 = (f32[64,128]{1,0:T(8,128)S(1)}, f32[64,128]{1,0:T(8,128)S(1)}, u32[]{:S(2)}, u32[]{:S(2)}) collective-permute-start(f32[64,128]{1,0:T(8,128)S(1)} %get-tuple-element.26), channel_id=1, source_target_pairs={{32,0},{64,32},{96,64},{128,96},{160,128},{192,160},{224,192},{33,... | collective-permute-start | bytes 98312 | tf_op jit(solution)/shard_map/ppermute | solution.py:341
  13.3 16.5 %collective-permute-start.3 = (f32[64,128]{1,0:T(8,128)S(1)}, f32[64,128]{1,0:T(8,128)S(1)}, u32[]{:S(2)}, u32[]{:S(2)}) collective-permute-start(f32[64,128]{1,0:T(8,128)S(1)} %get-tuple-element.26), channel_id=1, source_target_pairs={{0,32},{32,64},{64,96},{96,128},{128,160},{160,192},{192,224},{1,3... | collective-permute-start | bytes 98312 | tf_op jit(solution)/shard_map/ppermute | solution.py:342
  29.8 8.3 %collective-permute-start.5 = (f32[312,256]{1,0:T(8,128)S(1)}, f32[312,256]{1,0:T(8,128)S(1)}, u32[]{:S(2)}, u32[]{:S(2)}) collective-permute-start(f32[312,256]{1,0:T(8,128)S(1)} %get-tuple-element.28), channel_id=1, source_target_pairs={{1,2},{3,4},{5,6},{7,8},{9,10},{11,12},{13,14},{15,16},{17,18},{19... | collective-permute-start | bytes 958472 | tf_op jit(solution)/shard_map/ppermute | solution.py:351
  33.6 2.7 %collective-permute-start.6 = (f32[48,128]{1,0:T(8,128)S(1)}, f32[48,128]{1,0:T(8,128)S(1)}, u32[]{:S(2)}, u32[]{:S(2)}) collective-permute-start(f32[48,128]{1,0:T(8,128)S(1)} %get-tuple-element.29), channel_id=1, source_target_pairs={{0,1},{2,3},{4,5},{6,7},{8,9},{10,11},{12,13},{14,15},{16,17},{18,... | collective-permute-start | bytes 73736 | tf_op jit(solution)/shard_map/ppermute | solution.py:352
  42.3 22.8 %all-to-all-start = ((f32[256,1,128]{2,1,0:T(1,128)}), f32[256,1,128]{2,1,0:T(1,128)S(1)}, u32[]{:S(2)}, u32[]{:S(2)}) async-start(f32[256,1,128]{2,1,0:T(1,128)} %broadcast_in_dim.9), calls=%async_computation | async-start | bytes 262144 | tf_op jit(solution)/shard_map/all_to_all | solution.py:395

commit v7 on v6

--- a/solution.py
+++ b/solution.py
@@ -183,37 +183,41 @@
     return weights
 
 
-def finish_kernel(
-    shift_ref, taper_ref, wave_ref, mask_ref, high_ref, low_ref, th_ref, tl_ref, early_ref, late_ref, link_ref, chip_ref,
-    ends_ref, before_ref, after_ref, data_ref, mult_ref, sums_ref, kept_ref, frames_ref, pred_ref,
+def stored(mult_ref, squares_ref, f, own, extra):
+    near = iota(extra.shape, 1) < LANES // 2
+    total = jnp.concatenate(
+        [own[:, :LANES] + jnp.where(near, extra, 0.0), own[:, LANES:] + jnp.where(near, 0.0, extra)], axis=1
+    )
+    mult_ref[0, f] = total[:BLOCK]
+    mult_ref[1, f] = total[BLOCK:]
+    total = jnp.sum(total * total, axis=0, keepdims=True)
+    squares_ref[f : f + 1, :] = total[:, :LANES] + total[:, LANES:]
+
+
+def merge_kernel(
+    shift_ref, taper_ref, wave_ref, mask_ref, high_ref, low_ref, th_ref, tl_ref, early_ref, late_ref, chip_ref, ends_ref,
+    before_ref, after_ref, mult_ref, edge_ref, squares_ref, kept_ref, frames_ref, ph_ref, pl_ref, part_ref,
 ):
     start = SPARE + shift_ref[0]
     slices = wave_ref.shape[1]
     shots = wave_ref.shape[3]
     rows = 2 * BLOCK
-    mask = mask_column(mask_ref)
-
-    def linked(x, f):
-        at = (2 * (f - FIRST) + x) * HALO
-        return link_ref[at : at + HALO]
-
-    packed = link_ref[link_ref.shape[0] - HALO // 2 :]
+    count = FIRST - EARLY
+    packed = late_ref[late_ref.shape[0] - HALO // 2 :]
     packed = jnp.concatenate([packed[:, :LANES], packed[:, LANES:]], axis=0)
-    ends = framed(
-        frames_ref.at[slices - FIRST, 0, 0], merged_ends(before_ref, after_ref), ends_ref[...], packed, start
-    )
-    ends = split(ends)
+    ends = split(
+        framed(frames_ref.at[count, 0, 0], merged_ends(before_ref, after_ref), ends_ref[...], packed, start)
+    )
     kind = iota((LANES, LANES), 0) % 4
     source = jnp.where(kind < SHALF, kind - SHALF, kind - SHALF + shots)
     target = iota((LANES, LANES), 1)
     target = jnp.where(target < LANES // 2, target, target + shots - LANES)
     reach = split(weights_at(taper_ref, source - target))
-    for f in range(FIRST, slices):
-        data = window(frames_ref.at[f - FIRST], wave_ref, mask, chip_ref, lambda x, f=f: linked(x, f), f, start)
-        pred = split(product((high_ref[f], low_ref[f]), split(data)))
-        pred_ref[f - FIRST] = product(pred, (th_ref[...], tl_ref[...]))
-    near = iota((rows, LANES), 1) < LANES // 2
-    squares = []
+    gather_kernel(
+        EARLY, shift_ref, wave_ref, mask_ref, high_ref, low_ref, th_ref, tl_ref, late_ref, chip_ref, part_ref, frames_ref,
+        ph_ref, pl_ref,
+    )
+    kept_ref[...] = wave_ref[:, :KEPT]
     group = 4
     for first in range(0, slices, group):
         shape = (group, rows, LANES)
@@ -225,25 +229,31 @@
             edge = jnp.where(owner == x * slices, product(matrices, ends).reshape(shape), edge)
         edge = product(split(edge.reshape(group * rows, LANES)), reach)
         for f in range(first, first + group):
-            own = early_ref[f] if f < EARLY else late_ref[f - EARLY] if f < FIRST else pred_ref[f - FIRST]
             extra = edge[(f - first) * rows : (f - first + 1) * rows]
-            total = jnp.concatenate(
-                [own[:, :LANES] + jnp.where(near, extra, 0.0), own[:, LANES:] + jnp.where(near, 0.0, extra)], axis=1
-            )
-            mult_ref[0, f] = total[:BLOCK]
-            mult_ref[1, f] = total[BLOCK:]
-            total = jnp.sum(total * total, axis=0, keepdims=True)
-            squares.append(total[:, :LANES] + total[:, LANES:])
-    lane = iota((slices, LANES), 1) - iota((slices, LANES), 0)
-    row = iota((slices, LANES), 0)
-    pred_rows = jnp.zeros((slices, LANES), F32)
-    for f in range(slices):
-        pred_rows = jnp.where(row == f, squares[f], pred_rows)
-    pred_energy = jnp.sum(pred_rows, axis=1, keepdims=True)
+            if f >= FIRST:
+                edge_ref[f - FIRST] = extra
+            else:
+                stored(mult_ref, squares_ref, f, early_ref[f] if f < EARLY else part_ref[f - EARLY], extra)
+    squares_ref[FIRST:] = jnp.zeros((slices - FIRST, LANES), F32)
+
+
+def finish_kernel(
+    shift_ref, wave_ref, mask_ref, high_ref, low_ref, th_ref, tl_ref, link_ref, chip_ref, edge_ref, some_ref, data_ref,
+    _mult_in, mult_ref, sums_ref, frames_ref, ph_ref, pl_ref, part_ref, squares_ref,
+):
+    slices = wave_ref.shape[1]
+    gather_kernel(
+        FIRST, shift_ref, wave_ref, mask_ref, high_ref, low_ref, th_ref, tl_ref, link_ref, chip_ref, part_ref, frames_ref,
+        ph_ref, pl_ref,
+    )
+    squares_ref[...] = some_ref[...]
+    for f in range(FIRST, slices):
+        stored(mult_ref, squares_ref, f, part_ref[f - FIRST], edge_ref[f - FIRST])
+    pred_energy = jnp.sum(squares_ref[...], axis=1, keepdims=True)
     data_energy = jnp.sum(data_ref[...], axis=1, keepdims=True)
-    energies = jnp.where(lane == 0, data_energy, jnp.where(lane == slices, pred_energy, 0.0))
+    place = iota((slices, LANES), 1) - iota((slices, LANES), 0)
+    energies = jnp.where(place == 0, data_energy, jnp.where(place == slices, pred_energy, 0.0))
     sums_ref[...] = jnp.sum(energies, axis=0, keepdims=True)
-    kept_ref[...] = wave_ref[:, :KEPT]
 
 
 def subtract_kernel(total_ref, kept_ref, wave_ref, mult_ref, out_ref, held_ref, in_sems, out_sems):
@@ -331,8 +341,8 @@
         rest_kernel,
         [VMEM, VMEM],
         [
-            in_vmem(2 * (FIRST - EARLY) * HALO, shots),
-            in_vmem(2 * (slices - FIRST) * HALO + HALO // 2, shots),
+            in_vmem(2 * (FIRST - EARLY) * HALO + HALO // 2, shots),
+            in_vmem(2 * (slices - FIRST) * HALO, shots),
             in_vmem(2 * slices * HALO, shots),
             in_vmem(BLOCK, LANES),
         ],
@@ -340,16 +350,7 @@
     )(wave, mask)
     after = lax.ppermute(ends, SRC, src_down)
     before = lax.ppermute(ends, SRC, src_up)
-    late = lax.ppermute(late, RCV, swaps(RCV, 1))
-
     chip = lax.ppermute(chip, RCV, swaps(RCV, 0))
-
-    before, after, link = on_chip(before, after, link)
-    link, ends = call(
-        pack_kernel, [VMEM, VMEM, ANY], [in_vmem(*link.shape), in_vmem(HALO, LANES)], 1 << 16, aliases={2: 0}
-    )(before, after, link)
-    link = lax.ppermute(link, RCV, swaps(RCV, 1))
-    ends = lax.ppermute(ends, RCV, swaps(RCV, 0))
 
     high, low, taper_high, taper_low, data_energy = call(
         band_kernel,
@@ -363,33 +364,50 @@
         ],
         1 << 28,
     )(shot_taper, wave, band)
+
+    before, after, late = on_chip(before, after, late)
+    late, ends = call(
+        pack_kernel, [VMEM, VMEM, ANY], [in_vmem(*late.shape), in_vmem(HALO, LANES)], 1 << 16, aliases={2: 0}
+    )(before, after, late)
+    late = lax.ppermute(late, RCV, swaps(RCV, 1))
+    link = lax.ppermute(link, RCV, swaps(RCV, 1))
+    ends = lax.ppermute(ends, RCV, swaps(RCV, 0))
+
     matrices = on_chip(high, low, taper_high, taper_low)
     early, late, link, chip, ends = on_chip(early, late, link, chip, ends)
     frame = (2, shots // LANES, 2 * HALO + BLOCK, LANES)
 
-    def gathered(base, count, message):
-        (part,) = call(
-            functools.partial(gather_kernel, base),
-            [SMEM] + [VMEM] * 8,
-            [in_vmem(count, rows, shots)],
-            1 << 28,
-            scratch=[pltpu.VMEM((count,) + frame, F32)] + [pltpu.VMEM((count * rows, shots), BF16)] * 2,
-        )(band_shift, wave, mask, *matrices, message, chip)
-        return part
-
-    parts = on_chip(gathered(0, EARLY, early), gathered(EARLY, FIRST - EARLY, late))
-    multiples, sums, kept = call(
+    def workspace(count, frames):
+        return [pltpu.VMEM((frames,) + frame, F32)] + [pltpu.VMEM((count * rows, shots), BF16)] * 2
+
+    (part,) = call(
+        functools.partial(gather_kernel, 0),
+        [SMEM] + [VMEM] * 8,
+        [in_vmem(EARLY, rows, shots)],
+        1 << 28,
+        scratch=workspace(EARLY, EARLY),
+    )(band_shift, wave, mask, *matrices, early, chip)
+    middle, last = FIRST - EARLY, slices - FIRST
+    multiples, edge, squares, kept = call(
+        merge_kernel,
+        [SMEM, SMEM] + [VMEM] * 12,
+        [
+            in_vmem(2, slices, receivers, shots),
+            in_vmem(last, rows, LANES),
+            in_vmem(slices, LANES),
+            in_vmem(2, KEPT, receivers, shots),
+        ],
+        1 << 28,
+        scratch=workspace(middle, middle + 1) + [pltpu.VMEM((middle, rows, shots), F32)],
+    )(band_shift, shot_taper, wave, mask, *matrices, *on_chip(part), late, chip, ends, before, after)
+    multiples, sums = call(
         finish_kernel,
-        [SMEM, SMEM] + [VMEM] * 14,
-        [in_vmem(2, slices, receivers, shots), in_vmem(1, LANES), in_vmem(2, KEPT, receivers, shots)],
+        [SMEM] + [VMEM] * 11 + [ANY],
+        [in_vmem(2, slices, receivers, shots), in_vmem(1, LANES)],
         1 << 28,
-        scratch=[
-            pltpu.VMEM((slices - FIRST + 1,) + frame, F32),
-            pltpu.VMEM((slices - FIRST, rows, shots), F32),
-        ],
-    )(
-        band_shift, shot_taper, wave, mask, *matrices, *parts, link, chip, ends, before, after, *on_chip(data_energy),
-    )
+        scratch=workspace(last, last) + [pltpu.VMEM((last, rows, shots), F32), pltpu.VMEM((slices, LANES), F32)],
+        aliases={12: 0},
+    )(band_shift, wave, mask, *matrices, link, chip, *on_chip(edge, squares, data_energy, multiples))
 
     spread = jnp.broadcast_to(sums[None], (devices, 1, LANES))
     energies = lax.all_to_all(spread, SRC_RCV, 0, 0, tiled=True).reshape(devices, LANES)

time: 68.2 us -> 65.9 us (0.966)
  waiting for transfers between devices: 24.4 us -> 19.6 us
  starting transfers between devices: 27.6 us -> 30.2 us
    ppermute x1, waiting for transfers between devices: 11 us -> 0.01 us  [per_device(): after = lax.ppermute(ends, SRC, src_down)]
    ppermute x1, waiting for transfers between devices: 0.01 us -> 7.9 us  [per_device(): before = lax.ppermute(ends, SRC, src_up)]
    all_to_all x1, starting transfers between devices: 9.97 us -> 12.5 us  [per_device(): lax.all_to_all(spread, SRC_RCV, 0, 0, tiled=True).reshape(devices, LANES)]
    ppermute x1, waiting for transfers between devices: 1.81 us -> 0.01 us  [per_device(): link = lax.ppermute(link, RCV, swaps(RCV, 1))]
    ppermute x1, starting transfers between devices: 3.64 us -> 1.92 us  [per_device(): late = lax.ppermute(late, RCV, swaps(RCV, 1))]
    ppermute x1, starting transfers between devices: 1.92 us -> 3.64 us  [per_device(): link = lax.ppermute(link, RCV, swaps(RCV, 1))]
  transfers between devices with their start and end apart: 8 -> 8, of which waited for: 3 -> 3; matrix products, arithmetic and copies ran while one was open for 2% -> 2% of each run, Pallas kernels for 6% -> 9%
where the time goes in v7:
time: 65.9 us; the launch traced here: 65.6 us
  starting transfers between devices  30.2 us (46%)
  waiting for transfers between devices  19.6 us (30%)
  Pallas kernels  12.3 us (19%)
  local copies, waits for them, and re-layouts  2.07 us (3%)
  between operations  1.45 us (2%)
    all_to_all x1, starting transfers between devices, per_device(): lax.all_to_all(spread, SRC_RCV, 0, 0, tiled=True).reshape(devices, LANES)  12.5 us
    all_to_all x1, waiting for transfers between devices, per_device(): lax.all_to_all(spread, SRC_RCV, 0, 0, tiled=True).reshape(devices, LANES)  11.5 us
    ppermute x1, waiting for transfers between devices, per_device(): before = lax.ppermute(ends, SRC, src_up)  7.9 us
    ppermute x1, starting transfers between devices, per_device(): before = lax.ppermute(ends, SRC, src_up)  5.49 us
    ppermute x1, starting transfers between devices, per_device(): link = lax.ppermute(link, RCV, swaps(RCV, 1))  3.64 us
    pallas_call x1, Pallas kernels, per_device(): call(merge_kernel, [SMEM, SMEM] + [VMEM] * 12, [in_vmem(2, slices, receiv...  3.4 us
    ppermute x1, starting transfers between devices, per_device(): chip = lax.ppermute(chip, RCV, swaps(RCV, 0))  3.29 us
    pallas_call x1, Pallas kernels, per_device(): call(subtract_kernel, [VMEM, VMEM, HBM, VMEM], [jax.ShapeDtypeStruct((2,...  2.73 us
  transfers between devices with their start and end apart: 8, of which 3 were waited for; matrix products, arithmetic and copies ran while one was open for 2% of the time, Pallas kernels for 9%

profile of v7, /device:TPU:1, one launch (start us, length us, event | category | flops | bytes accessed | tf_op | source)
XLA Modules:
  0.0 65.6 jit_solution(11603932428919625116)
XLA Ops:
  0.6 0.0 copy-start.1
  0.6 0.0 copy-start
  0.7 0.0 copy-start.2
  0.7 1.6 %shard_map.68 = (f32[2,16,64,256]{3,2,1,0:T(8,128)S(1)}, f32[864,256]{1,0:T(8,128)S(1)}) custom-call(f32[2,16,64,256]{3,2,1,0:T(8,128)} %wave_ref.3, s32[1,64]{1,0:T(1,128)} %bitcast.4), custom_call_target="tpu_custom_call" | custom-call | flops 1048576 | bytes 1048576 | tf_op jit(solution)/shard_map/pallas_call | solution.py:330
  2.3 0.0 copy-done.1
  2.3 0.8 %shard_map.70 = (f32[408,256]{1,0:T(8,128)S(1)}, f32[288,256]{1,0:T(8,128)S(1)}, f32[1536,256]{1,0:T(8,128)S(1)}, f32[64,128]{1,0:T(8,128)S(1)}) custom-call(f32[2,16,64,256]{3,2,1,0:T(8,128)S(1)} %get-tuple-element.21.wave_ref, s32[1,64]{1,0:T(1,128)S(1)} %bitcast.5), custom_call_target="tpu_custom_call" | custom-call | flops 1048576 | bytes 1048576 | tf_op jit(solution)/shard_map/pallas_call | solution.py:340
  3.1 3.3 %collective-permute-start.1 = (f32[1536,256]{1,0:T(8,128)S(1)}, f32[1536,256]{1,0:T(8,128)S(1)}, u32[]{:S(2)}, u32[]{:S(2)}) collective-permute-start(f32[1536,256]{1,0:T(8,128)S(1)} %get-tuple-element.27), channel_id=1, source_target_pairs={{0,1},{2,3},{4,5},{6,7},{8,9},{10,11},{12,13},{14,15},{16,17},{18,... | collective-permute-start | bytes 4718600 | tf_op jit(solution)/shard_map/ppermute | solution.py:353
  6.4 1.9 %collective-permute-start.2 = (f32[864,256]{1,0:T(8,128)S(1)}, f32[864,256]{1,0:T(8,128)S(1)}, u32[]{:S(2)}, u32[]{:S(2)}) collective-permute-start(f32[864,256]{1,0:T(8,128)S(1)} %get-tuple-element.28), channel_id=1, source_target_pairs={{1,2},{3,4},{5,6},{7,8},{9,10},{11,12},{13,14},{15,16},{17,18},{19... | collective-permute-start | bytes 2654216 | tf_op jit(solution)/shard_map/ppermute | solution.py:337
  8.3 1.3 %collective-permute-start.4 = (f32[64,128]{1,0:T(8,128)S(1)}, f32[64,128]{1,0:T(8,128)S(1)}, u32[]{:S(2)}, u32[]{:S(2)}) collective-permute-start(f32[64,128]{1,0:T(8,128)S(1)} %get-tuple-element.29), channel_id=1, source_target_pairs={{32,0},{64,32},{96,64},{128,96},{160,128},{192,160},{224,192},{33,... | collective-permute-start | bytes 98312 | tf_op jit(solution)/shard_map/ppermute | solution.py:351
  9.6 5.5 %collective-permute-start.3 = (f32[64,128]{1,0:T(8,128)S(1)}, f32[64,128]{1,0:T(8,128)S(1)}, u32[]{:S(2)}, u32[]{:S(2)}) collective-permute-start(f32[64,128]{1,0:T(8,128)S(1)} %get-tuple-element.29), channel_id=1, source_target_pairs={{0,32},{32,64},{64,96},{96,128},{128,160},{160,192},{192,224},{1,3... | collective-permute-start | bytes 98312 | tf_op jit(solution)/shard_map/ppermute | solution.py:352
  15.1 0.0 collective-permute-done.4.after_ref
  15.1 7.9 %collective-permute-done.3.before_ref = f32[64,128]{1,0:T(8,128)S(1)} collective-permute-done((f32[64,128]{1,0:T(8,128)S(1)}, f32[64,128]{1,0:T(8,128)S(1)}, u32[]{:S(2)}, u32[]{:S(2)}) %collective-permute-start.3) | collective-permute-done | bytes 32800 | tf_op jit(solution)/shard_map/ppermute | solution.py:352
  23.1 1.9 %collective-permute-start.5 = (f32[408,256]{1,0:T(8,128)S(1)}, f32[408,256]{1,0:T(8,128)S(1)}, u32[]{:S(2)}, u32[]{:S(2)}) collective-permute-start(f32[408,256]{1,0:T(8,128)S(1)} %get-tuple-element.31), channel_id=1, source_target_pairs={{1,2},{3,4},{5,6},{7,8},{9,10},{11,12},{13,14},{15,16},{17,18},{19... | collective-permute-start | bytes 1253384 | tf_op jit(solution)/shard_map/ppermute | solution.py:372
  25.0 3.6 %collective-permute-start = (f32[288,256]{1,0:T(8,128)S(1)}, f32[288,256]{1,0:T(8,128)S(1)}, u32[]{:S(2)}, u32[]{:S(2)}) collective-permute-start(f32[288,256]{1,0:T(8,128)S(1)} %get-tuple-element.26), channel_id=1, source_target_pairs={{1,2},{3,4},{5,6},{7,8},{9,10},{11,12},{13,14},{15,16},{17,18},{19... | collective-permute-start | bytes 884744 | tf_op jit(solution)/shard_map/ppermute | solution.py:373
  29.3 0.0 copy-done
  29.3 0.0 copy-done.2
  29.3 1.2 %shard_map.69 = (bf16[16,128,256]{2,1,0:T(8,128)(2,1)S(1)}, bf16[16,128,256]{2,1,0:T(8,128)(2,1)S(1)}, bf16[256,256]{1,0:T(8,128)(2,1)S(1)}, bf16[256,256]{1,0:T(8,128)(2,1)S(1)}, f32[16,128]{1,0:T(8,128)S(1)}) custom-call(f32[5]{0:T(128)S(1)} %copy-done.2, f32[2,16,64,256]{3,2,1,0:T(8,128)S(1)} %get-tuple-element.21.wave_ref, f32[2,64,1024]{2,1,0:T(8,128)S(1)} %copy-done), custom_call_target="tpu_custom_call" | custom-call | flops 268435456 | bytes 1048576 | tf_op jit(solution)/shard_map/pallas_call | solution.py:355
  30.5 0.1 collective-permute-start.6
  30.6 0.0 collective-permute-done.2.link_ref
  30.6 0.0 collective-permute-done.1.chip_ref
  30.6 1.6 %shard_map.71.early_ref = f32[9,128,256]{2,1,0:T(8,128)S(1)} custom-call(s32[1]{0:T(128)S(6)} %copy.12.shift_ref, f32[2,16,64,256]{3,2,1,0:T(8,128)S(1)} %get-tuple-element.21.wave_ref, s32[1,64]{1,0:T(1,128)S(1)} %bitcast.6, bf16[16,128,256]{2,1,0:T(8,128)(2,1)S(1)} %get-tuple-element.22.high_ref, bf16[16,128,256]{2,1,0:T(8,128)(2,1)S(1)} %get-tuple-element.23.low_ref, ...), custom_call_target="tpu_custom_call" | custom-call | flops 268435456 | bytes 1048576 | tf_op jit(solution)/shard_map/pallas_call | solution.py:383
  32.2 0.0 collective-permute-done.6.ends_ref
  32.2 0.2 collective-permute-done.5.late_ref
  32.4 3.4 %shard_map.73 = (f32[2,16,64,256]{3,2,1,0:T(8,128)S(1)}, f32[3,128,128]{2,1,0:T(8,128)S(1)}, f32[16,128]{1,0:T(8,128)S(1)}, f32[2,8,64,256]{3,2,1,0:T(8,128)S(1)}) custom-call(s32[1]{0:T(128)S(6)} %copy.12.shift_ref, f32[5]{0:T(128)S(1)} %copy-done.2, f32[2,16,64,256]{3,2,1,0:T(8,128)S(1)} %get-tuple-element.21.wave_ref, s32[1,64]{1,0:T(1,128)S(1)} %bitcast.7, ...), custom_call_target="tpu_custom_call" | custom-call | flops 268435456 | bytes 1048576 | tf_op jit(solution)/shard_map/pallas_call | solution.py:391
  35.8 0.0 collective-permute-done.link_ref
  35.8 0.9 %shard_map.74 = (f32[2,16,64,256]{3,2,1,0:T(8,128)S(1)}, f32[1,128]{1,0:T(1,128)S(1)}) custom-call(s32[1]{0:T(128)S(6)} %copy.12.shift_ref, f32[2,16,64,256]{3,2,1,0:T(8,128)S(1)} %get-tuple-element.21.wave_ref, s32[1,64]{1,0:T(1,128)S(1)} %bitcast.8, bf16[16,128,256]{2,1,0:T(8,128)(2,1)S(1)} %get-tuple-element.22.high_ref, ...), custom_call_target="tpu_custom_call", output_to_operand_aliasing={{0}: (12, {})} | custom-call | flops 268435456 | bytes 1048576 | tf_op jit(solution)/shard_map/pallas_call | solution.py:403
  36.8 0.7 %broadcast_in_dim.9 = f32[256,1,128]{2,1,0:T(1,128)} broadcast(f32[128]{0:T(128)S(1)} %bitcast.9), dimensions={2} | broadcast | bytes 131584 | tf_op jit(solution)/shard_map/broadcast_in_dim | solution.py:412
  37.5 12.5 %all-to-all-start = ((f32[256,1,128]{2,1,0:T(1,128)}), f32[256,1,128]{2,1,0:T(1,128)S(1)}, u32[]{:S(2)}, u32[]{:S(2)}) async-start(f32[256,1,128]{2,1,0:T(1,128)} %broadcast_in_dim.9), calls=%async_computation | async-start | bytes 262144 | tf_op jit(solution)/shard_map/all_to_all | solution.py:413
  50.0 1.3 %copy.11 = f32[2,16,64,256]{3,2,1,0:T(8,128)} copy(f32[2,16,64,256]{3,2,1,0:T(8,128)S(1)} %get-tuple-element.40.mult_ref) | data formatting | bytes 4194304
  51.4 11.5 %all-to-all-done = f32[256,1,128]{2,1,0:T(1,128)S(1)} async-done(((f32[256,1,128]{2,1,0:T(1,128)}), f32[256,1,128]{2,1,0:T(1,128)S(1)}, u32[]{:S(2)}, u32[]{:S(2)}) %all-to-all-start) | async-done | bytes 131104 | tf_op jit(solution)/shard_map/all_to_all | solution.py:413
  62.9 2.7 %shard_map.75 = f32[2,16,64,256]{3,2,1,0:T(8,128)} custom-call(f32[256,128]{1,0:T(8,128)S(1)} %bitcast.3, f32[2,8,64,256]{3,2,1,0:T(8,128)S(1)} %get-tuple-element.39.kept_ref, f32[2,16,64,256]{3,2,1,0:T(8,128)} %wave_ref.3, f32[2,16,64,256]{3,2,1,0:T(8,128)S(1)} %get-tuple-element.40.mult_ref), custom_call_target="tpu_custom_call" | custom-call | flops 1048576 | bytes 1048576 | tf_op jit(solution)/shard_map/pallas_call | solution.py:415
  (1 shorter events, 0.0 us)
Async XLA Ops:
  0.6 1.7 %copy-start.1 = (s32[64]{0:T(128)S(1)}, s32[64]{0:T(128)}, u32[]{:S(2)}) copy-start(s32[64]{0:T(128)} %param.8) | copy-start | bytes 772
  0.6 28.6 %copy-start = (f32[2,64,1024]{2,1,0:T(8,128)S(1)}, f32[2,64,1024]{2,1,0:T(8,128)}, u32[]{:S(2)}) copy-start(f32[2,64,1024]{2,1,0:T(8,128)} %band_ref.1) | copy-start | bytes 1572868
  0.7 28.6 %copy-start.2 = (f32[5]{0:T(128)S(1)}, f32[5]{0:T(128)}, u32[]{:S(2)}) copy-start(f32[5]{0:T(128)} %taper_ref.3) | copy-start | bytes 64
  3.1 27.4 %collective-permute-start.1 = (f32[1536,256]{1,0:T(8,128)S(1)}, f32[1536,256]{1,0:T(8,128)S(1)}, u32[]{:S(2)}, u32[]{:S(2)}) collective-permute-start(f32[1536,256]{1,0:T(8,128)S(1)} %get-tuple-element.27), channel_id=1, source_target_pairs={{0,1},{2,3},{4,5},{6,7},{8,9},{10,11},{12,13},{14,15},{16,17},{18,... | collective-permute-start | bytes 4718600 | tf_op jit(solution)/shard_map/ppermute | solution.py:353
  6.4 24.1 %collective-permute-start.2 = (f32[864,256]{1,0:T(8,128)S(1)}, f32[864,256]{1,0:T(8,128)S(1)}, u32[]{:S(2)}, u32[]{:S(2)}) collective-permute-start(f32[864,256]{1,0:T(8,128)S(1)} %get-tuple-element.28), channel_id=1, source_target_pairs={{1,2},{3,4},{5,6},{7,8},{9,10},{11,12},{13,14},{15,16},{17,18},{19... | collective-permute-start | bytes 2654216 | tf_op jit(solution)/shard_map/ppermute | solution.py:337
  8.3 6.8 %collective-permute-start.4 = (f32[64,128]{1,0:T(8,128)S(1)}, f32[64,128]{1,0:T(8,128)S(1)}, u32[]{:S(2)}, u32[]{:S(2)}) collective-permute-start(f32[64,128]{1,0:T(8,128)S(1)} %get-tuple-element.29), channel_id=1, source_target_pairs={{32,0},{64,32},{96,64},{128,96},{160,128},{192,160},{224,192},{33,... | collective-permute-start | bytes 98312 | tf_op jit(solution)/shard_map/ppermute | solution.py:351
  9.6 13.4 %collective-permute-start.3 = (f32[64,128]{1,0:T(8,128)S(1)}, f32[64,128]{1,0:T(8,128)S(1)}, u32[]{:S(2)}, u32[]{:S(2)}) collective-permute-start(f32[64,128]{1,0:T(8,128)S(1)} %get-tuple-element.29), channel_id=1, source_target_pairs={{0,32},{32,64},{64,96},{96,128},{128,160},{160,192},{192,224},{1,3... | collective-permute-start | bytes 98312 | tf_op jit(solution)/shard_map/ppermute | solution.py:352
  23.1 9.4 %collective-permute-start.5 = (f32[408,256]{1,0:T(8,128)S(1)}, f32[408,256]{1,0:T(8,128)S(1)}, u32[]{:S(2)}, u32[]{:S(2)}) collective-permute-start(f32[408,256]{1,0:T(8,128)S(1)} %get-tuple-element.31), channel_id=1, source_target_pairs={{1,2},{3,4},{5,6},{7,8},{9,10},{11,12},{13,14},{15,16},{17,18},{19... | collective-permute-start | bytes 1253384 | tf_op jit(solution)/shard_map/ppermute | solution.py:372
  25.0 10.8 %collective-permute-start = (f32[288,256]{1,0:T(8,128)S(1)}, f32[288,256]{1,0:T(8,128)S(1)}, u32[]{:S(2)}, u32[]{:S(2)}) collective-permute-start(f32[288,256]{1,0:T(8,128)S(1)} %get-tuple-element.26), channel_id=1, source_target_pairs={{1,2},{3,4},{5,6},{7,8},{9,10},{11,12},{13,14},{15,16},{17,18},{19... | collective-permute-start | bytes 884744 | tf_op jit(solution)/shard_map/ppermute | solution.py:373
  30.5 1.8 %collective-permute-start.6 = (f32[48,128]{1,0:T(8,128)S(1)}, f32[48,128]{1,0:T(8,128)S(1)}, u32[]{:S(2)}, u32[]{:S(2)}) collective-permute-start(f32[48,128]{1,0:T(8,128)S(1)} %get-tuple-element.32), channel_id=1, source_target_pairs={{0,1},{2,3},{4,5},{6,7},{8,9},{10,11},{12,13},{14,15},{16,17},{18,... | collective-permute-start | bytes 73736 | tf_op jit(solution)/shard_map/ppermute | solution.py:374
  37.5 25.4 %all-to-all-start = ((f32[256,1,128]{2,1,0:T(1,128)}), f32[256,1,128]{2,1,0:T(1,128)S(1)}, u32[]{:S(2)}, u32[]{:S(2)}) async-start(f32[256,1,128]{2,1,0:T(1,128)} %broadcast_in_dim.9), calls=%async_computation | async-start | bytes 262144 | tf_op jit(solution)/shard_map/all_to_all | solution.py:413

commit v8 on v7

--- a/solution.py
+++ b/solution.py
@@ -22,7 +22,7 @@
 BF16 = jnp.bfloat16
 EARLY = 9
 FIRST = 13
-KEPT = 8
+KEPT = 9
 
 
 def iota(shape, dim):
@@ -73,12 +73,24 @@
     copies[2].wait()
 
 
-def rest_kernel(wave_ref, mask_ref, late_ref, link_ref, chip_ref, ends_ref):
+def ends_kernel(wave_ref, mask_ref, ends_ref):
+    slices = wave_ref.shape[1]
+    lane = iota((BLOCK, LANES), 1)
+    ends = jnp.zeros((BLOCK, LANES), F32)
+    for f in range(slices):
+        for x in range(2):
+            place = 4 * (x * slices + f)
+            last = pltpu.roll(wave_ref[x, f, :, -LANES:], (place + SHALF) % LANES, 1)
+            first = pltpu.roll(wave_ref[x, f, :, :LANES], place + SHALF, 1)
+            ends = jnp.where(lane // 2 == place // 2, last, ends)
+            ends = jnp.where(lane // 2 == place // 2 + 1, first, ends)
+    ends_ref[...] = ends * mask_column(mask_ref)
+
+
+def rest_kernel(wave_ref, mask_ref, late_ref, link_ref, chip_ref):
     odd = is_odd()
     mask = mask_column(mask_ref)
     slices = wave_ref.shape[1]
-    lane = iota((BLOCK, LANES), 1)
-    ends = jnp.zeros((BLOCK, LANES), F32)
     for f in range(slices):
         for x in range(2):
             masked = wave_ref[x, f] * mask
@@ -90,12 +102,6 @@
             elif f >= EARLY:
                 row -= 2 * EARLY * HALO
                 late_ref[row : row + HALO] = at_end(masked, odd)
-            place = 4 * (x * slices + f)
-            last = pltpu.roll(masked[:, -LANES:], (place + SHALF) % LANES, 1)
-            first = pltpu.roll(masked[:, :LANES], place + SHALF, 1)
-            ends = jnp.where(lane // 2 == place // 2, last, ends)
-            ends = jnp.where(lane // 2 == place // 2 + 1, first, ends)
-    ends_ref[...] = ends
 
 
 def merged_ends(before_ref, after_ref):
@@ -337,19 +343,19 @@
     early = lax.ppermute(early, RCV, swaps(RCV, 1))
 
     wave, band = on_chip(wave, surface_band)
-    late, link, chip, ends = call(
+    (ends,) = call(ends_kernel, [VMEM, VMEM], [in_vmem(BLOCK, LANES)], 1 << 20)(wave, mask)
+    after = lax.ppermute(ends, SRC, src_down)
+    before = lax.ppermute(ends, SRC, src_up)
+    late, link, chip = call(
         rest_kernel,
         [VMEM, VMEM],
         [
             in_vmem(2 * (FIRST - EARLY) * HALO + HALO // 2, shots),
             in_vmem(2 * (slices - FIRST) * HALO, shots),
             in_vmem(2 * slices * HALO, shots),
-            in_vmem(BLOCK, LANES),
         ],
         1 << 20,
     )(wave, mask)
-    after = lax.ppermute(ends, SRC, src_down)
-    before = lax.ppermute(ends, SRC, src_up)
     chip = lax.ppermute(chip, RCV, swaps(RCV, 0))
 
     high, low, taper_high, taper_low, data_energy = call(

time: 65.9 us -> 65.3 us (level)
  transfers between devices with their start and end apart: 8 -> 8, of which waited for: 3 -> 3; matrix products, arithmetic and copies ran while one was open for 2% -> 2% of each run, Pallas kernels for 9% -> 11%
where the time goes in v8:
time: 65.3 us; the launch traced here: 64.9 us
  starting transfers between devices  29.9 us (46%)
  waiting for transfers between devices  19.2 us (29%)
  Pallas kernels  12.3 us (19%)
  local copies, waits for them, and re-layouts  2.07 us (3%)
  between operations  1.45 us (2%)
    all_to_all x1, starting transfers between devices, per_device(): lax.all_to_all(spread, SRC_RCV, 0, 0, tiled=True).reshape(devices, LANES)  12.3 us
    all_to_all x1, waiting for transfers between devices, per_device(): lax.all_to_all(spread, SRC_RCV, 0, 0, tiled=True).reshape(devices, LANES)  11.5 us
    ppermute x1, waiting for transfers between devices, per_device(): before = lax.ppermute(ends, SRC, src_up)  7.52 us
    ppermute x1, starting transfers between devices, per_device(): before = lax.ppermute(ends, SRC, src_up)  5.49 us
    ppermute x1, starting transfers between devices, per_device(): link = lax.ppermute(link, RCV, swaps(RCV, 1))  3.64 us
    pallas_call x1, Pallas kernels, per_device(): call(merge_kernel, [SMEM, SMEM] + [VMEM] * 12, [in_vmem(2, slices, receiv...  3.41 us
    ppermute x1, starting transfers between devices, per_device(): chip = lax.ppermute(chip, RCV, swaps(RCV, 0))  3.29 us
    pallas_call x1, Pallas kernels, per_device(): call(subtract_kernel, [VMEM, VMEM, HBM, VMEM], [jax.ShapeDtypeStruct((2,...  2.66 us
  transfers between devices with their start and end apart: 8, of which 3 were waited for; matrix products, arithmetic and copies ran while one was open for 2% of the time, Pallas kernels for 11%

profile of v8, /device:TPU:1, one launch (start us, length us, event | category | flops | bytes accessed | tf_op | source)
XLA Modules:
  0.0 64.9 jit_solution(16664520048403109189)
XLA Ops:
  0.6 0.0 copy-start.1
  0.6 1.6 %shard_map.68 = (f32[2,16,64,256]{3,2,1,0:T(8,128)S(1)}, f32[864,256]{1,0:T(8,128)S(1)}) custom-call(f32[2,16,64,256]{3,2,1,0:T(8,128)} %wave_ref.3, s32[1,64]{1,0:T(1,128)} %bitcast.4), custom_call_target="tpu_custom_call" | custom-call | flops 1048576 | bytes 1048576 | tf_op jit(solution)/shard_map/pallas_call | solution.py:336
  2.2 0.0 copy-done.1
  2.2 0.0 copy-start
  2.3 0.0 copy-start.2
  2.3 0.3 shard_map.70
  2.5 3.3 %collective-permute-start.1 = (f32[1536,256]{1,0:T(8,128)S(1)}, f32[1536,256]{1,0:T(8,128)S(1)}, u32[]{:S(2)}, u32[]{:S(2)}) collective-permute-start(f32[1536,256]{1,0:T(8,128)S(1)} %get-tuple-element.26), channel_id=1, source_target_pairs={{0,1},{2,3},{4,5},{6,7},{8,9},{10,11},{12,13},{14,15},{16,17},{18,... | collective-permute-start | bytes 4718600 | tf_op jit(solution)/shard_map/ppermute | solution.py:359
  5.8 1.9 %collective-permute-start.2 = (f32[864,256]{1,0:T(8,128)S(1)}, f32[864,256]{1,0:T(8,128)S(1)}, u32[]{:S(2)}, u32[]{:S(2)}) collective-permute-start(f32[864,256]{1,0:T(8,128)S(1)} %get-tuple-element.27), channel_id=1, source_target_pairs={{1,2},{3,4},{5,6},{7,8},{9,10},{11,12},{13,14},{15,16},{17,18},{19... | collective-permute-start | bytes 2654216 | tf_op jit(solution)/shard_map/ppermute | solution.py:343
  7.7 0.6 shard_map.72
  8.4 1.3 %collective-permute-start.4 = (f32[64,128]{1,0:T(8,128)S(1)}, f32[64,128]{1,0:T(8,128)S(1)}, u32[]{:S(2)}, u32[]{:S(2)}) collective-permute-start(f32[64,128]{1,0:T(8,128)S(1)} %shard_map.72), channel_id=1, source_target_pairs={{32,0},{64,32},{96,64},{128,96},{160,128},{192,160},{224,192},{33,... | collective-permute-start | bytes 98312 | tf_op jit(solution)/shard_map/ppermute | solution.py:347
  9.7 5.5 %collective-permute-start.3 = (f32[64,128]{1,0:T(8,128)S(1)}, f32[64,128]{1,0:T(8,128)S(1)}, u32[]{:S(2)}, u32[]{:S(2)}) collective-permute-start(f32[64,128]{1,0:T(8,128)S(1)} %shard_map.72), channel_id=1, source_target_pairs={{0,32},{32,64},{64,96},{96,128},{128,160},{160,192},{192,224},{1,3... | collective-permute-start | bytes 98312 | tf_op jit(solution)/shard_map/ppermute | solution.py:348
  15.2 0.0 collective-permute-done.4.after_ref
  15.2 7.5 %collective-permute-done.3.before_ref = f32[64,128]{1,0:T(8,128)S(1)} collective-permute-done((f32[64,128]{1,0:T(8,128)S(1)}, f32[64,128]{1,0:T(8,128)S(1)}, u32[]{:S(2)}, u32[]{:S(2)}) %collective-permute-start.3) | collective-permute-done | bytes 32800 | tf_op jit(solution)/shard_map/ppermute | solution.py:348
  22.7 1.9 %collective-permute-start.5 = (f32[408,256]{1,0:T(8,128)S(1)}, f32[408,256]{1,0:T(8,128)S(1)}, u32[]{:S(2)}, u32[]{:S(2)}) collective-permute-start(f32[408,256]{1,0:T(8,128)S(1)} %get-tuple-element.29), channel_id=1, source_target_pairs={{1,2},{3,4},{5,6},{7,8},{9,10},{11,12},{13,14},{15,16},{17,18},{19... | collective-permute-start | bytes 1253384 | tf_op jit(solution)/shard_map/ppermute | solution.py:378
  24.7 3.6 %collective-permute-start = (f32[288,256]{1,0:T(8,128)S(1)}, f32[288,256]{1,0:T(8,128)S(1)}, u32[]{:S(2)}, u32[]{:S(2)}) collective-permute-start(f32[288,256]{1,0:T(8,128)S(1)} %get-tuple-element.25), channel_id=1, source_target_pairs={{1,2},{3,4},{5,6},{7,8},{9,10},{11,12},{13,14},{15,16},{17,18},{19... | collective-permute-start | bytes 884744 | tf_op jit(solution)/shard_map/ppermute | solution.py:379
  29.0 0.0 copy-done
  29.0 0.0 copy-done.2
  29.0 1.2 %shard_map.69 = (bf16[16,128,256]{2,1,0:T(8,128)(2,1)S(1)}, bf16[16,128,256]{2,1,0:T(8,128)(2,1)S(1)}, bf16[256,256]{1,0:T(8,128)(2,1)S(1)}, bf16[256,256]{1,0:T(8,128)(2,1)S(1)}, f32[16,128]{1,0:T(8,128)S(1)}) custom-call(f32[5]{0:T(128)S(1)} %copy-done.2, f32[2,16,64,256]{3,2,1,0:T(8,128)S(1)} %get-tuple-element.20.wave_ref, f32[2,64,1024]{2,1,0:T(8,128)S(1)} %copy-done), custom_call_target="tpu_custom_call" | custom-call | flops 268435456 | bytes 1048576 | tf_op jit(solution)/shard_map/pallas_call | solution.py:361
  30.1 0.1 collective-permute-start.6
  30.2 0.0 collective-permute-done.2.link_ref
  30.2 0.0 collective-permute-done.1.chip_ref
  30.3 1.6 %shard_map.71.early_ref = f32[9,128,256]{2,1,0:T(8,128)S(1)} custom-call(s32[1]{0:T(128)S(6)} %copy.12.shift_ref, f32[2,16,64,256]{3,2,1,0:T(8,128)S(1)} %get-tuple-element.20.wave_ref, s32[1,64]{1,0:T(1,128)S(1)} %bitcast.7, bf16[16,128,256]{2,1,0:T(8,128)(2,1)S(1)} %get-tuple-element.21.high_ref, bf16[16,128,256]{2,1,0:T(8,128)(2,1)S(1)} %get-tuple-element.22.low_ref, ...), custom_call_target="tpu_custom_call" | custom-call | flops 268435456 | bytes 1048576 | tf_op jit(solution)/shard_map/pallas_call | solution.py:389
  31.9 0.0 collective-permute-done.6.ends_ref
  31.9 0.2 collective-permute-done.5.late_ref
  32.1 3.4 %shard_map.74 = (f32[2,16,64,256]{3,2,1,0:T(8,128)S(1)}, f32[3,128,128]{2,1,0:T(8,128)S(1)}, f32[16,128]{1,0:T(8,128)S(1)}, f32[2,9,64,256]{3,2,1,0:T(8,128)S(1)}) custom-call(s32[1]{0:T(128)S(6)} %copy.12.shift_ref, f32[5]{0:T(128)S(1)} %copy-done.2, f32[2,16,64,256]{3,2,1,0:T(8,128)S(1)} %get-tuple-element.20.wave_ref, s32[1,64]{1,0:T(1,128)S(1)} %bitcast.8, ...), custom_call_target="tpu_custom_call" | custom-call | flops 268435456 | bytes 1048576 | tf_op jit(solution)/shard_map/pallas_call | solution.py:397
  35.5 0.0 collective-permute-done.link_ref
  35.5 0.9 %shard_map.75 = (f32[2,16,64,256]{3,2,1,0:T(8,128)S(1)}, f32[1,128]{1,0:T(1,128)S(1)}) custom-call(s32[1]{0:T(128)S(6)} %copy.12.shift_ref, f32[2,16,64,256]{3,2,1,0:T(8,128)S(1)} %get-tuple-element.20.wave_ref, s32[1,64]{1,0:T(1,128)S(1)} %bitcast.9, bf16[16,128,256]{2,1,0:T(8,128)(2,1)S(1)} %get-tuple-element.21.high_ref, ...), custom_call_target="tpu_custom_call", output_to_operand_aliasing={{0}: (12, {})} | custom-call | flops 268435456 | bytes 1048576 | tf_op jit(solution)/shard_map/pallas_call | solution.py:409
  36.4 0.7 %broadcast_in_dim.9 = f32[256,1,128]{2,1,0:T(1,128)} broadcast(f32[128]{0:T(128)S(1)} %bitcast.10), dimensions={2} | broadcast | bytes 131584 | tf_op jit(solution)/shard_map/broadcast_in_dim | solution.py:418
  37.2 12.3 %all-to-all-start = ((f32[256,1,128]{2,1,0:T(1,128)}), f32[256,1,128]{2,1,0:T(1,128)S(1)}, u32[]{:S(2)}, u32[]{:S(2)}) async-start(f32[256,1,128]{2,1,0:T(1,128)} %broadcast_in_dim.9), calls=%async_computation | async-start | bytes 262144 | tf_op jit(solution)/shard_map/all_to_all | solution.py:419
  49.4 1.3 %copy.11 = f32[2,16,64,256]{3,2,1,0:T(8,128)} copy(f32[2,16,64,256]{3,2,1,0:T(8,128)S(1)} %get-tuple-element.38.mult_ref) | data formatting | bytes 4194304
  50.7 11.5 %all-to-all-done = f32[256,1,128]{2,1,0:T(1,128)S(1)} async-done(((f32[256,1,128]{2,1,0:T(1,128)}), f32[256,1,128]{2,1,0:T(1,128)S(1)}, u32[]{:S(2)}, u32[]{:S(2)}) %all-to-all-start) | async-done | bytes 131104 | tf_op jit(solution)/shard_map/all_to_all | solution.py:419
  62.3 2.7 %shard_map.76 = f32[2,16,64,256]{3,2,1,0:T(8,128)} custom-call(f32[256,128]{1,0:T(8,128)S(1)} %bitcast.3, f32[2,9,64,256]{3,2,1,0:T(8,128)S(1)} %get-tuple-element.37.kept_ref, f32[2,16,64,256]{3,2,1,0:T(8,128)} %wave_ref.3, f32[2,16,64,256]{3,2,1,0:T(8,128)S(1)} %get-tuple-element.38.mult_ref), custom_call_target="tpu_custom_call" | custom-call | flops 1048576 | bytes 1048576 | tf_op jit(solution)/shard_map/pallas_call | solution.py:421
  (1 shorter events, 0.0 us)
Async XLA Ops:
  0.6 1.6 %copy-start.1 = (s32[64]{0:T(128)S(1)}, s32[64]{0:T(128)}, u32[]{:S(2)}) copy-start(s32[64]{0:T(128)} %param.8) | copy-start | bytes 772
  2.2 26.7 %copy-start = (f32[2,64,1024]{2,1,0:T(8,128)S(1)}, f32[2,64,1024]{2,1,0:T(8,128)}, u32[]{:S(2)}) copy-start(f32[2,64,1024]{2,1,0:T(8,128)} %band_ref.1) | copy-start | bytes 1572868
  2.3 26.7 %copy-start.2 = (f32[5]{0:T(128)S(1)}, f32[5]{0:T(128)}, u32[]{:S(2)}) copy-start(f32[5]{0:T(128)} %taper_ref.3) | copy-start | bytes 64
  2.5 27.7 %collective-permute-start.1 = (f32[1536,256]{1,0:T(8,128)S(1)}, f32[1536,256]{1,0:T(8,128)S(1)}, u32[]{:S(2)}, u32[]{:S(2)}) collective-permute-start(f32[1536,256]{1,0:T(8,128)S(1)} %get-tuple-element.26), channel_id=1, source_target_pairs={{0,1},{2,3},{4,5},{6,7},{8,9},{10,11},{12,13},{14,15},{16,17},{18,... | collective-permute-start | bytes 4718600 | tf_op jit(solution)/shard_map/ppermute | solution.py:359
  5.8 24.4 %collective-permute-start.2 = (f32[864,256]{1,0:T(8,128)S(1)}, f32[864,256]{1,0:T(8,128)S(1)}, u32[]{:S(2)}, u32[]{:S(2)}) collective-permute-start(f32[864,256]{1,0:T(8,128)S(1)} %get-tuple-element.27), channel_id=1, source_target_pairs={{1,2},{3,4},{5,6},{7,8},{9,10},{11,12},{13,14},{15,16},{17,18},{19... | collective-permute-start | bytes 2654216 | tf_op jit(solution)/shard_map/ppermute | solution.py:343
  8.4 6.8 %collective-permute-start.4 = (f32[64,128]{1,0:T(8,128)S(1)}, f32[64,128]{1,0:T(8,128)S(1)}, u32[]{:S(2)}, u32[]{:S(2)}) collective-permute-start(f32[64,128]{1,0:T(8,128)S(1)} %shard_map.72), channel_id=1, source_target_pairs={{32,0},{64,32},{96,64},{128,96},{160,128},{192,160},{224,192},{33,... | collective-permute-start | bytes 98312 | tf_op jit(solution)/shard_map/ppermute | solution.py:347
  9.7 13.0 %collective-permute-start.3 = (f32[64,128]{1,0:T(8,128)S(1)}, f32[64,128]{1,0:T(8,128)S(1)}, u32[]{:S(2)}, u32[]{:S(2)}) collective-permute-start(f32[64,128]{1,0:T(8,128)S(1)} %shard_map.72), channel_id=1, source_target_pairs={{0,32},{32,64},{64,96},{96,128},{128,160},{160,192},{192,224},{1,3... | collective-permute-start | bytes 98312 | tf_op jit(solution)/shard_map/ppermute | solution.py:348
  22.7 9.4 %collective-permute-start.5 = (f32[408,256]{1,0:T(8,128)S(1)}, f32[408,256]{1,0:T(8,128)S(1)}, u32[]{:S(2)}, u32[]{:S(2)}) collective-permute-start(f32[408,256]{1,0:T(8,128)S(1)} %get-tuple-element.29), channel_id=1, source_target_pairs={{1,2},{3,4},{5,6},{7,8},{9,10},{11,12},{13,14},{15,16},{17,18},{19... | collective-permute-start | bytes 1253384 | tf_op jit(solution)/shard_map/ppermute | solution.py:378
  24.7 10.8 %collective-permute-start = (f32[288,256]{1,0:T(8,128)S(1)}, f32[288,256]{1,0:T(8,128)S(1)}, u32[]{:S(2)}, u32[]{:S(2)}) collective-permute-start(f32[288,256]{1,0:T(8,128)S(1)} %get-tuple-element.25), channel_id=1, source_target_pairs={{1,2},{3,4},{5,6},{7,8},{9,10},{11,12},{13,14},{15,16},{17,18},{19... | collective-permute-start | bytes 884744 | tf_op jit(solution)/shard_map/ppermute | solution.py:379
  30.1 1.8 %collective-permute-start.6 = (f32[48,128]{1,0:T(8,128)S(1)}, f32[48,128]{1,0:T(8,128)S(1)}, u32[]{:S(2)}, u32[]{:S(2)}) collective-permute-start(f32[48,128]{1,0:T(8,128)S(1)} %get-tuple-element.30), channel_id=1, source_target_pairs={{0,1},{2,3},{4,5},{6,7},{8,9},{10,11},{12,13},{14,15},{16,17},{18,... | collective-permute-start | bytes 73736 | tf_op jit(solution)/shard_map/ppermute | solution.py:380
  37.2 25.1 %all-to-all-start = ((f32[256,1,128]{2,1,0:T(1,128)}), f32[256,1,128]{2,1,0:T(1,128)S(1)}, u32[]{:S(2)}, u32[]{:S(2)}) async-start(f32[256,1,128]{2,1,0:T(1,128)} %broadcast_in_dim.9), calls=%async_computation | async-start | bytes 262144 | tf_op jit(solution)/shard_map/all_to_all | solution.py:419
